TPU v7x, 32 devices: a whole 2x2x4 slice. The times are simulated.
32 devices in a mesh: dp: 4 (over z), col: 2 (over y), row: 4 (over x, core).
Axes of the slice: x: 2, y: 2, z: 4, core: 2. Of those that a mesh axis runs over, the one named last changes fastest.
Arguments:
- x_attn: bfloat16 [4096, 2048], P('dp', 'row')
- dy_attn: bfloat16 [4096, 2048], P('dp', 'col')
- x_mlp: bfloat16 [4096, 2048], P('dp', 'row')
- dy_gate: bfloat16 [4096, 16384], P('dp', 'col')
- dy_up: bfloat16 [4096, 16384], P('dp', 'col')
- h_mlp: bfloat16 [4096, 16384], P('dp', 'row')
- dy_out: bfloat16 [4096, 2048], P('dp', 'col')
- w_attn: float32 [2048, 2048], P('row', 'col')
- w_gate: float32 [2048, 16384], P('row', 'col')
- w_up: float32 [2048, 16384], P('row', 'col')
- w_down: float32 [16384, 2048], P('row', 'col')
- r_attn: float32 [2048], P('row')
- c_attn: float32 [2048], P('col')
- r_gate: float32 [2048], P('row')
- c_gate: float32 [16384], P('col')
- r_up: float32 [2048], P('row')
- c_up: float32 [16384], P('col')
- r_down: float32 [16384], P('row')
- c_down: float32 [2048], P('col')
- hyper_params: float32 [3], replicated
Outputs:
- output 1: float32 [2048, 2048], P('row', 'col')
- output 2: float32 [2048], P('row')
- output 3: float32 [2048], P('col')
- output 4: float32 [2048, 16384], P('row', 'col')
- output 5: float32 [2048], P('row')
- output 6: float32 [16384], P('col')
- output 7: float32 [2048, 16384], P('row', 'col')
- output 8: float32 [2048], P('row')
- output 9: float32 [16384], P('col')
- output 10: float32 [16384, 2048], P('row', 'col')
- output 11: float32 [16384], P('row')
- output 12: float32 [2048], P('col')
All inputs are finite; a program needn't handle non-finite values.
Results may differ from a plain program's by a relative error of at most 0.001.
Values are sent between devices in bfloat16 or wider.
A program may use at most 1 GiB of HBM per device.

v0:
```python
import functools
import jax
import jax.numpy as jnp
from jax import lax
from jax.sharding import PartitionSpec as P

EPS_ONE = 1e-30
EPS_TWO = 1e-3


def matrix_step(x_block, dy_block, w_block, row_old, col_old, hyper_vals, row_size, col_size):
    beta_two = hyper_vals[0]
    rho_step = hyper_vals[1]
    clip_thr = hyper_vals[2]
    m_total = w_block.shape[0] * row_size
    n_total = w_block.shape[1] * col_size
    part_grad = jnp.einsum('tm,tn->mn', x_block, dy_block, preferred_element_type=jnp.float32)
    grad_block = lax.psum(part_grad, 'dp')
    sq_grad = grad_block * grad_block + EPS_ONE
    row_sum = lax.psum(jnp.sum(sq_grad, axis=1), 'col')
    col_sum = lax.psum(jnp.sum(sq_grad, axis=0), 'row')
    new_row = beta_two * row_old + (1.0 - beta_two) * (row_sum / n_total)
    new_col = beta_two * col_old + (1.0 - beta_two) * (col_sum / m_total)
    row_total = lax.psum(jnp.sum(new_row), 'row')
    second_est = new_row[:, None] * new_col[None, :] / row_total
    update = grad_block / jnp.sqrt(second_est)
    upd_rms = jnp.sqrt(lax.psum(jnp.sum(update * update), ('row', 'col')) / (m_total * n_total))
    update = update / jnp.maximum(1.0, upd_rms / clip_thr)
    w_rms = jnp.sqrt(lax.psum(jnp.sum(w_block * w_block), ('row', 'col')) / (m_total * n_total))
    step_size = rho_step * jnp.maximum(EPS_TWO, w_rms)
    return (w_block - step_size * update, new_row, new_col)


def solution(mesh):
    row_size = mesh.shape['row']
    col_size = mesh.shape['col']
    act_spec = P('dp', 'row')
    grad_spec = P('dp', 'col')
    w_spec = P('row', 'col')
    row_spec = P('row')
    col_spec = P('col')
    in_specs = (act_spec, grad_spec, act_spec, grad_spec, grad_spec, act_spec, grad_spec,
                w_spec, w_spec, w_spec, w_spec,
                row_spec, col_spec, row_spec, col_spec, row_spec, col_spec, row_spec, col_spec, P())
    out_specs = (w_spec, row_spec, col_spec) * 4

    def per_device(x_attn, dy_attn, x_mlp, dy_gate, dy_up, h_mlp, dy_out, w_attn, w_gate, w_up, w_down,
                   r_attn, c_attn, r_gate, c_gate, r_up, c_up, r_down, c_down, hyper_params):
        apply_one = functools.partial(matrix_step, hyper_vals=hyper_params, row_size=row_size, col_size=col_size)
        return (apply_one(x_attn, dy_attn, w_attn, r_attn, c_attn)
                + apply_one(x_mlp, dy_gate, w_gate, r_gate, c_gate)
                + apply_one(x_mlp, dy_up, w_up, r_up, c_up)
                + apply_one(h_mlp, dy_out, w_down, r_down, c_down))

    return jax.shard_map(per_device, mesh=mesh, in_specs=in_specs, out_specs=out_specs, check_vma=False)
```

profile of v0, /device:TPU:0, one launch (start us, length us, event | category | flops | bytes accessed | tf_op | source)
XLA Modules:
  0.0 1946.9 jit_solution(17647180642533148188)
XLA Ops:
  7.2 0.0 copy-start
  7.2 0.0 all-reduce.7.cloned.1.call-start
  7.3 16.4 fusion.14
  23.6 14.5 fusion.15
  38.1 15.1 fusion.16
  53.2 2.6 fusion.13
  55.8 0.0 all-reduce.7.cloned.1.call-update
  55.8 0.6 copy-done.19
  56.5 0.7 fusion.12
  57.8 1.2 multiply_reduce_fusion.7
  59.0 10.7 multiply_reduce_fusion.1
  69.7 10.7 multiply_reduce_fusion.3
  80.4 10.8 multiply_reduce_fusion.5
  91.2 1675.8 %all-reduce.7.cloned.1.call-done = (f32[512,1024]{1,0:T(8,128)}, f32[512,8192]{1,0:T(8,128)}, f32[512,8192]{1,0:T(8,128)}, f32[4096,1024]{1,0:T(8,128)}) async-done(((f32[512,1024]{1,0:T(8,128)}, f32[512,8192]{1,0:T(8,128)}, f32[512,8192]{1,0:T(8,128)}, f32[4096,1024]{1,0:T(8,128)}), (f32[512,1024]{1,0:T(8,128)}, f32[512,8192]{1,0:T(8,128)}, f32[512,8192]{1,0:T(8,128)}, ...) | async-done | bytes 52428816 | tf_op jit(solution)/shard_map/psum | solution.py:18
  1767.0 13.0 fusion.2
  1779.9 0.0 copy-start.18
  1779.9 0.0 copy-start.22
  1779.9 0.0 copy-start.23
  1780.0 0.0 copy-start.24
  1780.0 0.0 copy-start.20
  1780.0 0.0 copy-start.13
  1780.0 0.0 copy-start.14
  1780.0 0.0 copy-start.21
  1780.0 12.7 fusion
  1792.7 8.6 fusion.4
  1801.3 0.4 fusion.6
  1801.7 8.3 all-reduce.3
  1810.0 1.3 fusion.8
  1811.2 1.3 fusion.11
  1812.5 1.2 fusion.9
  1813.7 1.2 fusion.10
  1815.0 12.2 all-reduce.8
  1827.2 0.6 multiply_add_fusion.7
  1827.8 0.0 copy-start.12
  1827.8 0.7 multiply_add_fusion.4
  1828.5 0.0 copy-start.8
  1828.5 0.7 multiply_add_fusion.5
  1829.2 0.0 copy-start.9
  1829.2 0.7 multiply_add_fusion.8
  1829.9 0.0 copy-start.11
  1829.9 11.0 multiply_reduce_fusion
  1840.9 10.4 multiply_reduce_fusion.2
  1851.3 6.0 multiply_reduce_fusion.4
  1857.3 2.1 multiply_reduce_fusion.6
  1859.4 13.1 all-reduce
  1883.2 18.4 multiply_subtract_fusion
  1901.6 2.6 multiply_subtract_fusion.3
  1904.2 35.6 %multiply_subtract_fusion.1 = (f32[512,8192]{1,0:T(8,128)}, f32[512,8192]{1,0:T(8,128)}) fusion(f32[512,8192]{1,0:T(8,128)} %param.29, f32[]{:T(128)S(6)} %max.29, f32[]{:T(128)S(6)} %mul.248, f32[512,8192]{1,0:T(8,128)} %get-tuple-element.38, f32[]{:T(128)} %get-tuple-element.32, f32[8192]{0:T(1024)S(1)} %multiply_add_fusion.4, ...), kind=kLoop, calls=%fused_computation.5 | loop fusion | flops 50331648 | bytes 100732952 | tf_op jit(solution)/shard_map/sub | solution.py:31
  (45 shorter events, 0.1 us)
Async XLA Ops:
  7.2 30.9 %copy-start = (bf16[1024,1024]{1,0:T(8,128)(2,1)S(1)}, bf16[1024,1024]{1,0:T(8,128)(2,1)}, u32[]{:S(2)}) copy-start(bf16[1024,1024]{1,0:T(8,128)(2,1)} %param.26) | copy-start | bytes 6291460
  7.2 1759.8 %all-reduce.7.cloned.1.call-start = ((), (), s32[]{:S(2)}) async-start(), calls=%async_computation | async-start | bytes 104857600 | tf_op jit(solution)/shard_map/psum | solution.py:18
  7.2 16.4 copy-start.3
  38.1 15.1 copy-start.6
  38.1 15.1 copy-start.7
  55.8 0.7 copy-start.19
  55.8 2.0 copy-start.4
  1779.9 21.4 %copy-start.2 = (f32[512,1024]{1,0:T(8,128)S(1)}, f32[512,1024]{1,0:T(8,128)}, u32[]{:S(2)}) copy-start(f32[512,1024]{1,0:T(8,128)} %get-tuple-element.36) | copy-start | bytes 6291460
  1779.9 30.0 %copy-start.18 = (f32[4096]{0:T(1024)S(1)}, f32[4096]{0:T(1024)}, u32[]{:S(2)}) copy-start(f32[4096]{0:T(1024)} %param.37) | copy-start | bytes 49156
  1779.9 31.3 %copy-start.22 = (f32[512]{0:T(512)S(1)}, f32[512]{0:T(512)}, u32[]{:S(2)}) copy-start(f32[512]{0:T(512)} %param.31) | copy-start | bytes 6148
  1779.9 32.5 %copy-start.23 = (f32[512]{0:T(512)S(1)}, f32[512]{0:T(512)}, u32[]{:S(2)}) copy-start(f32[512]{0:T(512)} %param.35) | copy-start | bytes 6148
  1780.0 33.8 %copy-start.24 = (f32[512]{0:T(512)S(1)}, f32[512]{0:T(512)}, u32[]{:S(2)}) copy-start(f32[512]{0:T(512)} %param.33) | copy-start | bytes 6148
  1780.0 47.2 %copy-start.20 = (f32[1024]{0:T(1024)S(1)}, f32[1024]{0:T(1024)}, u32[]{:S(2)}) copy-start(f32[1024]{0:T(1024)} %param.38) | copy-start | bytes 12292
  1780.0 47.8 %copy-start.13 = (f32[8192]{0:T(1024)S(1)}, f32[8192]{0:T(1024)}, u32[]{:S(2)}) copy-start(f32[8192]{0:T(1024)} %param.36) | copy-start | bytes 98308
  1780.0 48.5 %copy-start.14 = (f32[8192]{0:T(1024)S(1)}, f32[8192]{0:T(1024)}, u32[]{:S(2)}) copy-start(f32[8192]{0:T(1024)} %param.34) | copy-start | bytes 98308
  1780.0 49.2 %copy-start.21 = (f32[1024]{0:T(1024)S(1)}, f32[1024]{0:T(1024)}, u32[]{:S(2)}) copy-start(f32[1024]{0:T(1024)} %param.32) | copy-start | bytes 12292
  1811.2 71.9 %copy-start.10 = (f32[4096]{0:T(1024)}, f32[4096]{0:T(1024)S(1)}, u32[]{:S(2)}) copy-start(f32[4096]{0:T(1024)S(1)} %get-tuple-element.45) | copy-start | bytes 49156
  1812.5 89.2 %copy-start.15 = (f32[512]{0:T(512)}, f32[512]{0:T(512)S(1)}, u32[]{:S(2)}) copy-start(f32[512]{0:T(512)S(1)} %get-tuple-element.51) | copy-start | bytes 6148
  1813.7 90.5 %copy-start.16 = (f32[512]{0:T(512)}, f32[512]{0:T(512)S(1)}, u32[]{:S(2)}) copy-start(f32[512]{0:T(512)S(1)} %get-tuple-element.47) | copy-start | bytes 6148
  1815.0 89.2 %copy-start.17 = (f32[512]{0:T(512)}, f32[512]{0:T(512)S(1)}, u32[]{:S(2)}) copy-start(f32[512]{0:T(512)S(1)} %get-tuple-element.49) | copy-start | bytes 6148
  1827.8 55.3 %copy-start.12 = (f32[1024]{0:T(1024)}, f32[1024]{0:T(1024)S(1)}, u32[]{:S(2)}) copy-start(f32[1024]{0:T(1024)S(1)} %multiply_add_fusion.7) | copy-start | bytes 12292
  1828.5 75.7 %copy-start.8 = (f32[8192]{0:T(1024)}, f32[8192]{0:T(1024)S(1)}, u32[]{:S(2)}) copy-start(f32[8192]{0:T(1024)S(1)} %multiply_add_fusion.4) | copy-start | bytes 98308
  1829.2 75.0 %copy-start.9 = (f32[8192]{0:T(1024)}, f32[8192]{0:T(1024)S(1)}, u32[]{:S(2)}) copy-start(f32[8192]{0:T(1024)S(1)} %multiply_add_fusion.5) | copy-start | bytes 98308
  1829.9 71.8 %copy-start.11 = (f32[1024]{0:T(1024)}, f32[1024]{0:T(1024)S(1)}, u32[]{:S(2)}) copy-start(f32[1024]{0:T(1024)S(1)} %multiply_add_fusion.8) | copy-start | bytes 12292
  1829.9 21.4 %slice-start = ((s8[16777216]{0:T(1024)(128)(4,1)}), s8[4194304]{0:T(1024)(128)(4,1)S(1)}, s32[]{:S(2)}) async-start(s8[16777216]{0:T(1024)(128)(4,1)} %bitcast.11), calls=%async_computation.1 | async-start | bytes 8388608
  1829.9 21.4 %slice-start.1 = ((s8[16777216]{0:T(1024)(128)(4,1)}), s8[4194304]{0:T(1024)(128)(4,1)S(1)}, s32[]{:S(2)}) async-start(s8[16777216]{0:T(1024)(128)(4,1)} %bitcast.11), calls=%async_computation.2 | async-start | bytes 8388608
  1840.9 10.4 slice-start.2
  1840.9 10.4 slice-start.3
  1883.2 18.5 copy-start.5
  1904.2 35.6 %copy-start.1 = (bf16[1024,1024]{1,0:T(8,128)(2,1)S(1)}, bf16[1024,1024]{1,0:T(8,128)(2,1)}, u32[]{:S(2)}) copy-start(bf16[1024,1024]{1,0:T(8,128)(2,1)} %param.26) | copy-start | bytes 6291460
Sparse Core Ops, SparseCore 0:
  55.9 1710.9 all-reduce.6
where the time goes:
time: 1950 us
  waiting for transfers between devices  1680 us (86%)
  other arithmetic  162 us (8%)
  matrix products  48.5 us (2%)
  blocking collectives  33.5 us (2%)
  between operations  25.8 us (1%)
    psum x1, waiting for transfers between devices, matrix_step(): grad_block = lax.psum(part_grad, 'dp')  1680 us
    sub x3, other arithmetic, matrix_step(): return (w_block - step_size * update, new_row, new_col)  56.6 us
    dot_general x4, matrix products, matrix_step(): jnp.einsum('tm,tn->mn', x_block, dy_block, preferred_element_type=jnp.flo...  48.5 us
  transfers between devices with their start and end apart: 1, of which 1 were waited for; matrix products, arithmetic and copies ran while one was open for 2% of the time, Pallas kernels for 0%

commit v1 on v0

v1 whole, which is shorter than its diff:
```python
import functools
import jax
import jax.numpy as jnp
from jax import lax
from jax.experimental import pallas as pl
from jax.experimental.pallas import tpu as pltpu
from jax.sharding import PartitionSpec as P

EPS_ONE = 1e-30
EPS_TWO = 1e-3
MESH = pl.DeviceIdType.MESH
LANES = 128
F32 = jnp.float32
ATTN, GATE, UP, DOWN = range(4)


class Plan:
    def __init__(self, x_mlp, dy_gate, h_mlp, dy_out, mesh):
        self.dp, self.col, self.row = mesh.shape['dp'], mesh.shape['col'], mesh.shape['row']
        self.tok = x_mlp.shape[0]
        self.mc = x_mlp.shape[1]
        self.nc = dy_out.shape[1]
        self.ng = dy_gate.shape[1] // self.nc
        self.nh = h_mlp.shape[1] // self.mc
        self.tq = self.tok // self.row
        self.th = self.tok // self.col
        self.k_gate = 1
        self.k_up = 1 + self.ng
        self.k_out = 1 + 2 * self.ng
        self.k_h = self.k_out + 1
        self.k_xa = self.k_h + self.nh
        self.k_attn = self.k_xa + 1
        self.count = self.k_attn + 1
        self.n_dy = 2 * self.ng + 2
        self.n_x = self.nh + 2
        self.rows = {ATTN: self.mc, GATE: self.mc, UP: self.mc, DOWN: self.mc * self.nh}
        self.cols = {ATTN: self.nc, GATE: self.nc * self.ng, UP: self.nc * self.ng, DOWN: self.nc}

    def is_dy(self, k):
        return ((k >= self.k_gate) & (k <= self.k_out)) | (k == self.k_attn)

    def is_x(self, k):
        return (k == 0) | ((k >= self.k_h) & (k <= self.k_xa))

    def dy_at(self, k):
        return jnp.where(k == self.k_attn, self.n_dy - 1, k - 1)

    def x_at(self, k):
        return jnp.where(k == 0, 0, k - self.k_h + 1)


def kernel(plan, x_attn, dy_attn, x_mlp, dy_gate, dy_up, h_mlp, dy_out, w_attn, w_gate, w_up, w_down,
           r_attn, c_attn, r_gate, c_gate, r_up, c_up, r_down, c_down, hyper,
           g_attn, g_gate, g_up, g_down, nr_attn, nc_attn, nr_gate, nc_gate, nr_up, nc_up, nr_down, nc_down,
           al_attn, be_attn, al_gate, be_gate, al_up, be_up, al_down, be_down, buf_d, buf_x,
           lhs, tile_x, tile_d, grad, w_tile, r_lanes, r_row, c_sum, a_cols, w_sq, u_sq,
           rs_attn, rs_gate, rs_up, rs_down, cs_attn, cs_gate, cs_up, cs_down, st_all,
           z_send, z_recv, f_send, f_recv, c_send, c_recv, r1_send, r1_recv, r2_send, r2_recv, l_sem, g_sem, w_sem):
    p = plan
    z, y, r = lax.axis_index('dp'), lax.axis_index('col'), lax.axis_index('row')
    left, right = lax.rem(z + p.dp - 1, p.dp), lax.rem(z + 1, p.dp)
    w_refs = {ATTN: w_attn, GATE: w_gate, UP: w_up, DOWN: w_down}
    g_refs = {ATTN: g_attn, GATE: g_gate, UP: g_up, DOWN: g_down}
    old = {ATTN: (r_attn, c_attn), GATE: (r_gate, c_gate), UP: (r_up, c_up), DOWN: (r_down, c_down)}
    new = {ATTN: (nr_attn, nc_attn), GATE: (nr_gate, nc_gate), UP: (nr_up, nc_up), DOWN: (nr_down, nc_down)}
    fac = {ATTN: (al_attn, be_attn), GATE: (al_gate, be_gate), UP: (al_up, be_up), DOWN: (al_down, be_down)}
    rs = {ATTN: rs_attn, GATE: rs_gate, UP: rs_up, DOWN: rs_down}
    cs = {ATTN: cs_attn, GATE: cs_gate, UP: cs_up, DOWN: cs_down}

    def flip_row(v):
        bit0, bit1 = lax.rem(r, 2), lax.div(r, 2)
        if v & 1:
            bit0 = 1 - bit0
        if v & 2:
            bit1 = 1 - bit1
        return bit1 * 2 + bit0

    barrier = pltpu.get_barrier_semaphore()
    for to in (left, right):
        pl.semaphore_signal(barrier, inc=1, device_id=(to, y, r), device_id_type=MESH)
    for f in range(2):
        for v in range(4):
            if f or v:
                to_y = 1 - y if f else y
                pl.semaphore_signal(barrier, inc=1, device_id=(z, to_y, flip_row(v)), device_id_type=MESH)
    pl.semaphore_wait(barrier, 9)

    my_q = pl.ds(pl.multiple_of(r * p.tq, p.tq), p.tq)
    x_q = pl.ds(pl.multiple_of(flip_row(2) * p.tq, p.tq), p.tq)
    my_h = pl.ds(pl.multiple_of(y * p.th, p.th), p.th)

    def slot(k, s, dy):
        return buf_d.at[p.dy_at(k), s, my_q, :] if dy else buf_x.at[p.x_at(k), s, my_h, :]

    def ring(k, s, dy, src=None):
        return pltpu.make_async_remote_copy(
            src_ref=slot(k, s - 1, dy) if src is None else src, dst_ref=slot(k, s, dy),
            send_sem=z_send.at[k, s], recv_sem=z_recv.at[k, s],
            device_id=(left, y, r), device_id_type=MESH)

    def spread(k, s, dy):
        to = (z, y, flip_row(2)) if dy else (z, 1 - y, r)
        return pltpu.make_async_remote_copy(
            src_ref=slot(k, s, dy), dst_ref=slot(k, s, dy), send_sem=f_send.at[k, s], recv_sem=f_recv.at[k, s],
            device_id=to, device_id_type=MESH)

    def partner(k, which):
        part = buf_d.at[p.dy_at(k), :, x_q if which else my_q, :]
        return pltpu.make_async_remote_copy(
            src_ref=part, dst_ref=part, send_sem=c_send.at[p.dy_at(k), which], recv_sem=c_recv.at[p.dy_at(k), which],
            device_id=(z, y, flip_row(1)), device_id_type=MESH)

    def cut(ref, at, size):
        return ref.at[:, pl.ds(pl.multiple_of(at * size, size), size)]

    def send_own(k):
        def go(ref, at, size, dy):
            rows = my_q if dy else my_h
            ring(k, 0, dy, ref.at[rows, pl.ds(pl.multiple_of(at * size, size), size)]).start()

        pl.when(k == 0)(lambda: go(x_mlp, 0, p.mc, False))
        pl.when((k >= p.k_gate) & (k < p.k_up))(lambda: go(dy_gate, k - p.k_gate, p.nc, True))
        pl.when((k >= p.k_up) & (k < p.k_out))(lambda: go(dy_up, k - p.k_up, p.nc, True))
        pl.when(k == p.k_out)(lambda: go(dy_out, 0, p.nc, True))
        pl.when((k >= p.k_h) & (k < p.k_xa))(lambda: go(h_mlp, k - p.k_h, p.mc, False))
        pl.when(k == p.k_xa)(lambda: go(x_attn, 0, p.mc, False))
        pl.when(k == p.k_attn)(lambda: go(dy_attn, 0, p.nc, True))

    def arrive(k, s):
        def go(dy):
            ring(k, s, dy).wait_recv() if s else ring(k, 0, dy, slot(k, 0, dy)).wait_recv()
            if s < p.dp - 2:
                ring(k, s + 1, dy).start()
            spread(k, s, dy).start()
            if dy and s == p.dp - 2:
                partner(k, 0).start()

        pl.when(p.is_dy(k))(lambda: go(True))
        pl.when(p.is_x(k))(lambda: go(False))

    def spread_done(k):
        def go(dy):
            for s in range(p.dp - 1):
                spread(k, s, dy).wait_recv()
            if dy:
                partner(k, 1).start()

        pl.when(p.is_dy(k))(lambda: go(True))
        pl.when(p.is_x(k))(lambda: go(False))

    def load(src, at, size, buf, index, dst):
        copies = [pltpu.make_async_copy(cut(src, at, size), dst.at[z], l_sem.at[0])]
        for d in range(1, p.dp):
            copies.append(pltpu.make_async_copy(buf.at[index, d - 1], dst.at[lax.rem(z + d, p.dp)], l_sem.at[d]))
        for c in copies:
            c.start()
        for c in copies:
            c.wait()

    step_t = min(256, p.tok)

    def turn():
        @pl.loop(0, p.dp)
        def _(q):
            @pl.loop(0, p.tok // step_t)
            def _(t):
                at = pl.multiple_of(t * step_t, step_t)
                lhs[q, :, pl.ds(at, step_t)] = tile_x[q, pl.ds(at, step_t), :].T

    step_n = min(512, p.nc)

    def lane_sum(v):
        out = v[:, 0:LANES]
        for i in range(1, v.shape[1] // LANES):
            out = out + v[:, i * LANES:(i + 1) * LANES]
        return out

    def product(b, at):
        r_lanes[...] = jnp.zeros_like(r_lanes)

        @pl.loop(0, p.nc // step_n)
        def _(n):
            cols = pl.ds(pl.multiple_of(n * step_n, step_n), step_n)
            grad[at, :, cols] = jnp.dot(lhs[0], tile_d[b, 0, :, cols], preferred_element_type=F32)

            @pl.loop(1, p.dp)
            def _(q):
                grad[at, :, cols] += jnp.dot(lhs[q], tile_d[b, q, :, cols], preferred_element_type=F32)

            step_r = min(64, p.mc)

            def body(i, acc):
                rows = pl.ds(pl.multiple_of(i * step_r, step_r), step_r)
                block = grad[at, rows, cols]
                sq = block * block + EPS_ONE
                r_lanes[rows, :] += lane_sum(sq)
                return acc + jnp.sum(sq, axis=0, keepdims=True)

            c_sum[at, :, cols] = lax.fori_loop(0, p.mc // step_r, body, jnp.zeros((1, step_n), F32))

    def weigh(mat):
        block = w_tile[...]
        w_sq[mat] += jnp.sum(jnp.reshape(block * block, (p.mc * p.nc // (8 * LANES), 8, LANES)), axis=0)

    def to_row(block):
        return jnp.sum(block.T, axis=0, keepdims=True)

    def chunk(mat, i, b):
        last = mat == DOWN
        at_w = w_refs[mat].at[pl.ds(pl.multiple_of(i * p.mc, p.mc), p.mc), :] if last else cut(w_refs[mat], i, p.nc)
        get_w = pltpu.make_async_copy(at_w, w_tile, w_sem)
        get_w.start()
        product(b, i)
        at_g = g_refs[mat].at[pl.ds(pl.multiple_of(i * p.mc, p.mc), p.mc), :] if last else cut(g_refs[mat], i, p.nc)
        pltpu.make_async_copy(grad.at[i], at_g, g_sem.at[i]).start()
        if last:
            r_row[i] = to_row(r_lanes[...])
        else:
            row = to_row(r_lanes[...])
            r_row[0] = jnp.where(i == 0, row, r_row[0] + row)
        get_w.wait()
        weigh(mat)

    def total_first(mat):
        if mat == DOWN:
            for i in range(p.nh):
                rs[mat][y, :, i * p.mc:(i + 1) * p.mc] = r_row[i]
            block = c_sum[0]
            for i in range(1, p.nh):
                block = block + c_sum[i]
            cs[mat][r] = block
        else:
            rs[mat][y] = r_row[0]
            for i in range(p.cols[mat] // p.nc):
                cs[mat][r, :, i * p.nc:(i + 1) * p.nc] = c_sum[i]
        for c in first_copies(mat):
            c.start()

    def first_copies(mat):
        copies = [pltpu.make_async_remote_copy(
            src_ref=rs[mat].at[y], dst_ref=rs[mat].at[y], send_sem=r1_send.at[mat, 0], recv_sem=r1_recv.at[mat, 0],
            device_id=(z, 1 - y, r), device_id_type=MESH)]
        for v in range(1, 4):
            copies.append(pltpu.make_async_remote_copy(
                src_ref=cs[mat].at[r], dst_ref=cs[mat].at[r], send_sem=r1_send.at[mat, v],
                recv_sem=r1_recv.at[mat, v], device_id=(z, y, flip_row(v)), device_id_type=MESH))
        return copies

    def second_copies(mat):
        me = y * 4 + r
        copies = []
        for f in range(2):
            for v in range(4):
                if f or v:
                    copies.append(pltpu.make_async_remote_copy(
                        src_ref=st_all.at[mat, me], dst_ref=st_all.at[mat, me], send_sem=r2_send.at[mat, f * 4 + v],
                        recv_sem=r2_recv.at[mat, f * 4 + v],
                        device_id=(z, 1 - y if f else y, flip_row(v)), device_id_type=MESH))
        return copies

    def finish(mat):
        beta_two, rho_step, clip_thr = hyper[0], hyper[1], hyper[2]
        m_total, n_total = p.rows[mat] * p.row, p.cols[mat] * p.col
        total_first(mat)
        for c in first_copies(mat):
            c.wait_recv()
        r_new = beta_two * old[mat][0][...] + (1.0 - beta_two) * ((rs[mat][0] + rs[mat][1]) / n_total)
        c_all = ((cs[mat][0] + cs[mat][1]) + cs[mat][2]) + cs[mat][3]
        c_new = beta_two * old[mat][1][...] + (1.0 - beta_two) * (c_all / m_total)
        new[mat][0][...] = r_new
        new[mat][1][...] = c_new
        t_own = jnp.sum(r_new, axis=1, keepdims=True)
        a_row = jnp.sqrt(t_own) / jnp.sqrt(r_new)
        b_row = 1.0 / jnp.sqrt(c_new)
        fac[mat][1][...] = b_row
        parts = p.nh if mat == DOWN else 1
        for i in range(parts):
            a_cols[i] = jnp.broadcast_to(a_row[:, i * p.mc:(i + 1) * p.mc], (LANES, p.mc)).T
        u_sq[...] = jnp.zeros_like(u_sq)
        pieces = p.nh if mat == DOWN else p.cols[mat] // p.nc

        @pl.loop(0, pieces)
        def _(i):
            @pl.loop(0, p.nc // LANES)
            def _(n):
                cols = pl.ds(pl.multiple_of(n * LANES, LANES), LANES)
                if mat == DOWN:
                    a_block, b_block = a_cols[i], fac[mat][1][:, cols]
                else:
                    a_block = a_cols[0]
                    b_block = fac[mat][1][:, pl.ds(pl.multiple_of(i * p.nc + n * LANES, LANES), LANES)]
                upd = grad[i, :, cols] * a_block * b_block
                u_sq[...] += jnp.sum(jnp.reshape(upd * upd, (p.mc // 8, 8, LANES)), axis=0)

        def spot(v):
            return jnp.broadcast_to(jnp.sum(jnp.sum(v, axis=1, keepdims=True), axis=0, keepdims=True), (8, LANES))

        me = y * 4 + r
        st_all[mat, me, 0] = spot(u_sq[...])
        st_all[mat, me, 1] = spot(w_sq[mat])
        st_all[mat, me, 2] = jnp.broadcast_to(t_own, (8, LANES))
        for c in second_copies(mat):
            c.start()
        for c in second_copies(mat):
            c.wait_recv()
        t_all = st_all[mat, 0, 2]
        for i in range(1, p.row):
            t_all = t_all + st_all[mat, i, 2]
        u_all = st_all[mat, 0, 0] * (t_all / st_all[mat, 0, 2])
        w_all = st_all[mat, 0, 1]
        for i in range(1, p.row * p.col):
            u_all = u_all + st_all[mat, i, 0] * (t_all / st_all[mat, i, 2])
            w_all = w_all + st_all[mat, i, 1]
        upd_rms = jnp.sqrt(u_all / (m_total * n_total))
        w_rms = jnp.sqrt(w_all / (m_total * n_total))
        scale = rho_step * jnp.maximum(EPS_TWO, w_rms) / jnp.maximum(1.0, upd_rms / clip_thr)
        scale = scale * jnp.sqrt(t_all / st_all[mat, me, 2])
        fac[mat][0][...] = a_row * scale[0:1, 0:1]

        @pl.loop(0, pieces)
        def _(i):
            at_g = g_refs[mat].at[pl.ds(0, p.mc), pl.ds(0, p.nc)]
            pltpu.make_async_copy(grad.at[i], at_g, g_sem.at[i]).wait()

    def use_dy(k):
        @pl.when(p.is_dy(k))
        def _():
            partner(k, 0).wait_recv()
            partner(k, 1).wait_recv()
        b = jnp.where(k == p.k_out, 1, 0)

        @pl.when((k >= p.k_gate) & (k < p.k_up))
        def _():
            i = k - p.k_gate
            load(dy_gate, i, p.nc, buf_d, p.dy_at(k), tile_d.at[0])
            chunk(GATE, i, 0)
            pl.when(i == p.ng - 1)(lambda: finish(GATE))

        @pl.when((k >= p.k_up) & (k < p.k_out))
        def _():
            i = k - p.k_up
            load(dy_up, i, p.nc, buf_d, p.dy_at(k), tile_d.at[0])
            chunk(UP, i, 0)
            pl.when(i == p.ng - 1)(lambda: finish(UP))

        @pl.when(k == p.k_out)
        def _():
            load(dy_out, 0, p.nc, buf_d, p.dy_at(k), tile_d.at[1])

        @pl.when(k == p.k_attn)
        def _():
            load(dy_attn, 0, p.nc, buf_d, p.dy_at(k), tile_d.at[0])
            chunk(ATTN, 0, 0)
            finish(ATTN)

    def use_x(k):
        @pl.when(k == 0)
        def _():
            load(x_mlp, 0, p.mc, buf_x, 0, tile_x)
            turn()

        @pl.when((k >= p.k_h) & (k < p.k_xa))
        def _():
            i = k - p.k_h
            load(h_mlp, i, p.mc, buf_x, p.x_at(k), tile_x)
            turn()
            chunk(DOWN, i, 1)

        @pl.when(k == p.k_xa)
        def _():
            load(x_attn, 0, p.mc, buf_x, p.x_at(k), tile_x)
            turn()

    w_sq[...] = jnp.zeros_like(w_sq)
    send_own(0)
    send_own(1)

    @pl.loop(0, p.count + 4)
    def _(d):
        pl.when(d < p.count)(lambda: arrive(d, 0))
        pl.when((d >= 1) & (d - 1 < p.count))(lambda: arrive(d - 1, 1))
        pl.when((d >= 2) & (d - 2 < p.count))(lambda: arrive(d - 2, 2))
        pl.when(d + 2 < p.count)(lambda: send_own(d + 2))
        pl.when((d >= 3) & (d - 3 < p.count))(lambda: spread_done(d - 3))
        pl.when(d == p.count + 2)(lambda: finish(DOWN))
        pl.when(d >= 4)(lambda: use_dy(d - 4))
        pl.when((d >= 3) & (d - 3 < p.count))(lambda: use_x(d - 3))

    @pl.loop(0, p.count)
    def _(k):
        def go(dy):
            for s in range(p.dp - 1):
                ring(k, s, dy, slot(k, s, dy)).wait_send()
                spread(k, s, dy).wait_send()
            if dy:
                partner(k, 0).wait_send()
                partner(k, 1).wait_send()

        pl.when(p.is_dy(k))(lambda: go(True))
        pl.when(p.is_x(k))(lambda: go(False))

    for mat in range(4):
        for c in first_copies(mat) + second_copies(mat):
            c.wait_send()


def solution(mesh):
    act_spec = P('dp', 'row')
    grad_spec = P('dp', 'col')
    w_spec = P('row', 'col')
    row_spec = P('row')
    col_spec = P('col')
    in_specs = (act_spec, grad_spec, act_spec, grad_spec, grad_spec, act_spec, grad_spec,
                w_spec, w_spec, w_spec, w_spec,
                row_spec, col_spec, row_spec, col_spec, row_spec, col_spec, row_spec, col_spec, P())
    out_specs = (w_spec, row_spec, col_spec) * 4

    def per_device(x_attn, dy_attn, x_mlp, dy_gate, dy_up, h_mlp, dy_out, w_attn, w_gate, w_up, w_down,
                   r_attn, c_attn, r_gate, c_gate, r_up, c_up, r_down, c_down, hyper_params):
        p = Plan(x_mlp, dy_gate, h_mlp, dy_out, mesh)
        stats = [v.reshape(1, -1) for v in (r_attn, c_attn, r_gate, c_gate, r_up, c_up, r_down, c_down)]
        any_spec = pl.BlockSpec(memory_space=pl.ANY)
        vmem_spec = pl.BlockSpec(memory_space=pltpu.VMEM)
        row_shapes = []
        for mat in (ATTN, GATE, UP, DOWN):
            row_shapes += [jax.ShapeDtypeStruct((1, p.rows[mat]), F32), jax.ShapeDtypeStruct((1, p.cols[mat]), F32)]
        grads = [jax.ShapeDtypeStruct((p.rows[mat], p.cols[mat]), F32) for mat in (ATTN, GATE, UP, DOWN)]
        bf16 = jnp.bfloat16
        bufs = [jax.ShapeDtypeStruct((p.n_dy, p.dp - 1, p.tok, p.nc), bf16),
                jax.ShapeDtypeStruct((p.n_x, p.dp - 1, p.tok, p.mc), bf16)]
        pieces = max(p.ng, p.nh)
        dma = pltpu.SemaphoreType.DMA
        scratch = [
            pltpu.VMEM((p.dp, p.mc, p.tok), bf16),
            pltpu.VMEM((p.dp, p.tok, p.mc), bf16),
            pltpu.VMEM((2, p.dp, p.tok, p.nc), bf16),
            pltpu.VMEM((pieces, p.mc, p.nc), F32),
            pltpu.VMEM((p.mc, p.nc), F32),
            pltpu.VMEM((p.mc, LANES), F32),
            pltpu.VMEM((pieces, 1, p.mc), F32),
            pltpu.VMEM((pieces, 1, p.nc), F32),
            pltpu.VMEM((p.nh, p.mc, LANES), F32),
            pltpu.VMEM((4, 8, LANES), F32),
            pltpu.VMEM((8, LANES), F32),
        ]
        scratch += [pltpu.VMEM((2, 1, p.rows[mat]), F32) for mat in (ATTN, GATE, UP, DOWN)]
        scratch += [pltpu.VMEM((4, 1, p.cols[mat]), F32) for mat in (ATTN, GATE, UP, DOWN)]
        scratch += [
            pltpu.VMEM((4, 8, 3, 8, LANES), F32),
            dma((p.count, p.dp - 1)), dma((p.count, p.dp - 1)),
            dma((p.count, p.dp - 1)), dma((p.count, p.dp - 1)),
            dma((p.n_dy, 2)), dma((p.n_dy, 2)),
            dma((4, 4)), dma((4, 4)), dma((4, 8)), dma((4, 8)),
            dma((p.dp,)), dma((pieces,)), dma(()),
        ]
        out = pl.pallas_call(
            functools.partial(kernel, p),
            out_shape=grads + row_shapes + row_shapes + bufs,
            in_specs=[any_spec] * 11 + [vmem_spec] * 8 + [pl.BlockSpec(memory_space=pltpu.SMEM)],
            out_specs=[any_spec] * 4 + [vmem_spec] * 16 + [any_spec] * 2,
            scratch_shapes=scratch,
            compiler_params=pltpu.CompilerParams(collective_id=0, has_side_effects=True, vmem_limit_bytes=VMEM_LIMIT),
        )(x_attn, dy_attn, x_mlp, dy_gate, dy_up, h_mlp, dy_out, w_attn, w_gate, w_up, w_down, *stats, hyper_params)
        g_all, n_all, f_all = out[:4], out[4:12], out[12:20]
        result = []
        for mat, w_block in enumerate((w_attn, w_gate, w_up, w_down)):
            alpha, beta = f_all[2 * mat].reshape(-1), f_all[2 * mat + 1].reshape(-1)
            result.append(w_block - g_all[mat] * alpha[:, None] * beta[None, :])
            result.append(n_all[2 * mat].reshape(-1))
            result.append(n_all[2 * mat + 1].reshape(-1))
        return tuple(result)

    return jax.shard_map(per_device, mesh=mesh, in_specs=in_specs, out_specs=out_specs, check_vma=False)


VMEM_LIMIT = 66 * 1024 * 1024 // 1024 * 1024 - 3 * 1024 * 1024
```

time: 1950 us -> 1060 us (0.54)
  waiting for transfers between devices: 1680 us -> 0 us
  Pallas kernels: 0 us -> 1000 us
  other arithmetic: 162 us -> 57.4 us
  matrix products: 48.5 us -> 0 us
  blocking collectives: 33.5 us -> 0 us
  between operations: 25.8 us -> 0.76 us
    psum x1 -> x0, waiting for transfers between devices: 1680 us -> none  [matrix_step(): grad_block = lax.psum(part_grad, 'dp')]
    pallas_call x0 -> x1, Pallas kernels: none -> 1000 us  [per_device(): pl.pallas_call(functools.partial(kernel, p), out_shape=grads + row_shapes...]
    reduce_sum x16 -> x0, other arithmetic: 102 us -> none  [the longest x4 34.6 us: matrix_step(): col_sum = lax.psum(jnp.sum(sq_grad, axis=0), 'row')]
    dot_general x4 -> x0, matrix products: 48.5 us -> none  [matrix_step(): jnp.einsum('tm,tn->mn', x_block, dy_block, preferred_element_type=jnp.flo...]
    psum x3 -> x0, blocking collectives: 33.5 us -> none  [the longest x1 13.1 us: matrix_step(): lax.psum(jnp.sum(update * update), ('row', 'col')) / (m_total * n_total)]
  transfers between devices with their start and end apart: 1 -> 0, of which waited for: 1 -> 0; matrix products, arithmetic and copies ran while one was open for 2% -> 0% of each run, Pallas kernels for 0% -> 0%
where the time goes in v1:
time: 1060 us
  Pallas kernels  1000 us (94%)
  other arithmetic  57.4 us (5%)
    pallas_call x1, Pallas kernels, per_device(): pl.pallas_call(functools.partial(kernel, p), out_shape=grads + row_shapes...  1000 us
    sub x3, other arithmetic, per_device(): result.append(w_block - g_all[mat] * alpha[:, None] * beta[None, :])  57.4 us

profile of v1, /device:TPU:0, one launch (start us, length us, event | category | flops | bytes accessed | tf_op | source)
XLA Modules:
  0.0 1064.5 jit_solution(4008340610491644404)
XLA Ops:
  0.7 1001.5 %shard_map.283 = (f32[512,1024]{1,0:T(8,128)}, f32[512,8192]{1,0:T(8,128)}, f32[512,8192]{1,0:T(8,128)}, f32[4096,1024]{1,0:T(8,128)}, f32[1,512]{1,0:T(1,128)},...) custom-call(bf16[1024,512]{1,0:T(8,128)(2,1)} %x_attn.1, ...), custom_call_target="tpu_custom_call" | custom-call | tf_op jit(solution)/shard_map/pallas_call | solution.py:456
  1002.2 3.9 multiply_subtract_fusion.3
  1006.1 0.0 copy-start
  1006.1 0.0 copy-start.1
  1006.1 0.0 copy-start.7
  1006.1 0.0 copy-start.8
  1006.1 18.9 %multiply_subtract_fusion = f32[4096,1024]{1,0:T(8,128)} fusion(f32[4096,1024]{1,0:T(8,128)} %w_down.1, f32[4096,1024]{1,0:T(8,128)} %get-tuple-element.47, f32[1024]{0:T(1024)} %bitcast.33, f32[4096]{0:T(1024)} %bitcast.30), kind=kLoop, calls=%fused_computation | loop fusion | flops 12582912 | bytes 50352128 | tf_op jit(solution)/shard_map/sub | solution.py:468
  1025.0 0.0 copy-done
  1025.0 0.0 copy-done.1
  1025.0 0.0 copy-done.7
  1025.0 0.0 copy-done.8
  1025.0 0.0 copy-start.11
  1025.0 0.0 copy-start.6
  1025.0 0.0 copy-start.10
  1025.0 0.0 copy-start.3
  1025.0 0.0 copy-start.9
  1025.1 0.0 copy-start.2
  1025.1 0.0 copy-start.4
  1025.1 0.0 copy-start.5
  1025.1 34.6 %multiply_subtract_fusion.1 = (f32[512,8192]{1,0:T(8,128)}, f32[512,8192]{1,0:T(8,128)}) fusion(f32[512,8192]{1,0:T(8,128)} %w_up.1, f32[512,8192]{1,0:T(8,128)} %get-tuple-element.42, f32[8192]{0:T(1024)S(1)} %bitcast.27, f32[512]{0:T(512)S(1)} %bitcast.44, f32[512,8192]{1,0:T(8,128)} %w_gate.1, f32[8192]{0:T(1024)S(1)} %bitcast.26, ...), kind=kLoop, calls=%fused_computation.1 | loop fusion | flops 25165824 | bytes 100732928 | tf_op jit(solution)/shard_map/sub | solution.py:468
  1059.7 0.0 copy-done.11
  1059.7 0.6 copy.40
  1060.3 0.0 copy-done.6
  1060.3 0.6 copy.41
  1060.9 0.0 copy-done.10
  1060.9 0.6 copy.42
  1061.5 0.0 copy-done.3
  1061.5 0.6 copy.43
  1062.1 0.0 copy-done.9
  1062.1 0.6 copy.44
  1062.7 0.0 copy-done.2
  1062.7 0.6 copy.45
  1063.3 0.0 copy-done.4
  1063.3 0.6 copy.46
  1063.9 0.0 copy-done.5
  1063.9 0.6 copy.47
Async XLA Ops:
  1006.1 18.9 %copy-start = (f32[1,8192]{1,0:T(1,128)S(1)}, f32[1,8192]{1,0:T(1,128)}, u32[]{:S(2)}) copy-start(f32[1,8192]{1,0:T(1,128)} %get-tuple-element.39) | copy-start | bytes 98308
  1006.1 18.9 %copy-start.1 = (f32[1,8192]{1,0:T(1,128)S(1)}, f32[1,8192]{1,0:T(1,128)}, u32[]{:S(2)}) copy-start(f32[1,8192]{1,0:T(1,128)} %get-tuple-element.44) | copy-start | bytes 98308
  1006.1 18.9 %copy-start.7 = (f32[1,512]{1,0:T(1,128)S(1)}, f32[1,512]{1,0:T(1,128)}, u32[]{:S(2)}) copy-start(f32[1,512]{1,0:T(1,128)} %get-tuple-element.38) | copy-start | bytes 6148
  1006.1 18.9 %copy-start.8 = (f32[1,512]{1,0:T(1,128)S(1)}, f32[1,512]{1,0:T(1,128)}, u32[]{:S(2)}) copy-start(f32[1,512]{1,0:T(1,128)} %get-tuple-element.43) | copy-start | bytes 6148
  1025.0 34.7 %copy-start.11 = (f32[1,512]{1,0:T(1,128)S(1)}, f32[1,512]{1,0:T(1,128)}, u32[]{:S(2)}) copy-start(f32[1,512]{1,0:T(1,128)} %get-tuple-element.35) | copy-start | bytes 6148
  1025.0 35.3 %copy-start.6 = (f32[1,1024]{1,0:T(1,128)S(1)}, f32[1,1024]{1,0:T(1,128)}, u32[]{:S(2)}) copy-start(f32[1,1024]{1,0:T(1,128)} %get-tuple-element.36) | copy-start | bytes 12292
  1025.0 35.9 %copy-start.10 = (f32[1,512]{1,0:T(1,128)S(1)}, f32[1,512]{1,0:T(1,128)}, u32[]{:S(2)}) copy-start(f32[1,512]{1,0:T(1,128)} %get-tuple-element.40) | copy-start | bytes 6148
  1025.0 36.4 %copy-start.3 = (f32[1,8192]{1,0:T(1,128)S(1)}, f32[1,8192]{1,0:T(1,128)}, u32[]{:S(2)}) copy-start(f32[1,8192]{1,0:T(1,128)} %get-tuple-element.41) | copy-start | bytes 98308
  1025.0 37.1 %copy-start.9 = (f32[1,512]{1,0:T(1,128)S(1)}, f32[1,512]{1,0:T(1,128)}, u32[]{:S(2)}) copy-start(f32[1,512]{1,0:T(1,128)} %get-tuple-element.45) | copy-start | bytes 6148
  1025.1 37.6 %copy-start.2 = (f32[1,8192]{1,0:T(1,128)S(1)}, f32[1,8192]{1,0:T(1,128)}, u32[]{:S(2)}) copy-start(f32[1,8192]{1,0:T(1,128)} %get-tuple-element.46) | copy-start | bytes 98308
  1025.1 38.2 %copy-start.4 = (f32[1,4096]{1,0:T(1,128)S(1)}, f32[1,4096]{1,0:T(1,128)}, u32[]{:S(2)}) copy-start(f32[1,4096]{1,0:T(1,128)} %get-tuple-element.50) | copy-start | bytes 49156
  1025.1 38.8 %copy-start.5 = (f32[1,1024]{1,0:T(1,128)S(1)}, f32[1,1024]{1,0:T(1,128)}, u32[]{:S(2)}) copy-start(f32[1,1024]{1,0:T(1,128)} %get-tuple-element.51) | copy-start | bytes 12292

commit v2 on v1

v2 whole, which is shorter than its diff:
```python
import functools
import jax
import jax.numpy as jnp
from jax import lax
from jax.experimental import pallas as pl
from jax.experimental.pallas import tpu as pltpu
from jax.sharding import PartitionSpec as P

EPS_ONE = 1e-30
EPS_TWO = 1e-3
MESH = pl.DeviceIdType.MESH
LANES = 128
F32 = jnp.float32
BF16 = jnp.bfloat16
ATTN, GATE, UP, DOWN = range(4)
MATS = (ATTN, GATE, UP, DOWN)
AHEAD = 2
VMEM_LIMIT = 40 * 1024 * 1024
STORE_LIMIT = 20 * 1024 * 1024
KEPT = (0, 3) + tuple(range(4, 12))


class Plan:
    def __init__(self, x_mlp, dy_gate, h_mlp, dy_out, mesh):
        self.dp, self.col, self.row = mesh.shape['dp'], mesh.shape['col'], mesh.shape['row']
        assert (self.dp, self.col, self.row) == (4, 2, 4)
        self.tok = x_mlp.shape[0]
        self.mc = x_mlp.shape[1]
        self.nc = dy_out.shape[1]
        self.ng = dy_gate.shape[1] // self.nc
        self.nh = h_mlp.shape[1] // self.mc
        self.tq = self.tok // self.row
        self.th = self.tok // self.col
        self.k_gate = 1
        self.k_xa = 1 + self.ng
        self.k_attn = self.k_xa + 1
        self.k_up = self.k_attn + 1
        self.k_out = self.k_up + self.ng
        self.k_h = self.k_out + 1
        self.count = self.k_h + self.nh
        self.n_dy = 2 * self.ng + 2
        self.n_x = self.nh + 2
        self.pieces = max(self.ng, self.nh)
        self.rows = {ATTN: self.mc, GATE: self.mc, UP: self.mc, DOWN: self.mc * self.nh}
        self.cols = {ATTN: self.nc, GATE: self.nc * self.ng, UP: self.nc * self.ng, DOWN: self.nc}
        self.parts = {ATTN: 1, GATE: self.ng, UP: self.ng, DOWN: self.nh}

    def is_dy(self, k):
        return ((k >= self.k_gate) & (k < self.k_xa)) | ((k >= self.k_attn) & (k <= self.k_out))

    def is_x(self, k):
        return (k == 0) | (k == self.k_xa) | (k >= self.k_h)

    def is_attn(self, k):
        return (k == self.k_xa) | (k == self.k_attn)

    def dy_at(self, k):
        return jnp.where(k < self.k_xa, k - 1, k - 2)

    def x_at(self, k):
        return jnp.where(k == 0, 0, jnp.where(k == self.k_xa, 1, k - self.k_h + 2))


def gather_kernel(plan, x_attn, dy_attn, x_mlp, dy_gate, dy_up, h_mlp, dy_out, w_attn, w_gate, w_up, w_down,
                  r_attn, c_attn, r_gate, c_gate, r_up, c_up, r_down, c_down, hyper,
                  o_attn, o_gate, o_up, grad, nr_attn, nc_attn, nr_gate, nc_gate, nr_up, nc_up, nr_down, nc_down,
                  buf_d, buf_x,
                  lhs, tile_x, tile_d, w_buf, r_lanes, r_row, c_sum, a_cols, w_sq, u_sq,
                  b_attn, b_gate, b_up, b_down,
                  rs_attn, rs_gate, rs_up, rs_down, cs_attn, cs_gate, cs_up, cs_down, st_all,
                  z_send, z_recv, f_send, f_recv, c_send, c_recv, r1_send, r1_recv, r2_send, r2_recv,
                  e_send, e_recv, l_sem, wi_sem, wo_sem):
    p = plan
    z, y, r = lax.axis_index('dp'), lax.axis_index('col'), lax.axis_index('row')
    low = z < 2
    mid = (z == 1) | (z == 2)
    end_z = jnp.where(low, 0, 3)
    mate_z = 3 - z
    w_refs = {ATTN: w_attn, GATE: w_gate, UP: w_up, DOWN: w_down}
    old = {ATTN: (r_attn, c_attn), GATE: (r_gate, c_gate), UP: (r_up, c_up), DOWN: (r_down, c_down)}
    new = {ATTN: (nr_attn, nc_attn), GATE: (nr_gate, nc_gate), UP: (nr_up, nc_up), DOWN: (nr_down, nc_down)}
    b_rows = {ATTN: b_attn, GATE: b_gate, UP: b_up, DOWN: b_down}
    rs = {ATTN: rs_attn, GATE: rs_gate, UP: rs_up, DOWN: rs_down}
    cs = {ATTN: cs_attn, GATE: cs_gate, UP: cs_up, DOWN: cs_down}

    def flip_row(v):
        bit0, bit1 = lax.rem(r, 2), lax.div(r, 2)
        if v & 1:
            bit0 = 1 - bit0
        if v & 2:
            bit1 = 1 - bit1
        return bit1 * 2 + bit0

    peers = [(f, v) for f in range(2) for v in range(4) if f or v]
    barrier = pltpu.get_barrier_semaphore()
    for f, v in peers:
        pl.semaphore_signal(barrier, inc=1, device_id=(z, 1 - y if f else y, flip_row(v)), device_id_type=MESH)

    @pl.when(mid)
    def _():
        pl.semaphore_signal(barrier, inc=1, device_id=(end_z, y, r), device_id_type=MESH)
        pl.semaphore_signal(barrier, inc=1, device_id=(mate_z, y, r), device_id_type=MESH)
        pl.semaphore_wait(barrier, len(peers) + 2)

    @pl.when(jnp.logical_not(mid))
    def _():
        pl.semaphore_signal(barrier, inc=1, device_id=(jnp.where(low, 1, 2), y, r), device_id_type=MESH)
        pl.semaphore_wait(barrier, len(peers) + 1)

    my_q = pl.ds(pl.multiple_of(r * p.tq, p.tq), p.tq)
    x_q = pl.ds(pl.multiple_of(flip_row(2) * p.tq, p.tq), p.tq)
    my_h = pl.ds(pl.multiple_of(y * p.th, p.th), p.th)

    def slot(k, s, dy):
        return buf_d.at[p.dy_at(k), s, my_q, :] if dy else buf_x.at[p.x_at(k), s, my_h, :]

    def pass_on(k, dy, src, to_z, to_slot, sem):
        return pltpu.make_async_remote_copy(
            src_ref=src, dst_ref=slot(k, to_slot, dy), send_sem=z_send.at[k, sem], recv_sem=z_recv.at[k, to_slot],
            device_id=(to_z, y, r), device_id_type=MESH)

    def spread(k, s, dy):
        to = (z, y, flip_row(2)) if dy else (z, 1 - y, r)
        return pltpu.make_async_remote_copy(
            src_ref=slot(k, s, dy), dst_ref=slot(k, s, dy), send_sem=f_send.at[k, s], recv_sem=f_recv.at[k, s],
            device_id=to, device_id_type=MESH)

    def partner(k, which):
        part = buf_d.at[p.dy_at(k), :, x_q if which else my_q, :]
        return pltpu.make_async_remote_copy(
            src_ref=part, dst_ref=part, send_sem=c_send.at[p.dy_at(k), which], recv_sem=c_recv.at[p.dy_at(k), which],
            device_id=(z, y, flip_row(1)), device_id_type=MESH)

    def typed(k, go):
        used = mid | jnp.logical_not(p.is_attn(k))
        pl.when(p.is_dy(k) & used)(lambda: go(True))
        pl.when(p.is_x(k) & used)(lambda: go(False))

    def cut(ref, at, size):
        return ref.at[:, pl.ds(pl.multiple_of(at * size, size), size)]

    def down_rows(ref, i):
        return ref.at[pl.ds(pl.multiple_of(i * p.mc, p.mc), p.mc), :]

    def own_to(k, dy, src):
        @pl.when(jnp.logical_not(mid))
        def _():
            pass_on(k, dy, src, jnp.where(low, 1, 2), jnp.where(low, 2, 0), 0).start()

        @pl.when(mid)
        def _():
            @pl.when(jnp.logical_not(p.is_attn(k)))
            def _():
                pass_on(k, dy, src, end_z, jnp.where(low, 0, 2), 0).start()
            pass_on(k, dy, src, mate_z, jnp.where(low, 2, 0), 1).start()

    def send_own(k):
        def go(ref, at, size, dy):
            own_to(k, dy, ref.at[my_q if dy else my_h, pl.ds(pl.multiple_of(at * size, size), size)])

        pl.when(k == 0)(lambda: go(x_mlp, 0, p.mc, False))
        pl.when((k >= p.k_gate) & (k < p.k_xa))(lambda: go(dy_gate, k - p.k_gate, p.nc, True))
        pl.when(k == p.k_xa)(lambda: go(x_attn, 0, p.mc, False))
        pl.when(k == p.k_attn)(lambda: go(dy_attn, 0, p.nc, True))
        pl.when((k >= p.k_up) & (k < p.k_out))(lambda: go(dy_up, k - p.k_up, p.nc, True))
        pl.when(k == p.k_out)(lambda: go(dy_out, 0, p.nc, True))
        pl.when(k >= p.k_h)(lambda: go(h_mlp, k - p.k_h, p.mc, False))

    def own_first_left(k):
        @pl.when(jnp.logical_not(mid & p.is_attn(k)))
        def _():
            pl.when(p.is_dy(k))(lambda: pass_on(k, True, slot(k, 0, True), z, 0, 0).wait_send())
            pl.when(p.is_x(k))(lambda: pass_on(k, False, slot(k, 0, False), z, 0, 0).wait_send())

    def arrive(k, turn_no):
        e = jnp.where(mid, lax.rem(turn_no + 2, 3), turn_no)
        s = jnp.where(low, e, 2 - e)

        def go(dy):
            pass_on(k, dy, slot(k, s, dy), z, s, 0).wait_recv()

            @pl.when(mid & (e == 2))
            def _():
                pass_on(k, dy, slot(k, s, dy), mate_z, 1, 4).start()

            @pl.when(mid & (e < 2) & jnp.logical_not(p.is_attn(k)))
            def _():
                pass_on(k, dy, slot(k, s, dy), end_z, jnp.where(low, s + 1, s - 1), 2 + e).start()

            spread(k, s, dy).start()
            if dy and turn_no == 2:
                partner(k, 0).start()

        typed(k, go)

    def spread_done(k):
        def go(dy):
            for s in range(p.dp - 1):
                spread(k, s, dy).wait_recv()
            if dy:
                partner(k, 1).start()

        typed(k, go)

    def load(src, at, size, buf, index, dst):
        copies = [pltpu.make_async_copy(cut(src, at, size), dst.at[z], l_sem.at[0])]
        for d in range(1, p.dp):
            copies.append(pltpu.make_async_copy(buf.at[index, d - 1], dst.at[lax.rem(z + d, p.dp)], l_sem.at[d]))
        for c in copies:
            c.start()
        for c in copies:
            c.wait()

    step_t = min(256, p.tok)

    def turn():
        @pl.loop(0, p.dp)
        def _(q):
            @pl.loop(0, p.tok // step_t)
            def _(t):
                at = pl.multiple_of(t * step_t, step_t)
                lhs[q, :, pl.ds(at, step_t)] = tile_x[q, pl.ds(at, step_t), :].T

    step_n = min(512, p.nc)
    step_r = min(64, p.mc)

    def lane_sum(v):
        out = v[:, 0:LANES]
        for i in range(1, v.shape[1] // LANES):
            out = out + v[:, i * LANES:(i + 1) * LANES]
        return out

    def product(at):
        r_lanes[...] = jnp.zeros_like(r_lanes)

        @pl.loop(0, p.nc // step_n)
        def _(n):
            cols = pl.ds(pl.multiple_of(n * step_n, step_n), step_n)
            grad[at, :, cols] = jnp.dot(lhs[0], tile_d[0, :, cols], preferred_element_type=F32)

            @pl.loop(1, p.dp)
            def _(q):
                grad[at, :, cols] += jnp.dot(lhs[q], tile_d[q, :, cols], preferred_element_type=F32)

            def body(i, acc):
                rows = pl.ds(pl.multiple_of(i * step_r, step_r), step_r)
                block = grad[at, rows, cols]
                sq = block * block + EPS_ONE
                r_lanes[rows, :] += lane_sum(sq)
                return acc + jnp.sum(sq, axis=0, keepdims=True)

            c_sum[at, :, cols] = lax.fori_loop(0, p.mc // step_r, body, jnp.zeros((1, step_n), F32))

    def to_row(block):
        return jnp.sum(block.T, axis=0, keepdims=True)

    def get_w(mat, i):
        src = down_rows(w_refs[mat], i) if mat == DOWN else cut(w_refs[mat], i, p.nc)
        return pltpu.make_async_copy(src, w_buf.at[lax.rem(i, 3)], wi_sem.at[lax.rem(i, 3)])

    def put_w(mat, i):
        dst = cut(o_gate if mat == GATE else o_up, i, p.nc)
        return pltpu.make_async_copy(w_buf.at[lax.rem(i, 3)], dst, wo_sem.at[lax.rem(i, 3)])

    def chunk(mat, i):
        get_w(mat, i).start()
        product(i)
        row = to_row(r_lanes[...])
        if mat == DOWN:
            r_row[i] = row
        else:
            r_row[0] = jnp.where(i == 0, row, r_row[0] + row)
        get_w(mat, i).wait()

        def body(n, acc):
            rows = pl.ds(pl.multiple_of(n * step_r, step_r), step_r)
            block = lane_sum(w_buf[lax.rem(i, 3), rows, :] * w_buf[lax.rem(i, 3), rows, :])
            return acc + jnp.sum(jnp.reshape(block, (step_r // 8, 8, LANES)), axis=0)

        w_sq[mat] += lax.fori_loop(0, p.mc // step_r, body, jnp.zeros((8, LANES), F32))

    def first_copies(mat):
        copies = [pltpu.make_async_remote_copy(
            src_ref=rs[mat].at[y], dst_ref=rs[mat].at[y], send_sem=r1_send.at[mat, 0], recv_sem=r1_recv.at[mat, 0],
            device_id=(z, 1 - y, r), device_id_type=MESH)]
        for v in range(1, 4):
            copies.append(pltpu.make_async_remote_copy(
                src_ref=cs[mat].at[r], dst_ref=cs[mat].at[r], send_sem=r1_send.at[mat, v],
                recv_sem=r1_recv.at[mat, v], device_id=(z, y, flip_row(v)), device_id_type=MESH))
        return copies

    def second_copies(mat):
        me = y * 4 + r
        return [pltpu.make_async_remote_copy(
            src_ref=st_all.at[mat, me], dst_ref=st_all.at[mat, me], send_sem=r2_send.at[mat, f * 4 + v],
            recv_sem=r2_recv.at[mat, f * 4 + v], device_id=(z, 1 - y if f else y, flip_row(v)), device_id_type=MESH)
            for f, v in peers]

    def finish(mat):
        beta_two, rho_step, clip_thr = hyper[0], hyper[1], hyper[2]
        m_total, n_total = p.rows[mat] * p.row, p.cols[mat] * p.col
        parts = p.parts[mat]
        for i in range(min(2, parts)):
            get_w(mat, jnp.int32(i)).start()
        if mat == DOWN:
            block = c_sum[0]
            for i in range(parts):
                rs[mat][y, :, i * p.mc:(i + 1) * p.mc] = r_row[i]
                if i:
                    block = block + c_sum[i]
            cs[mat][r] = block
        else:
            rs[mat][y] = r_row[0]
            for i in range(parts):
                cs[mat][r, :, i * p.nc:(i + 1) * p.nc] = c_sum[i]
        for c in first_copies(mat):
            c.start()
        for c in first_copies(mat):
            c.wait_recv()
        r_new = beta_two * old[mat][0][...] + (1.0 - beta_two) * ((rs[mat][0] + rs[mat][1]) / n_total)
        c_all = ((cs[mat][0] + cs[mat][1]) + cs[mat][2]) + cs[mat][3]
        c_new = beta_two * old[mat][1][...] + (1.0 - beta_two) * (c_all / m_total)
        new[mat][0][...] = r_new
        new[mat][1][...] = c_new
        t_own = jnp.sum(r_new, axis=1, keepdims=True)
        a_row = jnp.sqrt(t_own) / jnp.sqrt(r_new)
        b_rows[mat][...] = 1.0 / jnp.sqrt(c_new)
        for i in range(parts if mat == DOWN else 1):
            a_cols[i] = jnp.broadcast_to(a_row[:, i * p.mc:(i + 1) * p.mc], (LANES, p.mc)).T
        u_sq[...] = jnp.zeros_like(u_sq)
        groups = p.nc // LANES

        def factors(i, n):
            if mat == DOWN:
                return a_cols[i], b_rows[mat][:, pl.ds(pl.multiple_of(n * LANES, LANES), LANES)]
            return a_cols[0], b_rows[mat][:, pl.ds(pl.multiple_of(i * p.nc + n * LANES, LANES), LANES)]

        @pl.loop(0, parts * groups)
        def _(j):
            i, n = lax.div(j, groups), lax.rem(j, groups)
            a_block, b_block = factors(i, n)
            upd = grad[i, :, pl.ds(pl.multiple_of(n * LANES, LANES), LANES)] * a_block * b_block
            u_sq[...] += jnp.sum(jnp.reshape(upd * upd, (p.mc // 8, 8, LANES)), axis=0)

        def spot(v):
            return jnp.broadcast_to(jnp.sum(jnp.sum(v, axis=1, keepdims=True), axis=0, keepdims=True), (8, LANES))

        me = y * 4 + r
        st_all[mat, me, 0] = spot(u_sq[...])
        st_all[mat, me, 1] = spot(w_sq[mat])
        st_all[mat, me, 2] = jnp.broadcast_to(t_own, (8, LANES))
        for c in second_copies(mat):
            c.start()
        for c in second_copies(mat):
            c.wait_recv()
        t_all = st_all[mat, 0, 2]
        for i in range(1, p.row):
            t_all = t_all + st_all[mat, i, 2]
        u_all = st_all[mat, 0, 0] * (t_all / st_all[mat, 0, 2])
        w_all = st_all[mat, 0, 1]
        for i in range(1, p.row * p.col):
            u_all = u_all + st_all[mat, i, 0] * (t_all / st_all[mat, i, 2])
            w_all = w_all + st_all[mat, i, 1]
        upd_rms = jnp.sqrt(u_all / (m_total * n_total))
        w_rms = jnp.sqrt(w_all / (m_total * n_total))
        scale = rho_step * jnp.maximum(EPS_TWO, w_rms) / jnp.maximum(1.0, upd_rms / clip_thr)
        scale = scale * jnp.sqrt(t_all / st_all[mat, me, 2])
        b_rows[mat][...] = b_rows[mat][...] * scale[0:1, 0:1]

        @pl.loop(0, parts)
        def _(i):
            at = lax.rem(i, 3)
            get_w(mat, i).wait()

            @pl.loop(0, groups)
            def _(n):
                cols = pl.ds(pl.multiple_of(n * LANES, LANES), LANES)
                a_block, b_block = factors(i, n)
                fresh = w_buf[at, :, cols] - grad[i, :, cols] * a_block * b_block
                if mat == ATTN:
                    o_attn[:, cols] = fresh
                elif mat == DOWN:
                    grad[i, :, cols] = fresh
                else:
                    w_buf[at, :, cols] = fresh

            if mat in (GATE, UP):
                put_w(mat, i).start()
                pl.when(i >= 1)(lambda: put_w(mat, i - 1).wait())
            pl.when(i + 2 < parts)(lambda: get_w(mat, i + 2).start())

        if mat in (GATE, UP):
            put_w(mat, jnp.int32(parts - 1)).wait()

    def use_dy(k):
        @pl.when((k >= p.k_gate) & (k < p.k_xa))
        def _():
            i = k - p.k_gate
            load(dy_gate, i, p.nc, buf_d, p.dy_at(k), tile_d)
            chunk(GATE, i)
            pl.when(i == p.ng - 1)(lambda: finish(GATE))

        @pl.when((k == p.k_attn) & mid)
        def _():
            load(dy_attn, 0, p.nc, buf_d, p.dy_at(k), tile_d)
            chunk(ATTN, jnp.int32(0))
            finish(ATTN)

        @pl.when((k >= p.k_up) & (k < p.k_out))
        def _():
            i = k - p.k_up

            @pl.when(i == 0)
            def _():
                load(x_mlp, 0, p.mc, buf_x, 0, tile_x)
                turn()

            load(dy_up, i, p.nc, buf_d, p.dy_at(k), tile_d)
            chunk(UP, i)
            pl.when(i == p.ng - 1)(lambda: finish(UP))

        pl.when(k == p.k_out)(lambda: load(dy_out, 0, p.nc, buf_d, p.dy_at(k), tile_d))

    def got_partner(k):
        @pl.when(p.is_dy(k) & (mid | jnp.logical_not(p.is_attn(k))))
        def _():
            partner(k, 0).wait_recv()
            partner(k, 1).wait_recv()

    def use_x(k):
        @pl.when(k == 0)
        def _():
            load(x_mlp, 0, p.mc, buf_x, 0, tile_x)
            turn()

        @pl.when((k == p.k_xa) & mid)
        def _():
            load(x_attn, 0, p.mc, buf_x, p.x_at(k), tile_x)
            turn()

        @pl.when(k >= p.k_h)
        def _():
            i = k - p.k_h
            load(h_mlp, i, p.mc, buf_x, p.x_at(k), tile_x)
            turn()
            chunk(DOWN, i)
            pl.when(i == p.nh - 1)(lambda: finish(DOWN))

    def to_end():
        pairs = ((o_attn, o_attn), (nr_attn, nr_attn), (nc_attn, nc_attn))
        return [pltpu.make_async_remote_copy(
            src_ref=a, dst_ref=b, send_sem=e_send.at[i], recv_sem=e_recv.at[i],
            device_id=(end_z, y, r), device_id_type=MESH) for i, (a, b) in enumerate(pairs)]

    w_sq[...] = jnp.zeros_like(w_sq)
    for k in range(AHEAD):
        send_own(jnp.int32(k))

    @pl.loop(0, p.count + 1)
    def _(d):
        pl.when(d >= 1)(lambda: own_first_left(d - 1))

        @pl.when(d < p.count)
        def _():
            for i in range(3):
                arrive(d, i)

        pl.when(d + AHEAD < p.count)(lambda: send_own(d + AHEAD))

        @pl.when((d == p.count - 1) & mid)
        def _():
            for c in to_end():
                c.start()

        pl.when(d >= 1)(lambda: spread_done(d - 1))

        @pl.when(d >= 2)
        def _():
            got_partner(d - 2)
            use_dy(d - 2)

        pl.when(d >= 1)(lambda: use_x(d - 1))

    @pl.loop(0, p.count)
    def _(k):
        def go(dy):
            some = slot(k, 0, dy)

            @pl.when(mid)
            def _():
                pass_on(k, dy, some, z, 0, 1).wait_send()
                pass_on(k, dy, some, z, 0, 4).wait_send()

                @pl.when(jnp.logical_not(p.is_attn(k)))
                def _():
                    pass_on(k, dy, some, z, 0, 2).wait_send()
                    pass_on(k, dy, some, z, 0, 3).wait_send()

            for s in range(p.dp - 1):
                spread(k, s, dy).wait_send()
            if dy:
                partner(k, 0).wait_send()
                partner(k, 1).wait_send()

        typed(k, go)

    for mat in (GATE, UP, DOWN):
        for c in first_copies(mat) + second_copies(mat):
            c.wait_send()

    @pl.when(mid)
    def _():
        for c in first_copies(ATTN) + second_copies(ATTN):
            c.wait_send()
        for c in to_end():
            c.wait_send()

    @pl.when(jnp.logical_not(mid))
    def _():
        for c in to_end():
            c.wait_recv()


def store_kernel(plan, o_attn, o_gate, o_up, o_down, *refs):
    p = plan
    stats, (w_attn, w_gate, w_up, w_down), outs = refs[:8], refs[8:12], refs[12:20]
    bounce, in_sem, out_sem, s_sem = refs[20:]
    depth = bounce.shape[0]

    def cut(ref, i):
        return ref.at[:, i * p.nc:(i + 1) * p.nc]

    through = [(cut(o_gate, i), cut(w_gate, i)) for i in range(p.ng)] + [(cut(o_up, i), cut(w_up, i)) for i in range(p.ng)]
    loads = [pltpu.make_async_copy(a, bounce.at[i % depth], in_sem.at[i]) for i, (a, _) in enumerate(through)]
    puts = [pltpu.make_async_copy(bounce.at[i % depth], b, out_sem.at[i]) for i, (_, b) in enumerate(through)]
    for c in loads[:depth]:
        c.start()
    copies = [pltpu.make_async_copy(a, b, s_sem.at[i]) for i, (a, b) in enumerate(zip(stats, outs))]
    copies.append(pltpu.make_async_copy(o_attn, w_attn, s_sem.at[8]))
    for i in range(p.nh):
        copies.append(pltpu.make_async_copy(o_down.at[i], w_down.at[i * p.mc:(i + 1) * p.mc, :], s_sem.at[9 + i]))
    for c in copies:
        c.start()
    for i in range(len(through)):
        loads[i].wait()
        puts[i].start()
        again = i - depth // 2
        if 0 <= again and again + depth < len(through):
            puts[again].wait()
            loads[again + depth].start()
    for i in range(max(0, len(through) - depth), len(through)):
        puts[i].wait()
    for c in copies:
        c.wait()


def solution(mesh):
    act_spec = P('dp', 'row')
    grad_spec = P('dp', 'col')
    w_spec = P('row', 'col')
    row_spec = P('row')
    col_spec = P('col')
    in_specs = (act_spec, grad_spec, act_spec, grad_spec, grad_spec, act_spec, grad_spec,
                w_spec, w_spec, w_spec, w_spec,
                row_spec, col_spec, row_spec, col_spec, row_spec, col_spec, row_spec, col_spec, P())
    out_specs = (w_spec, row_spec, col_spec) * 4

    def per_device(x_attn, dy_attn, x_mlp, dy_gate, dy_up, h_mlp, dy_out, w_attn, w_gate, w_up, w_down,
                   r_attn, c_attn, r_gate, c_gate, r_up, c_up, r_down, c_down, hyper_params):
        p = Plan(x_mlp, dy_gate, h_mlp, dy_out, mesh)
        stats = [v.reshape(1, -1) for v in (r_attn, c_attn, r_gate, c_gate, r_up, c_up, r_down, c_down)]
        any_spec = pl.BlockSpec(memory_space=pl.ANY)
        vmem_spec = pl.BlockSpec(memory_space=pltpu.VMEM)
        row_shapes = []
        for mat in MATS:
            row_shapes += [jax.ShapeDtypeStruct((1, p.rows[mat]), F32), jax.ShapeDtypeStruct((1, p.cols[mat]), F32)]
        w_shapes = [jax.ShapeDtypeStruct((p.rows[mat], p.cols[mat]), F32) for mat in MATS]
        o_shapes = [pltpu.VMEM((p.mc, p.nc), F32), w_shapes[GATE], w_shapes[UP],
                    pltpu.VMEM((p.pieces, p.mc, p.nc), F32)]
        bufs = [jax.ShapeDtypeStruct((p.n_dy, p.dp - 1, p.tok, p.nc), BF16),
                jax.ShapeDtypeStruct((p.n_x, p.dp - 1, p.tok, p.mc), BF16)]
        dma = pltpu.SemaphoreType.DMA
        scratch = [
            pltpu.VMEM((p.dp, p.mc, p.tok), BF16),
            pltpu.VMEM((p.dp, p.tok, p.mc), BF16),
            pltpu.VMEM((p.dp, p.tok, p.nc), BF16),
            pltpu.VMEM((3, p.mc, p.nc), F32),
            pltpu.VMEM((p.mc, LANES), F32),
            pltpu.VMEM((p.pieces, 1, p.mc), F32),
            pltpu.VMEM((p.pieces, 1, p.nc), F32),
            pltpu.VMEM((p.nh, p.mc, LANES), F32),
            pltpu.VMEM((4, 8, LANES), F32),
            pltpu.VMEM((8, LANES), F32),
        ]
        scratch += [pltpu.VMEM((1, p.cols[mat]), F32) for mat in MATS]
        scratch += [pltpu.VMEM((2, 1, p.rows[mat]), F32) for mat in MATS]
        scratch += [pltpu.VMEM((4, 1, p.cols[mat]), F32) for mat in MATS]
        scratch += [
            pltpu.VMEM((4, 8, 3, 8, LANES), F32),
            dma((p.count, 5)), dma((p.count, p.dp - 1)),
            dma((p.count, p.dp - 1)), dma((p.count, p.dp - 1)),
            dma((p.n_dy, 2)), dma((p.n_dy, 2)),
            dma((4, 4)), dma((4, 4)), dma((4, 8)), dma((4, 8)),
            dma((3,)), dma((3,)),
            dma((p.dp,)), dma((3,)), dma((3,)),
        ]
        out = pl.pallas_call(
            functools.partial(gather_kernel, p),
            out_shape=o_shapes + [pltpu.VMEM(v.shape, F32) for v in row_shapes] + bufs,
            in_specs=[any_spec] * 11 + [vmem_spec] * 8 + [pl.BlockSpec(memory_space=pltpu.SMEM)],
            out_specs=[vmem_spec, any_spec, any_spec, vmem_spec] + [vmem_spec] * 8 + [any_spec] * 2,
            scratch_shapes=scratch,
            compiler_params=pltpu.CompilerParams(collective_id=0, has_side_effects=True, vmem_limit_bytes=VMEM_LIMIT),
        )(x_attn, dy_attn, x_mlp, dy_gate, dy_up, h_mlp, dy_out, w_attn, w_gate, w_up, w_down, *stats, hyper_params)
        res = pl.pallas_call(
            functools.partial(store_kernel, p),
            out_shape=w_shapes + row_shapes,
            in_specs=[vmem_spec, any_spec, any_spec, vmem_spec] + [vmem_spec] * 8,
            out_specs=[any_spec] * 12,
            scratch_shapes=[pltpu.VMEM((8, p.mc, p.nc), F32), dma((2 * p.ng,)), dma((2 * p.ng,)), dma((9 + p.nh,))],
            compiler_params=pltpu.CompilerParams(vmem_limit_bytes=STORE_LIMIT),
        )(*[pltpu.with_memory_space_constraint(v, pltpu.VMEM) if i in KEPT else v for i, v in enumerate(out[:12])])
        result = []
        for mat in MATS:
            result += [res[mat], res[4 + 2 * mat].reshape(-1), res[5 + 2 * mat].reshape(-1)]
        return tuple(result)

    return jax.shard_map(per_device, mesh=mesh, in_specs=in_specs, out_specs=out_specs, check_vma=False)
```

time: 1060 us -> 1070 us (level)
  Pallas kernels: 1000 us -> 1070 us
  other arithmetic: 57.4 us -> 0 us
    pallas_call x1 -> x2, Pallas kernels: 1000 us -> 1070 us  [the longest x1 1040 us: per_device(): pl.pallas_call(functools.partial(gather_kernel, p), out_shape=o_shapes +...]
    sub x3 -> x0, other arithmetic: 57.4 us -> none  [per_device(): result.append(w_block - g_all[mat] * alpha[:, None] * beta[None, :])]
where the time goes in v2:
time: 1070 us
  Pallas kernels  1070 us (100%)
    pallas_call x1, Pallas kernels, per_device(): pl.pallas_call(functools.partial(gather_kernel, p), out_shape=o_shapes +...  1040 us
    pallas_call x1, Pallas kernels, per_device(): pl.pallas_call(functools.partial(store_kernel, p), out_shape=w_shapes + r...  29.1 us

profile of v2, /device:TPU:0, one launch (start us, length us, event | category | flops | bytes accessed | tf_op | source)
XLA Modules:
  0.0 1072.7 jit_solution(2260124734209023428)
XLA Ops:
  0.7 1043.0 %shard_map.283 = (f32[512,1024]{1,0:T(8,128)S(1)}, f32[512,8192]{1,0:T(8,128)}, f32[512,8192]{1,0:T(8,128)}, f32[8,512,1024]{2,1,0:T(8,128)S(1)}, f32[1,512]{1,0...) custom-call(bf16[1024,512]{1,0:T(8,128)(2,1)} %x_attn.1, ...), custom_call_target="tpu_custom_call" | custom-call | tf_op jit(solution)/shard_map/pallas_call | solution.py:607
  1043.6 29.1 %shard_map.284 = (f32[512,1024]{1,0:T(8,128)}, f32[512,8192]{1,0:T(8,128)}, f32[512,8192]{1,0:T(8,128)}, f32[4096,1024]{1,0:T(8,128)}, f32[1,512]{1,0:T(1,128)},...) custom-call(f32[512,1024]{1,0:T(8,128)S(1)} %get-tuple-element.36.o_, ...), custom_call_target="tpu_custom_call" | custom-call | tf_op jit(solution)/shard_map/pallas_call | solution.py:615

commit v3 on v2

--- a/solution.py
+++ b/solution.py
@@ -14,7 +14,8 @@
 BF16 = jnp.bfloat16
 ATTN, GATE, UP, DOWN = range(4)
 MATS = (ATTN, GATE, UP, DOWN)
-AHEAD = 2
+AHEAD = 3
+LATE = 3
 VMEM_LIMIT = 40 * 1024 * 1024
 STORE_LIMIT = 20 * 1024 * 1024
 KEPT = (0, 3) + tuple(range(4, 12))
@@ -65,7 +66,7 @@
                   r_attn, c_attn, r_gate, c_gate, r_up, c_up, r_down, c_down, hyper,
                   o_attn, o_gate, o_up, grad, nr_attn, nc_attn, nr_gate, nc_gate, nr_up, nc_up, nr_down, nc_down,
                   buf_d, buf_x,
-                  lhs, tile_x, tile_d, w_buf, r_lanes, r_row, c_sum, a_cols, w_sq, u_sq,
+                  lhs, tile_x, tile_d, w_buf, r_lanes, r_row, c_sum, a_cols, w_sq,
                   b_attn, b_gate, b_up, b_down,
                   rs_attn, rs_gate, rs_up, rs_down, cs_attn, cs_gate, cs_up, cs_down, st_all,
                   z_send, z_recv, f_send, f_recv, c_send, c_recv, r1_send, r1_recv, r2_send, r2_recv,
@@ -193,14 +194,9 @@
 
         typed(k, go)
 
-    def spread_done(k):
-        def go(dy):
-            for s in range(p.dp - 1):
-                spread(k, s, dy).wait_recv()
-            if dy:
-                partner(k, 1).start()
-
-        typed(k, go)
+    def spread_done(k, dy):
+        for s in range(p.dp - 1):
+            spread(k, s, dy).wait_recv()
 
     def load(src, at, size, buf, index, dst):
         copies = [pltpu.make_async_copy(cut(src, at, size), dst.at[z], l_sem.at[0])]
@@ -250,6 +246,12 @@
                 return acc + jnp.sum(sq, axis=0, keepdims=True)
 
             c_sum[at, :, cols] = lax.fori_loop(0, p.mc // step_r, body, jnp.zeros((1, step_n), F32))
+
+    def fold(v):
+        v = jnp.reshape(v, (v.shape[0] // 8, 8, LANES))
+        while v.shape[0] > 1:
+            v = v[:v.shape[0] // 2] + v[v.shape[0] // 2:]
+        return v[0]
 
     def to_row(block):
         return jnp.sum(block.T, axis=0, keepdims=True)
@@ -275,7 +277,7 @@
         def body(n, acc):
             rows = pl.ds(pl.multiple_of(n * step_r, step_r), step_r)
             block = lane_sum(w_buf[lax.rem(i, 3), rows, :] * w_buf[lax.rem(i, 3), rows, :])
-            return acc + jnp.sum(jnp.reshape(block, (step_r // 8, 8, LANES)), axis=0)
+            return acc + fold(block)
 
         w_sq[mat] += lax.fori_loop(0, p.mc // step_r, body, jnp.zeros((8, LANES), F32))
 
@@ -327,26 +329,29 @@
         b_rows[mat][...] = 1.0 / jnp.sqrt(c_new)
         for i in range(parts if mat == DOWN else 1):
             a_cols[i] = jnp.broadcast_to(a_row[:, i * p.mc:(i + 1) * p.mc], (LANES, p.mc)).T
-        u_sq[...] = jnp.zeros_like(u_sq)
-        groups = p.nc // LANES
+        blocks = p.mc // step_r
 
         def factors(i, n):
+            rows = pl.ds(pl.multiple_of(n * step_r, step_r), step_r)
             if mat == DOWN:
-                return a_cols[i], b_rows[mat][:, pl.ds(pl.multiple_of(n * LANES, LANES), LANES)]
-            return a_cols[0], b_rows[mat][:, pl.ds(pl.multiple_of(i * p.nc + n * LANES, LANES), LANES)]
-
-        @pl.loop(0, parts * groups)
-        def _(j):
-            i, n = lax.div(j, groups), lax.rem(j, groups)
-            a_block, b_block = factors(i, n)
-            upd = grad[i, :, pl.ds(pl.multiple_of(n * LANES, LANES), LANES)] * a_block * b_block
-            u_sq[...] += jnp.sum(jnp.reshape(upd * upd, (p.mc // 8, 8, LANES)), axis=0)
+                return rows, a_cols[i, rows, :], b_rows[mat].at[:, :]
+            return rows, a_cols[0, rows, :], b_rows[mat].at[:, pl.ds(pl.multiple_of(i * p.nc, p.nc), p.nc)]
+
+        def add_up(j, acc):
+            i, n = lax.div(j, blocks), lax.rem(j, blocks)
+            rows, a_block, b_ref = factors(i, n)
+            for c in range(0, p.nc, LANES):
+                upd = grad[i, rows, c:c + LANES] * a_block * b_ref[:, c:c + LANES]
+                acc = acc + fold(upd * upd)
+            return acc
+
+        u_part = lax.fori_loop(0, parts * blocks, add_up, jnp.zeros((8, LANES), F32))
 
         def spot(v):
             return jnp.broadcast_to(jnp.sum(jnp.sum(v, axis=1, keepdims=True), axis=0, keepdims=True), (8, LANES))
 
         me = y * 4 + r
-        st_all[mat, me, 0] = spot(u_sq[...])
+        st_all[mat, me, 0] = spot(u_part)
         st_all[mat, me, 1] = spot(w_sq[mat])
         st_all[mat, me, 2] = jnp.broadcast_to(t_own, (8, LANES))
         for c in second_copies(mat):
@@ -372,17 +377,18 @@
             at = lax.rem(i, 3)
             get_w(mat, i).wait()
 
-            @pl.loop(0, groups)
+            @pl.loop(0, blocks)
             def _(n):
-                cols = pl.ds(pl.multiple_of(n * LANES, LANES), LANES)
-                a_block, b_block = factors(i, n)
-                fresh = w_buf[at, :, cols] - grad[i, :, cols] * a_block * b_block
-                if mat == ATTN:
-                    o_attn[:, cols] = fresh
-                elif mat == DOWN:
-                    grad[i, :, cols] = fresh
-                else:
-                    w_buf[at, :, cols] = fresh
+                rows, a_block, b_ref = factors(i, n)
+                for c in range(0, p.nc, LANES):
+                    cols = slice(c, c + LANES)
+                    fresh = w_buf[at, rows, cols] - grad[i, rows, cols] * a_block * b_ref[:, cols]
+                    if mat == ATTN:
+                        o_attn[rows, cols] = fresh
+                    elif mat == DOWN:
+                        grad[i, rows, cols] = fresh
+                    else:
+                        w_buf[at, rows, cols] = fresh
 
             if mat in (GATE, UP):
                 put_w(mat, i).start()
@@ -392,16 +398,32 @@
         if mat in (GATE, UP):
             put_w(mat, jnp.int32(parts - 1)).wait()
 
+    def take_x(src, at, k):
+        spread_done(k, False)
+        load(src, at, p.mc, buf_x, p.x_at(k), tile_x)
+        turn()
+
+    def again_x():
+        load(x_mlp, 0, p.mc, buf_x, 0, tile_x)
+        turn()
+
     def use_dy(k):
+        @pl.when(p.is_dy(k) & (mid | jnp.logical_not(p.is_attn(k))))
+        def _():
+            partner(k, 0).wait_recv()
+            partner(k, 1).wait_recv()
+
         @pl.when((k >= p.k_gate) & (k < p.k_xa))
         def _():
             i = k - p.k_gate
+            pl.when(i == 0)(lambda: take_x(x_mlp, 0, jnp.int32(0)))
             load(dy_gate, i, p.nc, buf_d, p.dy_at(k), tile_d)
             chunk(GATE, i)
             pl.when(i == p.ng - 1)(lambda: finish(GATE))
 
         @pl.when((k == p.k_attn) & mid)
         def _():
+            take_x(x_attn, 0, jnp.int32(p.k_xa))
             load(dy_attn, 0, p.nc, buf_d, p.dy_at(k), tile_d)
             chunk(ATTN, jnp.int32(0))
             finish(ATTN)
@@ -409,42 +431,21 @@
         @pl.when((k >= p.k_up) & (k < p.k_out))
         def _():
             i = k - p.k_up
-
-            @pl.when(i == 0)
-            def _():
-                load(x_mlp, 0, p.mc, buf_x, 0, tile_x)
-                turn()
-
+            pl.when(i == 0)(again_x)
             load(dy_up, i, p.nc, buf_d, p.dy_at(k), tile_d)
             chunk(UP, i)
             pl.when(i == p.ng - 1)(lambda: finish(UP))
 
         pl.when(k == p.k_out)(lambda: load(dy_out, 0, p.nc, buf_d, p.dy_at(k), tile_d))
 
-    def got_partner(k):
-        @pl.when(p.is_dy(k) & (mid | jnp.logical_not(p.is_attn(k))))
-        def _():
-            partner(k, 0).wait_recv()
-            partner(k, 1).wait_recv()
-
-    def use_x(k):
-        @pl.when(k == 0)
-        def _():
-            load(x_mlp, 0, p.mc, buf_x, 0, tile_x)
-            turn()
-
-        @pl.when((k == p.k_xa) & mid)
-        def _():
-            load(x_attn, 0, p.mc, buf_x, p.x_at(k), tile_x)
-            turn()
-
-        @pl.when(k >= p.k_h)
-        def _():
-            i = k - p.k_h
-            load(h_mlp, i, p.mc, buf_x, p.x_at(k), tile_x)
-            turn()
-            chunk(DOWN, i)
-            pl.when(i == p.nh - 1)(lambda: finish(DOWN))
+    def h_until(d):
+        late = jnp.where(mid, LATE, 1)
+        return jnp.clip(jnp.minimum(2 * (d - p.k_out - LATE), d - p.k_out - late), 0, p.nh)
+
+    def use_h(i):
+        take_x(h_mlp, i, p.k_h + i)
+        chunk(DOWN, i)
+        pl.when(i == p.nh - 1)(lambda: finish(DOWN))
 
     def to_end():
         pairs = ((o_attn, o_attn), (nr_attn, nr_attn), (nc_attn, nc_attn))
@@ -456,9 +457,9 @@
     for k in range(AHEAD):
         send_own(jnp.int32(k))
 
-    @pl.loop(0, p.count + 1)
+    @pl.loop(0, p.count + LATE)
     def _(d):
-        pl.when(d >= 1)(lambda: own_first_left(d - 1))
+        pl.when((d >= 1) & (d <= p.count))(lambda: own_first_left(d - 1))
 
         @pl.when(d < p.count)
         def _():
@@ -472,14 +473,19 @@
             for c in to_end():
                 c.start()
 
-        pl.when(d >= 1)(lambda: spread_done(d - 1))
-
-        @pl.when(d >= 2)
-        def _():
-            got_partner(d - 2)
-            use_dy(d - 2)
-
-        pl.when(d >= 1)(lambda: use_x(d - 1))
+        k = d - LATE
+
+        @pl.when((k >= 0) & p.is_dy(k) & (mid | jnp.logical_not(p.is_attn(k))))
+        def _():
+            spread_done(k, True)
+            partner(k, 1).start()
+
+        pl.when(d > LATE)(lambda: use_dy(d - LATE - 1))
+
+        @pl.loop(0, 2)
+        def _(j):
+            i = h_until(d - 1) + j
+            pl.when(i < h_until(d))(lambda: use_h(i))
 
     @pl.loop(0, p.count)
     def _(k):
@@ -590,7 +596,6 @@
             pltpu.VMEM((p.pieces, 1, p.nc), F32),
             pltpu.VMEM((p.nh, p.mc, LANES), F32),
             pltpu.VMEM((4, 8, LANES), F32),
-            pltpu.VMEM((8, LANES), F32),
         ]
         scratch += [pltpu.VMEM((1, p.cols[mat]), F32) for mat in MATS]
         scratch += [pltpu.VMEM((2, 1, p.rows[mat]), F32) for mat in MATS]

time: 1070 us -> 1050 us (0.981)
  Pallas kernels: 1070 us -> 1050 us
    pallas_call x1, Pallas kernels: 1040 us -> 1020 us  [per_device(): pl.pallas_call(functools.partial(gather_kernel, p), out_shape=o_shapes +...]
where the time goes in v3:
time: 1050 us
  Pallas kernels  1050 us (100%)
    pallas_call x1, Pallas kernels, per_device(): pl.pallas_call(functools.partial(gather_kernel, p), out_shape=o_shapes +...  1020 us
    pallas_call x1, Pallas kernels, per_device(): pl.pallas_call(functools.partial(store_kernel, p), out_shape=w_shapes + r...  29.1 us

profile of v3, /device:TPU:0, one launch (start us, length us, event | category | flops | bytes accessed | tf_op | source)
XLA Modules:
  0.0 1050.6 jit_solution(17822209707823809188)
XLA Ops:
  0.7 1020.9 %shard_map.283 = (f32[512,1024]{1,0:T(8,128)S(1)}, f32[512,8192]{1,0:T(8,128)}, f32[512,8192]{1,0:T(8,128)}, f32[8,512,1024]{2,1,0:T(8,128)S(1)}, f32[1,512]{1,0...) custom-call(bf16[1024,512]{1,0:T(8,128)(2,1)} %x_attn.1, ...), custom_call_target="tpu_custom_call" | custom-call | tf_op jit(solution)/shard_map/pallas_call | solution.py:612
  1021.6 29.1 %shard_map.284 = (f32[512,1024]{1,0:T(8,128)}, f32[512,8192]{1,0:T(8,128)}, f32[512,8192]{1,0:T(8,128)}, f32[4096,1024]{1,0:T(8,128)}, f32[1,512]{1,0:T(1,128)},...) custom-call(f32[512,1024]{1,0:T(8,128)S(1)} %get-tuple-element.36.o_, ...), custom_call_target="tpu_custom_call" | custom-call | tf_op jit(solution)/shard_map/pallas_call | solution.py:620

commit v4 on v3

--- a/solution.py
+++ b/solution.py
@@ -14,11 +14,19 @@
 BF16 = jnp.bfloat16
 ATTN, GATE, UP, DOWN = range(4)
 MATS = (ATTN, GATE, UP, DOWN)
-AHEAD = 3
+AHEAD_MID, AHEAD_END = 2, 6
 LATE = 3
 VMEM_LIMIT = 40 * 1024 * 1024
 STORE_LIMIT = 20 * 1024 * 1024
 KEPT = (0, 3) + tuple(range(4, 12))
+
+
+def look(k, table):
+    out = jnp.int32(0)
+    for i, v in enumerate(table):
+        if v:
+            out = jnp.where(k == i, v, out)
+    return out
 
 
 class Plan:
@@ -32,34 +40,55 @@
         self.nh = h_mlp.shape[1] // self.mc
         self.tq = self.tok // self.row
         self.th = self.tok // self.col
-        self.k_gate = 1
-        self.k_xa = 1 + self.ng
-        self.k_attn = self.k_xa + 1
-        self.k_up = self.k_attn + 1
-        self.k_out = self.k_up + self.ng
-        self.k_h = self.k_out + 1
-        self.count = self.k_h + self.nh
+        g = [('gate', i) for i in range(self.ng)]
+        u = [('up', i) for i in range(self.ng)]
+        h = [('h', i) for i in range(self.nh)]
+        one, two = max(1, self.ng // 4), max(2, 3 * self.ng // 4)
+        self.order = ([('x_mlp', 0)] + g[:one] + h[:1] + g[one:two] + h[1:2] + g[two:] + [('x_attn', 0), ('attn', 0)]
+                      + u + [('out', 0)] + h[2:])
+        self.count = len(self.order)
+        self.place = {v: k for k, v in enumerate(self.order)}
         self.n_dy = 2 * self.ng + 2
         self.n_x = self.nh + 2
         self.pieces = max(self.ng, self.nh)
         self.rows = {ATTN: self.mc, GATE: self.mc, UP: self.mc, DOWN: self.mc * self.nh}
         self.cols = {ATTN: self.nc, GATE: self.nc * self.ng, UP: self.nc * self.ng, DOWN: self.nc}
         self.parts = {ATTN: 1, GATE: self.ng, UP: self.ng, DOWN: self.nh}
+        base = {'gate': 0, 'up': self.ng, 'out': 2 * self.ng, 'attn': 2 * self.ng + 1, 'x_mlp': 0, 'x_attn': 1, 'h': 2}
+        self.dy_table = [1 if n in ('gate', 'up', 'out', 'attn') else 0 for n, _ in self.order]
+        self.at_table = [base[n] + i for n, i in self.order]
+        self.attn_table = [1 if n in ('x_attn', 'attn') else 0 for n, _ in self.order]
+        self.steps = {m: self.schedule(m) for m in (True, False)}
+        last = max(max(v.values()) for v in self.steps.values())
+        self.turns = max(last + 1, 3 * (self.count + LATE + 1))
+
+    def schedule(self, mid):
+        tasks = []
+        for name, mat in (('gate', GATE), ('attn', ATTN), ('up', UP), ('out', None), ('h', DOWN)):
+            if name == 'attn' and not mid:
+                continue
+            for i in range(sum(1 for n, _ in self.order if n == name)):
+                need = [(self.place[name, i], 1 if name == 'h' and not mid else LATE + (name != 'h'))]
+                if i == 0 and name in ('gate', 'attn'):
+                    need.append((self.place['x_mlp' if name == 'gate' else 'x_attn', 0], LATE))
+                tasks.append(((name, i), max(k + late for k, late in need)))
+            if mat is not None:
+                tasks += [(('finish', mat, stage), 0) for stage in range(4 if self.parts[mat] > 1 else 3)]
+        out, t = {}, 0
+        for task, first in tasks:
+            t = max(t, 3 * first)
+            out[task] = t
+            t += 1
+        return out
 
     def is_dy(self, k):
-        return ((k >= self.k_gate) & (k < self.k_xa)) | ((k >= self.k_attn) & (k <= self.k_out))
-
-    def is_x(self, k):
-        return (k == 0) | (k == self.k_xa) | (k >= self.k_h)
+        return look(k, self.dy_table) == 1
 
     def is_attn(self, k):
-        return (k == self.k_xa) | (k == self.k_attn)
-
-    def dy_at(self, k):
-        return jnp.where(k < self.k_xa, k - 1, k - 2)
-
-    def x_at(self, k):
-        return jnp.where(k == 0, 0, jnp.where(k == self.k_xa, 1, k - self.k_h + 2))
+        return look(k, self.attn_table) == 1
+
+    def at(self, k):
+        return look(k, self.at_table)
 
 
 def gather_kernel(plan, x_attn, dy_attn, x_mlp, dy_gate, dy_up, h_mlp, dy_out, w_attn, w_gate, w_up, w_down,
@@ -113,7 +142,7 @@
     my_h = pl.ds(pl.multiple_of(y * p.th, p.th), p.th)
 
     def slot(k, s, dy):
-        return buf_d.at[p.dy_at(k), s, my_q, :] if dy else buf_x.at[p.x_at(k), s, my_h, :]
+        return buf_d.at[p.at(k), s, my_q, :] if dy else buf_x.at[p.at(k), s, my_h, :]
 
     def pass_on(k, dy, src, to_z, to_slot, sem):
         return pltpu.make_async_remote_copy(
@@ -127,15 +156,15 @@
             device_id=to, device_id_type=MESH)
 
     def partner(k, which):
-        part = buf_d.at[p.dy_at(k), :, x_q if which else my_q, :]
+        part = buf_d.at[p.at(k), :, x_q if which else my_q, :]
         return pltpu.make_async_remote_copy(
-            src_ref=part, dst_ref=part, send_sem=c_send.at[p.dy_at(k), which], recv_sem=c_recv.at[p.dy_at(k), which],
+            src_ref=part, dst_ref=part, send_sem=c_send.at[p.at(k), which], recv_sem=c_recv.at[p.at(k), which],
             device_id=(z, y, flip_row(1)), device_id_type=MESH)
 
     def typed(k, go):
         used = mid | jnp.logical_not(p.is_attn(k))
         pl.when(p.is_dy(k) & used)(lambda: go(True))
-        pl.when(p.is_x(k) & used)(lambda: go(False))
+        pl.when(jnp.logical_not(p.is_dy(k)) & used)(lambda: go(False))
 
     def cut(ref, at, size):
         return ref.at[:, pl.ds(pl.multiple_of(at * size, size), size)]
@@ -159,22 +188,19 @@
         def go(ref, at, size, dy):
             own_to(k, dy, ref.at[my_q if dy else my_h, pl.ds(pl.multiple_of(at * size, size), size)])
 
-        pl.when(k == 0)(lambda: go(x_mlp, 0, p.mc, False))
-        pl.when((k >= p.k_gate) & (k < p.k_xa))(lambda: go(dy_gate, k - p.k_gate, p.nc, True))
-        pl.when(k == p.k_xa)(lambda: go(x_attn, 0, p.mc, False))
-        pl.when(k == p.k_attn)(lambda: go(dy_attn, 0, p.nc, True))
-        pl.when((k >= p.k_up) & (k < p.k_out))(lambda: go(dy_up, k - p.k_up, p.nc, True))
-        pl.when(k == p.k_out)(lambda: go(dy_out, 0, p.nc, True))
-        pl.when(k >= p.k_h)(lambda: go(h_mlp, k - p.k_h, p.mc, False))
+        for name, ref, dy in (('x_mlp', x_mlp, False), ('gate', dy_gate, True), ('x_attn', x_attn, False),
+                              ('attn', dy_attn, True), ('up', dy_up, True), ('out', dy_out, True), ('h', h_mlp, False)):
+            at = look(k, [i + 1 if n == name else 0 for n, i in p.order])
+            size = p.nc if dy else p.mc
+            pl.when(at > 0)(functools.partial(go, ref, at - 1, size, dy))
 
     def own_first_left(k):
         @pl.when(jnp.logical_not(mid & p.is_attn(k)))
         def _():
             pl.when(p.is_dy(k))(lambda: pass_on(k, True, slot(k, 0, True), z, 0, 0).wait_send())
-            pl.when(p.is_x(k))(lambda: pass_on(k, False, slot(k, 0, False), z, 0, 0).wait_send())
-
-    def arrive(k, turn_no):
-        e = jnp.where(mid, lax.rem(turn_no + 2, 3), turn_no)
+            pl.when(jnp.logical_not(p.is_dy(k)))(lambda: pass_on(k, False, slot(k, 0, False), z, 0, 0).wait_send())
+
+    def arrive(k, e, whole):
         s = jnp.where(low, e, 2 - e)
 
         def go(dy):
@@ -189,8 +215,8 @@
                 pass_on(k, dy, slot(k, s, dy), end_z, jnp.where(low, s + 1, s - 1), 2 + e).start()
 
             spread(k, s, dy).start()
-            if dy and turn_no == 2:
-                partner(k, 0).start()
+            if dy:
+                pl.when(whole)(lambda: partner(k, 0).start())
 
         typed(k, go)
 
@@ -298,9 +324,18 @@
             recv_sem=r2_recv.at[mat, f * 4 + v], device_id=(z, 1 - y if f else y, flip_row(v)), device_id_type=MESH)
             for f, v in peers]
 
-    def finish(mat):
-        beta_two, rho_step, clip_thr = hyper[0], hyper[1], hyper[2]
-        m_total, n_total = p.rows[mat] * p.row, p.cols[mat] * p.col
+    def scale_rows(mat):
+        return p.rows[mat] * p.row, p.cols[mat] * p.col
+
+    blocks = p.mc // step_r
+
+    def factors(mat, i, n):
+        rows = pl.ds(pl.multiple_of(n * step_r, step_r), step_r)
+        if mat == DOWN:
+            return rows, a_cols[i, rows, :], b_rows[mat].at[:, :]
+        return rows, a_cols[0, rows, :], b_rows[mat].at[:, pl.ds(pl.multiple_of(i * p.nc, p.nc), p.nc)]
+
+    def finish_first(mat):
         parts = p.parts[mat]
         for i in range(min(2, parts)):
             get_w(mat, jnp.int32(i)).start()
@@ -317,6 +352,11 @@
                 cs[mat][r, :, i * p.nc:(i + 1) * p.nc] = c_sum[i]
         for c in first_copies(mat):
             c.start()
+
+    def finish_second(mat):
+        beta_two = hyper[0]
+        m_total, n_total = scale_rows(mat)
+        parts = p.parts[mat]
         for c in first_copies(mat):
             c.wait_recv()
         r_new = beta_two * old[mat][0][...] + (1.0 - beta_two) * ((rs[mat][0] + rs[mat][1]) / n_total)
@@ -329,17 +369,10 @@
         b_rows[mat][...] = 1.0 / jnp.sqrt(c_new)
         for i in range(parts if mat == DOWN else 1):
             a_cols[i] = jnp.broadcast_to(a_row[:, i * p.mc:(i + 1) * p.mc], (LANES, p.mc)).T
-        blocks = p.mc // step_r
-
-        def factors(i, n):
-            rows = pl.ds(pl.multiple_of(n * step_r, step_r), step_r)
-            if mat == DOWN:
-                return rows, a_cols[i, rows, :], b_rows[mat].at[:, :]
-            return rows, a_cols[0, rows, :], b_rows[mat].at[:, pl.ds(pl.multiple_of(i * p.nc, p.nc), p.nc)]
 
         def add_up(j, acc):
             i, n = lax.div(j, blocks), lax.rem(j, blocks)
-            rows, a_block, b_ref = factors(i, n)
+            rows, a_block, b_ref = factors(mat, i, n)
             for c in range(0, p.nc, LANES):
                 upd = grad[i, rows, c:c + LANES] * a_block * b_ref[:, c:c + LANES]
                 acc = acc + fold(upd * upd)
@@ -356,6 +389,11 @@
         st_all[mat, me, 2] = jnp.broadcast_to(t_own, (8, LANES))
         for c in second_copies(mat):
             c.start()
+
+    def finish_third(mat):
+        rho_step, clip_thr = hyper[1], hyper[2]
+        m_total, n_total = scale_rows(mat)
+        me = y * 4 + r
         for c in second_copies(mat):
             c.wait_recv()
         t_all = st_all[mat, 0, 2]
@@ -372,14 +410,17 @@
         scale = scale * jnp.sqrt(t_all / st_all[mat, me, 2])
         b_rows[mat][...] = b_rows[mat][...] * scale[0:1, 0:1]
 
-        @pl.loop(0, parts)
+    def renew(mat, low_i, high_i):
+        parts = p.parts[mat]
+
+        @pl.loop(low_i, high_i)
         def _(i):
             at = lax.rem(i, 3)
             get_w(mat, i).wait()
 
             @pl.loop(0, blocks)
             def _(n):
-                rows, a_block, b_ref = factors(i, n)
+                rows, a_block, b_ref = factors(mat, i, n)
                 for c in range(0, p.nc, LANES):
                     cols = slice(c, c + LANES)
                     fresh = w_buf[at, rows, cols] - grad[i, rows, cols] * a_block * b_ref[:, cols]
@@ -395,57 +436,77 @@
                 pl.when(i >= 1)(lambda: put_w(mat, i - 1).wait())
             pl.when(i + 2 < parts)(lambda: get_w(mat, i + 2).start())
 
-        if mat in (GATE, UP):
+        if mat in (GATE, UP) and high_i == parts:
             put_w(mat, jnp.int32(parts - 1)).wait()
+
+    def finish(mat, stage):
+        parts = p.parts[mat]
+        half = parts // 2 if parts > 1 else parts
+        if stage == 0:
+            finish_first(mat)
+        elif stage == 1:
+            finish_second(mat)
+        elif stage == 2:
+            finish_third(mat)
+            renew(mat, 0, half)
+        else:
+            renew(mat, half, parts)
 
     def take_x(src, at, k):
         spread_done(k, False)
-        load(src, at, p.mc, buf_x, p.x_at(k), tile_x)
+        load(src, at, p.mc, buf_x, p.at(k), tile_x)
         turn()
 
     def again_x():
         load(x_mlp, 0, p.mc, buf_x, 0, tile_x)
         turn()
 
-    def use_dy(k):
-        @pl.when(p.is_dy(k) & (mid | jnp.logical_not(p.is_attn(k))))
-        def _():
-            partner(k, 0).wait_recv()
-            partner(k, 1).wait_recv()
-
-        @pl.when((k >= p.k_gate) & (k < p.k_xa))
-        def _():
-            i = k - p.k_gate
-            pl.when(i == 0)(lambda: take_x(x_mlp, 0, jnp.int32(0)))
-            load(dy_gate, i, p.nc, buf_d, p.dy_at(k), tile_d)
-            chunk(GATE, i)
-            pl.when(i == p.ng - 1)(lambda: finish(GATE))
-
-        @pl.when((k == p.k_attn) & mid)
-        def _():
-            take_x(x_attn, 0, jnp.int32(p.k_xa))
-            load(dy_attn, 0, p.nc, buf_d, p.dy_at(k), tile_d)
-            chunk(ATTN, jnp.int32(0))
-            finish(ATTN)
-
-        @pl.when((k >= p.k_up) & (k < p.k_out))
-        def _():
-            i = k - p.k_up
-            pl.when(i == 0)(again_x)
-            load(dy_up, i, p.nc, buf_d, p.dy_at(k), tile_d)
-            chunk(UP, i)
-            pl.when(i == p.ng - 1)(lambda: finish(UP))
-
-        pl.when(k == p.k_out)(lambda: load(dy_out, 0, p.nc, buf_d, p.dy_at(k), tile_d))
-
-    def h_until(d):
-        late = jnp.where(mid, LATE, 1)
-        return jnp.clip(jnp.minimum(2 * (d - p.k_out - LATE), d - p.k_out - late), 0, p.nh)
+    def got(name, i):
+        k = look(i, [p.place[name, j] for j in range(sum(1 for n, _ in p.order if n == name))])
+        partner(k, 0).wait_recv()
+        partner(k, 1).wait_recv()
+        return k
+
+    def use_gate(i):
+        pl.when(i == 0)(lambda: take_x(x_mlp, 0, jnp.int32(p.place['x_mlp', 0])))
+        k = got('gate', i)
+        load(dy_gate, i, p.nc, buf_d, p.at(k), tile_d)
+        chunk(GATE, i)
+
+    def use_attn(i):
+        take_x(x_attn, 0, jnp.int32(p.place['x_attn', 0]))
+        k = got('attn', i)
+        load(dy_attn, 0, p.nc, buf_d, p.at(k), tile_d)
+        chunk(ATTN, i)
+
+    def use_up(i):
+        pl.when(i == 0)(again_x)
+        k = got('up', i)
+        load(dy_up, i, p.nc, buf_d, p.at(k), tile_d)
+        chunk(UP, i)
+
+    def use_out(i):
+        k = got('out', i)
+        load(dy_out, 0, p.nc, buf_d, p.at(k), tile_d)
 
     def use_h(i):
-        take_x(h_mlp, i, p.k_h + i)
+        take_x(h_mlp, i, look(i, [p.place['h', j] for j in range(p.nh)]))
         chunk(DOWN, i)
-        pl.when(i == p.nh - 1)(lambda: finish(DOWN))
+
+    def work(t):
+        for name, use in (('gate', use_gate), ('attn', use_attn), ('up', use_up), ('out', use_out), ('h', use_h)):
+            at = jnp.int32(0)
+            for i in range(sum(1 for n, _ in p.order if n == name)):
+                when_mid = p.steps[True].get((name, i), -1)
+                when_end = p.steps[False].get((name, i), -1)
+                at = jnp.where(t == jnp.where(mid, when_mid, when_end), i + 1, at)
+            pl.when(at > 0)(functools.partial(use, at - 1))
+        for mat in MATS:
+            for stage in range(4):
+                when_mid = p.steps[True].get(('finish', mat, stage), -1)
+                when_end = p.steps[False].get(('finish', mat, stage), -1)
+                if when_mid >= 0:
+                    pl.when(t == jnp.where(mid, when_mid, when_end))(functools.partial(finish, mat, stage))
 
     def to_end():
         pairs = ((o_attn, o_attn), (nr_attn, nr_attn), (nc_attn, nc_attn))
@@ -454,38 +515,42 @@
             device_id=(end_z, y, r), device_id_type=MESH) for i, (a, b) in enumerate(pairs)]
 
     w_sq[...] = jnp.zeros_like(w_sq)
-    for k in range(AHEAD):
-        send_own(jnp.int32(k))
-
-    @pl.loop(0, p.count + LATE)
-    def _(d):
-        pl.when((d >= 1) & (d <= p.count))(lambda: own_first_left(d - 1))
-
-        @pl.when(d < p.count)
+    ahead = jnp.where(mid, AHEAD_MID, AHEAD_END)
+
+    @pl.loop(0, AHEAD_END)
+    def _(k):
+        pl.when(k < ahead)(lambda: send_own(k))
+
+    @pl.when(mid)
+    def _():
+        arrive(jnp.int32(0), jnp.int32(2), jnp.bool_(False))
+
+    @pl.loop(0, p.turns)
+    def _(t):
+        d, turn_no = lax.div(t, 3), lax.rem(t, 3)
+        pl.when((turn_no == 0) & (d >= 1) & (d <= p.count))(lambda: own_first_left(d - 1))
+        early = mid & (turn_no == 0)
+        k = jnp.where(early, d + 1, d)
+        e = jnp.where(mid, lax.rem(turn_no + 2, 3), turn_no)
+        pl.when(k < p.count)(lambda: arrive(k, e, turn_no == 2))
+
+        @pl.when(turn_no == 2)
         def _():
-            for i in range(3):
-                arrive(d, i)
-
-        pl.when(d + AHEAD < p.count)(lambda: send_own(d + AHEAD))
-
-        @pl.when((d == p.count - 1) & mid)
-        def _():
-            for c in to_end():
-                c.start()
-
-        k = d - LATE
-
-        @pl.when((k >= 0) & p.is_dy(k) & (mid | jnp.logical_not(p.is_attn(k))))
-        def _():
-            spread_done(k, True)
-            partner(k, 1).start()
-
-        pl.when(d > LATE)(lambda: use_dy(d - LATE - 1))
-
-        @pl.loop(0, 2)
-        def _(j):
-            i = h_until(d - 1) + j
-            pl.when(i < h_until(d))(lambda: use_h(i))
+            pl.when(d + ahead < p.count)(lambda: send_own(d + ahead))
+
+            @pl.when((d == p.count - 1) & mid)
+            def _():
+                for c in to_end():
+                    c.start()
+
+            k = d - LATE
+
+            @pl.when((k >= 0) & (k < p.count) & p.is_dy(k) & (mid | jnp.logical_not(p.is_attn(k))))
+            def _():
+                spread_done(k, True)
+                partner(k, 1).start()
+
+        work(t)
 
     @pl.loop(0, p.count)
     def _(k):

time: 1050 us -> 987 us (0.940)
  Pallas kernels: 1050 us -> 986 us
    pallas_call x1, Pallas kernels: 1020 us -> 957 us  [per_device(): pl.pallas_call(functools.partial(gather_kernel, p), out_shape=o_shapes +...]
where the time goes in v4:
time: 987 us
  Pallas kernels  986 us (100%)
    pallas_call x1, Pallas kernels, per_device(): pl.pallas_call(functools.partial(gather_kernel, p), out_shape=o_shapes +...  957 us
    pallas_call x1, Pallas kernels, per_device(): pl.pallas_call(functools.partial(store_kernel, p), out_shape=w_shapes + r...  29.1 us

profile of v4, /device:TPU:0, one launch (start us, length us, event | category | flops | bytes accessed | tf_op | source)
XLA Modules:
  0.0 986.5 jit_solution(17609533886610604584)
XLA Ops:
  0.7 956.8 %shard_map.283 = (f32[512,1024]{1,0:T(8,128)S(1)}, f32[512,8192]{1,0:T(8,128)}, f32[512,8192]{1,0:T(8,128)}, f32[8,512,1024]{2,1,0:T(8,128)S(1)}, f32[1,512]{1,0...) custom-call(bf16[1024,512]{1,0:T(8,128)(2,1)} %x_attn.1, ...), custom_call_target="tpu_custom_call" | custom-call | tf_op jit(solution)/shard_map/pallas_call | solution.py:677
  957.5 29.1 %shard_map.284 = (f32[512,1024]{1,0:T(8,128)}, f32[512,8192]{1,0:T(8,128)}, f32[512,8192]{1,0:T(8,128)}, f32[4096,1024]{1,0:T(8,128)}, f32[1,512]{1,0:T(1,128)},...) custom-call(f32[512,1024]{1,0:T(8,128)S(1)} %get-tuple-element.36.o_, ...), custom_call_target="tpu_custom_call" | custom-call | tf_op jit(solution)/shard_map/pallas_call | solution.py:685

commit v5 on v4

--- a/solution.py
+++ b/solution.py
@@ -14,11 +14,14 @@
 BF16 = jnp.bfloat16
 ATTN, GATE, UP, DOWN = range(4)
 MATS = (ATTN, GATE, UP, DOWN)
+FIRST = {'gate': ('x_mlp', 0), 'attn': ('x_attn', 0), 'up': ('x_mlp', 0), 'h': ('out', 0)}
 AHEAD_MID, AHEAD_END = 2, 6
 LATE = 3
-VMEM_LIMIT = 40 * 1024 * 1024
-STORE_LIMIT = 20 * 1024 * 1024
-KEPT = (0, 3) + tuple(range(4, 12))
+VMEM_LIMIT = 28 * 1024 * 1024
+STORE_LIMIT = 28 * 1024 * 1024
+UP_KEPT = True
+HBM_KEPT = (1,) if UP_KEPT else (1, 2)
+DEPTH, WIDE = 4, 4
 
 
 def look(k, table):
@@ -43,9 +46,7 @@
         g = [('gate', i) for i in range(self.ng)]
         u = [('up', i) for i in range(self.ng)]
         h = [('h', i) for i in range(self.nh)]
-        one, two = max(1, self.ng // 4), max(2, 3 * self.ng // 4)
-        self.order = ([('x_mlp', 0)] + g[:one] + h[:1] + g[one:two] + h[1:2] + g[two:] + [('x_attn', 0), ('attn', 0)]
-                      + u + [('out', 0)] + h[2:])
+        self.order = [('x_mlp', 0)] + g + [('x_attn', 0), ('attn', 0)] + u + [('out', 0)] + h
         self.count = len(self.order)
         self.place = {v: k for k, v in enumerate(self.order)}
         self.n_dy = 2 * self.ng + 2
@@ -64,19 +65,20 @@
 
     def schedule(self, mid):
         tasks = []
-        for name, mat in (('gate', GATE), ('attn', ATTN), ('up', UP), ('out', None), ('h', DOWN)):
+        for name, mat in (('gate', GATE), ('attn', ATTN), ('up', UP), ('h', DOWN)):
             if name == 'attn' and not mid:
                 continue
-            for i in range(sum(1 for n, _ in self.order if n == name)):
-                need = [(self.place[name, i], 1 if name == 'h' and not mid else LATE + (name != 'h'))]
-                if i == 0 and name in ('gate', 'attn'):
-                    need.append((self.place['x_mlp' if name == 'gate' else 'x_attn', 0], LATE))
-                tasks.append(((name, i), max(k + late for k, late in need)))
-            if mat is not None:
-                tasks += [(('finish', mat, stage), 0) for stage in range(4 if self.parts[mat] > 1 else 3)]
+            for i in range(self.parts[mat]):
+                k = self.place[name, i]
+                need = [3 * (k + LATE + 1)] if name != 'h' else [3 * (k + LATE) if mid else 3 * k + 5]
+                if i == 0:
+                    need.append(3 * (self.place[FIRST[name]] + LATE + (name == 'h')))
+                tasks.append(((name, i), max(need)))
+            stages = {ATTN: (1, 2), DOWN: (1, 2)}.get(mat, (1, 2, 3))
+            tasks += [(('finish', mat, stage), 0) for stage in stages]
         out, t = {}, 0
         for task, first in tasks:
-            t = max(t, 3 * first)
+            t = max(t, first)
             out[task] = t
             t += 1
         return out
@@ -94,8 +96,8 @@
 def gather_kernel(plan, x_attn, dy_attn, x_mlp, dy_gate, dy_up, h_mlp, dy_out, w_attn, w_gate, w_up, w_down,
                   r_attn, c_attn, r_gate, c_gate, r_up, c_up, r_down, c_down, hyper,
                   o_attn, o_gate, o_up, grad, nr_attn, nc_attn, nr_gate, nc_gate, nr_up, nc_up, nr_down, nc_down,
-                  buf_d, buf_x,
-                  lhs, tile_x, tile_d, w_buf, r_lanes, r_row, c_sum, a_cols, w_sq,
+                  al_down, be_down, buf_d, buf_x,
+                  lhs, tile_x, tile_d, w_buf, r_lanes, r_row, c_sum, a_cols, a_rows, w_sq,
                   b_attn, b_gate, b_up, b_down,
                   rs_attn, rs_gate, rs_up, rs_down, cs_attn, cs_gate, cs_up, cs_down, st_all,
                   z_send, z_recv, f_send, f_recv, c_send, c_recv, r1_send, r1_recv, r2_send, r2_recv,
@@ -215,8 +217,8 @@
                 pass_on(k, dy, slot(k, s, dy), end_z, jnp.where(low, s + 1, s - 1), 2 + e).start()
 
             spread(k, s, dy).start()
-            if dy:
-                pl.when(whole)(lambda: partner(k, 0).start())
+            if dy and whole:
+                pl.when(e == jnp.where(mid, 1, 2))(lambda: partner(k, 0).start())
 
         typed(k, go)
 
@@ -337,8 +339,9 @@
 
     def finish_first(mat):
         parts = p.parts[mat]
-        for i in range(min(2, parts)):
-            get_w(mat, jnp.int32(i)).start()
+        if mat != DOWN:
+            for i in range(min(2, parts)):
+                get_w(mat, jnp.int32(i)).start()
         if mat == DOWN:
             block = c_sum[0]
             for i in range(parts):
@@ -367,6 +370,8 @@
         t_own = jnp.sum(r_new, axis=1, keepdims=True)
         a_row = jnp.sqrt(t_own) / jnp.sqrt(r_new)
         b_rows[mat][...] = 1.0 / jnp.sqrt(c_new)
+        if mat == DOWN:
+            a_rows[...] = a_row
         for i in range(parts if mat == DOWN else 1):
             a_cols[i] = jnp.broadcast_to(a_row[:, i * p.mc:(i + 1) * p.mc], (LANES, p.mc)).T
 
@@ -426,29 +431,31 @@
                     fresh = w_buf[at, rows, cols] - grad[i, rows, cols] * a_block * b_ref[:, cols]
                     if mat == ATTN:
                         o_attn[rows, cols] = fresh
-                    elif mat == DOWN:
-                        grad[i, rows, cols] = fresh
+                    elif mat == UP and UP_KEPT:
+                        o_up[i, rows, cols] = fresh
                     else:
                         w_buf[at, rows, cols] = fresh
 
-            if mat in (GATE, UP):
+            if mat == GATE or (mat == UP and not UP_KEPT):
                 put_w(mat, i).start()
                 pl.when(i >= 1)(lambda: put_w(mat, i - 1).wait())
             pl.when(i + 2 < parts)(lambda: get_w(mat, i + 2).start())
 
-        if mat in (GATE, UP) and high_i == parts:
+        if (mat == GATE or (mat == UP and not UP_KEPT)) and high_i == parts:
             put_w(mat, jnp.int32(parts - 1)).wait()
 
     def finish(mat, stage):
         parts = p.parts[mat]
         half = parts // 2 if parts > 1 else parts
-        if stage == 0:
-            finish_first(mat)
-        elif stage == 1:
+        if stage == 1:
             finish_second(mat)
         elif stage == 2:
             finish_third(mat)
-            renew(mat, 0, half)
+            if mat == DOWN:
+                al_down[...] = a_rows[...]
+                be_down[...] = b_rows[mat][...]
+            else:
+                renew(mat, 0, half)
         else:
             renew(mat, half, parts)
 
@@ -472,29 +479,34 @@
         k = got('gate', i)
         load(dy_gate, i, p.nc, buf_d, p.at(k), tile_d)
         chunk(GATE, i)
+        pl.when(i == p.parts[GATE] - 1)(lambda: finish_first(GATE))
 
     def use_attn(i):
         take_x(x_attn, 0, jnp.int32(p.place['x_attn', 0]))
         k = got('attn', i)
         load(dy_attn, 0, p.nc, buf_d, p.at(k), tile_d)
         chunk(ATTN, i)
+        finish_first(ATTN)
 
     def use_up(i):
         pl.when(i == 0)(again_x)
         k = got('up', i)
         load(dy_up, i, p.nc, buf_d, p.at(k), tile_d)
         chunk(UP, i)
-
-    def use_out(i):
-        k = got('out', i)
+        pl.when(i == p.parts[UP] - 1)(lambda: finish_first(UP))
+
+    def use_out():
+        k = got('out', jnp.int32(0))
         load(dy_out, 0, p.nc, buf_d, p.at(k), tile_d)
 
     def use_h(i):
+        pl.when(i == 0)(use_out)
         take_x(h_mlp, i, look(i, [p.place['h', j] for j in range(p.nh)]))
         chunk(DOWN, i)
+        pl.when(i == p.parts[DOWN] - 1)(lambda: finish_first(DOWN))
 
     def work(t):
-        for name, use in (('gate', use_gate), ('attn', use_attn), ('up', use_up), ('out', use_out), ('h', use_h)):
+        for name, use in (('gate', use_gate), ('attn', use_attn), ('up', use_up), ('h', use_h)):
             at = jnp.int32(0)
             for i in range(sum(1 for n, _ in p.order if n == name)):
                 when_mid = p.steps[True].get((name, i), -1)
@@ -502,7 +514,7 @@
                 at = jnp.where(t == jnp.where(mid, when_mid, when_end), i + 1, at)
             pl.when(at > 0)(functools.partial(use, at - 1))
         for mat in MATS:
-            for stage in range(4):
+            for stage in (1, 2, 3):
                 when_mid = p.steps[True].get(('finish', mat, stage), -1)
                 when_end = p.steps[False].get(('finish', mat, stage), -1)
                 if when_mid >= 0:
@@ -523,16 +535,21 @@
 
     @pl.when(mid)
     def _():
-        arrive(jnp.int32(0), jnp.int32(2), jnp.bool_(False))
+        arrive(jnp.int32(0), jnp.int32(2), False)
+
+    @pl.when(jnp.logical_not(mid))
+    def _():
+        for k in range(AHEAD_MID):
+            arrive(jnp.int32(k), jnp.int32(0), False)
 
     @pl.loop(0, p.turns)
     def _(t):
         d, turn_no = lax.div(t, 3), lax.rem(t, 3)
         pl.when((turn_no == 0) & (d >= 1) & (d <= p.count))(lambda: own_first_left(d - 1))
-        early = mid & (turn_no == 0)
-        k = jnp.where(early, d + 1, d)
-        e = jnp.where(mid, lax.rem(turn_no + 2, 3), turn_no)
-        pl.when(k < p.count)(lambda: arrive(k, e, turn_no == 2))
+        early = jnp.where(mid, jnp.where(turn_no == 0, 1, 0), jnp.where(turn_no == 2, AHEAD_MID, 0))
+        e = lax.rem(turn_no + jnp.where(mid, 2, 1), 3)
+        k = d + early
+        pl.when(k < p.count)(lambda: arrive(k, e, True))
 
         @pl.when(turn_no == 2)
         def _():
@@ -592,33 +609,68 @@
             c.wait_recv()
 
 
-def store_kernel(plan, o_attn, o_gate, o_up, o_down, *refs):
+def store_kernel(plan, o_attn, o_gate, o_up, grad, *refs):
     p = plan
-    stats, (w_attn, w_gate, w_up, w_down), outs = refs[:8], refs[8:12], refs[12:20]
-    bounce, in_sem, out_sem, s_sem = refs[20:]
-    depth = bounce.shape[0]
+    stats, al_down, be_down, w_old, (w_attn, w_gate, w_up, w_down), outs = (
+        refs[:8], refs[8], refs[9], refs[10], refs[11:15], refs[15:23])
+    bounce, w_buf, a_col, in_sem, out_sem, s_sem, wi_sem, wo_sem = refs[23:]
+    depth, wide = bounce.shape[0], w_buf.shape[0]
 
     def cut(ref, i):
         return ref.at[:, i * p.nc:(i + 1) * p.nc]
 
-    through = [(cut(o_gate, i), cut(w_gate, i)) for i in range(p.ng)] + [(cut(o_up, i), cut(w_up, i)) for i in range(p.ng)]
+    def rows(ref, i):
+        return ref.at[i * p.mc:(i + 1) * p.mc, :]
+
+    through = [(cut(o_gate, i), cut(w_gate, i)) for i in range(p.ng)]
+    if not UP_KEPT:
+        through += [(cut(o_up, i), cut(w_up, i)) for i in range(p.ng)]
     loads = [pltpu.make_async_copy(a, bounce.at[i % depth], in_sem.at[i]) for i, (a, _) in enumerate(through)]
     puts = [pltpu.make_async_copy(bounce.at[i % depth], b, out_sem.at[i]) for i, (_, b) in enumerate(through)]
+    w_in = [pltpu.make_async_copy(rows(w_old, i), w_buf.at[i % wide], wi_sem.at[i]) for i in range(p.nh)]
+    w_out = [pltpu.make_async_copy(w_buf.at[i % wide], rows(w_down, i), wo_sem.at[i]) for i in range(p.nh)]
+    for i in range(wide // 2):
+        w_in[i].start()
     for c in loads[:depth]:
         c.start()
     copies = [pltpu.make_async_copy(a, b, s_sem.at[i]) for i, (a, b) in enumerate(zip(stats, outs))]
     copies.append(pltpu.make_async_copy(o_attn, w_attn, s_sem.at[8]))
-    for i in range(p.nh):
-        copies.append(pltpu.make_async_copy(o_down.at[i], w_down.at[i * p.mc:(i + 1) * p.mc, :], s_sem.at[9 + i]))
+    if UP_KEPT:
+        copies += [pltpu.make_async_copy(o_up.at[i], cut(w_up, i), s_sem.at[9 + i]) for i in range(p.ng)]
     for c in copies:
         c.start()
-    for i in range(len(through)):
-        loads[i].wait()
-        puts[i].start()
-        again = i - depth // 2
-        if 0 <= again and again + depth < len(through):
-            puts[again].wait()
-            loads[again + depth].start()
+    step_r = min(64, p.mc)
+    per = -(-len(through) // p.nh)
+    done = 0
+    for i in range(p.nh):
+        a_col[...] = jnp.broadcast_to(al_down[:, i * p.mc:(i + 1) * p.mc], (LANES, p.mc)).T
+        w_in[i].wait()
+
+        @pl.loop(0, p.mc // step_r)
+        def _(n):
+            at = pl.ds(pl.multiple_of(n * step_r, step_r), step_r)
+            a_block = a_col[at, :]
+            for c in range(0, p.nc, LANES):
+                cols = slice(c, c + LANES)
+                w_buf[i % wide, at, cols] = w_buf[i % wide, at, cols] - grad[i, at, cols] * a_block * be_down[:, cols]
+
+        w_out[i].start()
+        again = i + wide // 2
+        if again < p.nh:
+            if again >= wide:
+                w_out[again - wide].wait()
+            w_in[again].start()
+        for j in range(done, min(len(through), done + per)):
+            loads[j].wait()
+            puts[j].start()
+            again = j + depth // 2
+            if depth <= again < len(through):
+                puts[again - depth].wait()
+                loads[again].start()
+        done += per
+    for i in range(max(0, p.nh - wide), p.nh):
+        if i + wide >= p.nh:
+            w_out[i].wait()
     for i in range(max(0, len(through) - depth), len(through)):
         puts[i].wait()
     for c in copies:
@@ -642,11 +694,13 @@
         stats = [v.reshape(1, -1) for v in (r_attn, c_attn, r_gate, c_gate, r_up, c_up, r_down, c_down)]
         any_spec = pl.BlockSpec(memory_space=pl.ANY)
         vmem_spec = pl.BlockSpec(memory_space=pltpu.VMEM)
+        up_spec = vmem_spec if UP_KEPT else any_spec
         row_shapes = []
         for mat in MATS:
             row_shapes += [jax.ShapeDtypeStruct((1, p.rows[mat]), F32), jax.ShapeDtypeStruct((1, p.cols[mat]), F32)]
         w_shapes = [jax.ShapeDtypeStruct((p.rows[mat], p.cols[mat]), F32) for mat in MATS]
-        o_shapes = [pltpu.VMEM((p.mc, p.nc), F32), w_shapes[GATE], w_shapes[UP],
+        o_shapes = [pltpu.VMEM((p.mc, p.nc), F32), w_shapes[GATE],
+                    pltpu.VMEM((p.ng, p.mc, p.nc), F32) if UP_KEPT else w_shapes[UP],
                     pltpu.VMEM((p.pieces, p.mc, p.nc), F32)]
         bufs = [jax.ShapeDtypeStruct((p.n_dy, p.dp - 1, p.tok, p.nc), BF16),
                 jax.ShapeDtypeStruct((p.n_x, p.dp - 1, p.tok, p.mc), BF16)]
@@ -660,6 +714,7 @@
             pltpu.VMEM((p.pieces, 1, p.mc), F32),
             pltpu.VMEM((p.pieces, 1, p.nc), F32),
             pltpu.VMEM((p.nh, p.mc, LANES), F32),
+            pltpu.VMEM((1, p.rows[DOWN]), F32),
             pltpu.VMEM((4, 8, LANES), F32),
         ]
         scratch += [pltpu.VMEM((1, p.cols[mat]), F32) for mat in MATS]
@@ -676,20 +731,23 @@
         ]
         out = pl.pallas_call(
             functools.partial(gather_kernel, p),
-            out_shape=o_shapes + [pltpu.VMEM(v.shape, F32) for v in row_shapes] + bufs,
+            out_shape=o_shapes + [pltpu.VMEM(v.shape, F32) for v in row_shapes + row_shapes[-2:]] + bufs,
             in_specs=[any_spec] * 11 + [vmem_spec] * 8 + [pl.BlockSpec(memory_space=pltpu.SMEM)],
-            out_specs=[vmem_spec, any_spec, any_spec, vmem_spec] + [vmem_spec] * 8 + [any_spec] * 2,
+            out_specs=[vmem_spec, any_spec, up_spec, vmem_spec] + [vmem_spec] * 10 + [any_spec] * 2,
             scratch_shapes=scratch,
             compiler_params=pltpu.CompilerParams(collective_id=0, has_side_effects=True, vmem_limit_bytes=VMEM_LIMIT),
         )(x_attn, dy_attn, x_mlp, dy_gate, dy_up, h_mlp, dy_out, w_attn, w_gate, w_up, w_down, *stats, hyper_params)
         res = pl.pallas_call(
             functools.partial(store_kernel, p),
             out_shape=w_shapes + row_shapes,
-            in_specs=[vmem_spec, any_spec, any_spec, vmem_spec] + [vmem_spec] * 8,
+            in_specs=[vmem_spec, any_spec, up_spec, vmem_spec] + [vmem_spec] * 10 + [any_spec],
             out_specs=[any_spec] * 12,
-            scratch_shapes=[pltpu.VMEM((8, p.mc, p.nc), F32), dma((2 * p.ng,)), dma((2 * p.ng,)), dma((9 + p.nh,))],
+            scratch_shapes=[pltpu.VMEM((DEPTH, p.mc, p.nc), F32), pltpu.VMEM((WIDE, p.mc, p.nc), F32),
+                            pltpu.VMEM((p.mc, LANES), F32), dma((2 * p.ng,)), dma((2 * p.ng,)), dma((9 + p.ng,)),
+                            dma((p.nh,)), dma((p.nh,))],
             compiler_params=pltpu.CompilerParams(vmem_limit_bytes=STORE_LIMIT),
-        )(*[pltpu.with_memory_space_constraint(v, pltpu.VMEM) if i in KEPT else v for i, v in enumerate(out[:12])])
+        )(*[pltpu.with_memory_space_constraint(v, pltpu.VMEM) if i not in HBM_KEPT else v for i, v in enumerate(out[:14])],
+          w_down)
         result = []
         for mat in MATS:
             result += [res[mat], res[4 + 2 * mat].reshape(-1), res[5 + 2 * mat].reshape(-1)]

time: 987 us -> 988 us (level)
  no operation moved by 1% of the time
where the time goes in v5:
time: 988 us
  Pallas kernels  987 us (100%)
    pallas_call x1, Pallas kernels, per_device(): pl.pallas_call(functools.partial(gather_kernel, p), out_shape=o_shapes +...  958 us
    pallas_call x1, Pallas kernels, per_device(): pl.pallas_call(functools.partial(store_kernel, p), out_shape=w_shapes + r...  29.8 us

profile of v5, /device:TPU:0, one launch (start us, length us, event | category | flops | bytes accessed | tf_op | source)
XLA Modules:
  0.0 988.1 jit_solution(1900263167393783788)
XLA Ops:
  0.7 957.7 %shard_map.283 = (f32[512,1024]{1,0:T(8,128)S(1)}, f32[512,8192]{1,0:T(8,128)}, f32[8,512,1024]{2,1,0:T(8,128)S(1)}, f32[8,512,1024]{2,1,0:T(8,128)S(1)}, f32[1,...) custom-call(bf16[1024,512]{1,0:T(8,128)(2,1)} %x_attn.1, ...), custom_call_target="tpu_custom_call" | custom-call | tf_op jit(solution)/shard_map/pallas_call | solution.py:732
  958.3 29.8 %shard_map.284 = (f32[512,1024]{1,0:T(8,128)}, f32[512,8192]{1,0:T(8,128)}, f32[512,8192]{1,0:T(8,128)}, f32[4096,1024]{1,0:T(8,128)}, f32[1,512]{1,0:T(1,128)},...) custom-call(f32[512,1024]{1,0:T(8,128)S(1)} %get-tuple-element.38.o_, ...), custom_call_target="tpu_custom_call" | custom-call | tf_op jit(solution)/shard_map/pallas_call | solution.py:740

commit v6 on v5

--- a/solution.py
+++ b/solution.py
@@ -16,7 +16,7 @@
 MATS = (ATTN, GATE, UP, DOWN)
 FIRST = {'gate': ('x_mlp', 0), 'attn': ('x_attn', 0), 'up': ('x_mlp', 0), 'h': ('out', 0)}
 AHEAD_MID, AHEAD_END = 2, 6
-LATE = 3
+LATE_MID, LATE_END = 3, 2
 VMEM_LIMIT = 28 * 1024 * 1024
 STORE_LIMIT = 28 * 1024 * 1024
 UP_KEPT = True
@@ -46,7 +46,9 @@
         g = [('gate', i) for i in range(self.ng)]
         u = [('up', i) for i in range(self.ng)]
         h = [('h', i) for i in range(self.nh)]
-        self.order = [('x_mlp', 0)] + g + [('x_attn', 0), ('attn', 0)] + u + [('out', 0)] + h
+        one, two = max(1, self.ng // 4), max(2, 3 * self.ng // 4)
+        self.order = ([('x_mlp', 0)] + g[:one] + h[:1] + g[one:two] + h[1:2] + g[two:] + [('x_attn', 0), ('attn', 0)]
+                      + u + [('out', 0)] + h[2:])
         self.count = len(self.order)
         self.place = {v: k for k, v in enumerate(self.order)}
         self.n_dy = 2 * self.ng + 2
@@ -61,18 +63,19 @@
         self.attn_table = [1 if n in ('x_attn', 'attn') else 0 for n, _ in self.order]
         self.steps = {m: self.schedule(m) for m in (True, False)}
         last = max(max(v.values()) for v in self.steps.values())
-        self.turns = max(last + 1, 3 * (self.count + LATE + 1))
+        self.turns = max(last + 1, 3 * (self.count + LATE_MID + 1))
 
     def schedule(self, mid):
+        late = LATE_MID if mid else LATE_END
         tasks = []
         for name, mat in (('gate', GATE), ('attn', ATTN), ('up', UP), ('h', DOWN)):
             if name == 'attn' and not mid:
                 continue
             for i in range(self.parts[mat]):
                 k = self.place[name, i]
-                need = [3 * (k + LATE + 1)] if name != 'h' else [3 * (k + LATE) if mid else 3 * k + 5]
+                need = [3 * (k + late + 1)] if name != 'h' else [3 * (k + late) if mid else 3 * k + 5]
                 if i == 0:
-                    need.append(3 * (self.place[FIRST[name]] + LATE + (name == 'h')))
+                    need.append(3 * (self.place[FIRST[name]] + late + (name == 'h')))
                 tasks.append(((name, i), max(need)))
             stages = {ATTN: (1, 2), DOWN: (1, 2)}.get(mat, (1, 2, 3))
             tasks += [(('finish', mat, stage), 0) for stage in stages]
@@ -560,7 +563,7 @@
                 for c in to_end():
                     c.start()
 
-            k = d - LATE
+            k = d - jnp.where(mid, LATE_MID, LATE_END)
 
             @pl.when((k >= 0) & (k < p.count) & p.is_dy(k) & (mid | jnp.logical_not(p.is_attn(k))))
             def _():

time: 988 us -> 967 us (0.979)
  Pallas kernels: 987 us -> 966 us
    pallas_call x1, Pallas kernels: 958 us -> 936 us  [per_device(): pl.pallas_call(functools.partial(gather_kernel, p), out_shape=o_shapes +...]
where the time goes in v6:
time: 967 us
  Pallas kernels  966 us (100%)
    pallas_call x1, Pallas kernels, per_device(): pl.pallas_call(functools.partial(gather_kernel, p), out_shape=o_shapes +...  936 us
    pallas_call x1, Pallas kernels, per_device(): pl.pallas_call(functools.partial(store_kernel, p), out_shape=w_shapes + r...  29.8 us

profile of v6, /device:TPU:0, one launch (start us, length us, event | category | flops | bytes accessed | tf_op | source)
XLA Modules:
  0.0 966.5 jit_solution(1285160816443179829)
XLA Ops:
  0.7 936.1 %shard_map.283 = (f32[512,1024]{1,0:T(8,128)S(1)}, f32[512,8192]{1,0:T(8,128)}, f32[8,512,1024]{2,1,0:T(8,128)S(1)}, f32[8,512,1024]{2,1,0:T(8,128)S(1)}, f32[1,...) custom-call(bf16[1024,512]{1,0:T(8,128)(2,1)} %x_attn.1, ...), custom_call_target="tpu_custom_call" | custom-call | tf_op jit(solution)/shard_map/pallas_call | solution.py:735
  936.8 29.8 %shard_map.284 = (f32[512,1024]{1,0:T(8,128)}, f32[512,8192]{1,0:T(8,128)}, f32[512,8192]{1,0:T(8,128)}, f32[4096,1024]{1,0:T(8,128)}, f32[1,512]{1,0:T(1,128)},...) custom-call(f32[512,1024]{1,0:T(8,128)S(1)} %get-tuple-element.38.o_, ...), custom_call_target="tpu_custom_call" | custom-call | tf_op jit(solution)/shard_map/pallas_call | solution.py:743

commit v7 on v6

--- a/solution.py
+++ b/solution.py
@@ -17,8 +17,8 @@
 FIRST = {'gate': ('x_mlp', 0), 'attn': ('x_attn', 0), 'up': ('x_mlp', 0), 'h': ('out', 0)}
 AHEAD_MID, AHEAD_END = 2, 6
 LATE_MID, LATE_END = 3, 2
-VMEM_LIMIT = 28 * 1024 * 1024
-STORE_LIMIT = 28 * 1024 * 1024
+VMEM_LIMIT = 29 * 1024 * 1024
+STORE_LIMIT = 29 * 1024 * 1024
 UP_KEPT = True
 HBM_KEPT = (1,) if UP_KEPT else (1, 2)
 DEPTH, WIDE = 4, 4
@@ -51,6 +51,7 @@
                       + u + [('out', 0)] + h[2:])
         self.count = len(self.order)
         self.place = {v: k for k, v in enumerate(self.order)}
+        self.first_rows = self.mc // 2
         self.n_dy = 2 * self.ng + 2
         self.n_x = self.nh + 2
         self.pieces = max(self.ng, self.nh)
@@ -78,7 +79,8 @@
                     need.append(3 * (self.place[FIRST[name]] + late + (name == 'h')))
                 tasks.append(((name, i), max(need)))
             stages = {ATTN: (1, 2), DOWN: (1, 2)}.get(mat, (1, 2, 3))
-            tasks += [(('finish', mat, stage), 0) for stage in stages]
+            if mid or mat != DOWN:
+                tasks += [(('finish', mat, stage), 0) for stage in stages]
         out, t = {}, 0
         for task, first in tasks:
             t = max(t, first)
@@ -99,7 +101,7 @@
 def gather_kernel(plan, x_attn, dy_attn, x_mlp, dy_gate, dy_up, h_mlp, dy_out, w_attn, w_gate, w_up, w_down,
                   r_attn, c_attn, r_gate, c_gate, r_up, c_up, r_down, c_down, hyper,
                   o_attn, o_gate, o_up, grad, nr_attn, nc_attn, nr_gate, nc_gate, nr_up, nc_up, nr_down, nc_down,
-                  al_down, be_down, buf_d, buf_x,
+                  al_down, be_down, o_rest, buf_d, buf_x,
                   lhs, tile_x, tile_d, w_buf, r_lanes, r_row, c_sum, a_cols, a_rows, w_sq,
                   b_attn, b_gate, b_up, b_down,
                   rs_attn, rs_gate, rs_up, rs_down, cs_attn, cs_gate, cs_up, cs_down, st_all,
@@ -257,7 +259,7 @@
             out = out + v[:, i * LANES:(i + 1) * LANES]
         return out
 
-    def product(at):
+    def product(at, count):
         r_lanes[...] = jnp.zeros_like(r_lanes)
 
         @pl.loop(0, p.nc // step_n)
@@ -276,7 +278,9 @@
                 r_lanes[rows, :] += lane_sum(sq)
                 return acc + jnp.sum(sq, axis=0, keepdims=True)
 
-            c_sum[at, :, cols] = lax.fori_loop(0, p.mc // step_r, body, jnp.zeros((1, step_n), F32))
+            @pl.when(count)
+            def _():
+                c_sum[at, :, cols] = lax.fori_loop(0, p.mc // step_r, body, jnp.zeros((1, step_n), F32))
 
     def fold(v):
         v = jnp.reshape(v, (v.shape[0] // 8, 8, LANES))
@@ -296,21 +300,25 @@
         return pltpu.make_async_copy(w_buf.at[lax.rem(i, 3)], dst, wo_sem.at[lax.rem(i, 3)])
 
     def chunk(mat, i):
-        get_w(mat, i).start()
-        product(i)
-        row = to_row(r_lanes[...])
-        if mat == DOWN:
-            r_row[i] = row
-        else:
-            r_row[0] = jnp.where(i == 0, row, r_row[0] + row)
-        get_w(mat, i).wait()
-
-        def body(n, acc):
-            rows = pl.ds(pl.multiple_of(n * step_r, step_r), step_r)
-            block = lane_sum(w_buf[lax.rem(i, 3), rows, :] * w_buf[lax.rem(i, 3), rows, :])
-            return acc + fold(block)
-
-        w_sq[mat] += lax.fori_loop(0, p.mc // step_r, body, jnp.zeros((8, LANES), F32))
+        count = mid if mat == DOWN else jnp.bool_(True)
+        pl.when(count)(lambda: get_w(mat, i).start())
+        product(i, count)
+
+        @pl.when(count)
+        def _():
+            row = to_row(r_lanes[...])
+            if mat == DOWN:
+                r_row[i] = row
+            else:
+                r_row[0] = jnp.where(i == 0, row, r_row[0] + row)
+            get_w(mat, i).wait()
+
+            def body(n, acc):
+                rows = pl.ds(pl.multiple_of(n * step_r, step_r), step_r)
+                block = lane_sum(w_buf[lax.rem(i, 3), rows, :] * w_buf[lax.rem(i, 3), rows, :])
+                return acc + fold(block)
+
+            w_sq[mat] += lax.fori_loop(0, p.mc // step_r, body, jnp.zeros((8, LANES), F32))
 
     def first_copies(mat):
         copies = [pltpu.make_async_remote_copy(
@@ -439,6 +447,9 @@
                     else:
                         w_buf[at, rows, cols] = fresh
 
+            if mat == ATTN:
+                put_rest().start()
+                put_rest().wait()
             if mat == GATE or (mat == UP and not UP_KEPT):
                 put_w(mat, i).start()
                 pl.when(i >= 1)(lambda: put_w(mat, i - 1).wait())
@@ -446,6 +457,9 @@
 
         if (mat == GATE or (mat == UP and not UP_KEPT)) and high_i == parts:
             put_w(mat, jnp.int32(parts - 1)).wait()
+
+    def put_rest():
+        return pltpu.make_async_copy(o_attn.at[pl.ds(p.first_rows, p.mc - p.first_rows), :], o_rest, wo_sem.at[0])
 
     def finish(mat, stage):
         parts = p.parts[mat]
@@ -457,6 +471,8 @@
             if mat == DOWN:
                 al_down[...] = a_rows[...]
                 be_down[...] = b_rows[mat][...]
+                for c in to_end_down():
+                    c.start()
             else:
                 renew(mat, 0, half)
         else:
@@ -506,7 +522,7 @@
         pl.when(i == 0)(use_out)
         take_x(h_mlp, i, look(i, [p.place['h', j] for j in range(p.nh)]))
         chunk(DOWN, i)
-        pl.when(i == p.parts[DOWN] - 1)(lambda: finish_first(DOWN))
+        pl.when((i == p.parts[DOWN] - 1) & mid)(lambda: finish_first(DOWN))
 
     def work(t):
         for name, use in (('gate', use_gate), ('attn', use_attn), ('up', use_up), ('h', use_h)):
@@ -523,11 +539,16 @@
                 if when_mid >= 0:
                     pl.when(t == jnp.where(mid, when_mid, when_end))(functools.partial(finish, mat, stage))
 
+    def sent_to_end(refs, first):
+        return [pltpu.make_async_remote_copy(
+            src_ref=ref, dst_ref=ref, send_sem=e_send.at[first + i], recv_sem=e_recv.at[first + i],
+            device_id=(end_z, y, r), device_id_type=MESH) for i, ref in enumerate(refs)]
+
     def to_end():
-        pairs = ((o_attn, o_attn), (nr_attn, nr_attn), (nc_attn, nc_attn))
-        return [pltpu.make_async_remote_copy(
-            src_ref=a, dst_ref=b, send_sem=e_send.at[i], recv_sem=e_recv.at[i],
-            device_id=(end_z, y, r), device_id_type=MESH) for i, (a, b) in enumerate(pairs)]
+        return sent_to_end((nr_attn, nc_attn, o_attn.at[pl.ds(0, p.first_rows), :]), 0)
+
+    def to_end_down():
+        return sent_to_end((nr_down, nc_down, al_down, be_down), 3)
 
     w_sq[...] = jnp.zeros_like(w_sq)
     ahead = jnp.where(mid, AHEAD_MID, AHEAD_END)
@@ -548,7 +569,7 @@
     @pl.loop(0, p.turns)
     def _(t):
         d, turn_no = lax.div(t, 3), lax.rem(t, 3)
-        pl.when((turn_no == 0) & (d >= 1) & (d <= p.count))(lambda: own_first_left(d - 1))
+        pl.when((turn_no == 0) & (d >= 1) & (d < p.count))(lambda: own_first_left(d - 1))
         early = jnp.where(mid, jnp.where(turn_no == 0, 1, 0), jnp.where(turn_no == 2, AHEAD_MID, 0))
         e = lax.rem(turn_no + jnp.where(mid, 2, 1), 3)
         k = d + early
@@ -595,20 +616,22 @@
 
         typed(k, go)
 
-    for mat in (GATE, UP, DOWN):
+    own_first_left(jnp.int32(p.count - 1))
+    for mat in (GATE, UP):
         for c in first_copies(mat) + second_copies(mat):
             c.wait_send()
 
     @pl.when(mid)
     def _():
-        for c in first_copies(ATTN) + second_copies(ATTN):
-            c.wait_send()
-        for c in to_end():
+        for mat in (ATTN, DOWN):
+            for c in first_copies(mat) + second_copies(mat):
+                c.wait_send()
+        for c in to_end() + to_end_down():
             c.wait_send()
 
     @pl.when(jnp.logical_not(mid))
     def _():
-        for c in to_end():
+        for c in to_end() + to_end_down():
             c.wait_recv()
 
 
@@ -707,6 +730,7 @@
                     pltpu.VMEM((p.pieces, p.mc, p.nc), F32)]
         bufs = [jax.ShapeDtypeStruct((p.n_dy, p.dp - 1, p.tok, p.nc), BF16),
                 jax.ShapeDtypeStruct((p.n_x, p.dp - 1, p.tok, p.mc), BF16)]
+        rest = jax.ShapeDtypeStruct((p.mc - p.first_rows, p.nc), F32)
         dma = pltpu.SemaphoreType.DMA
         scratch = [
             pltpu.VMEM((p.dp, p.mc, p.tok), BF16),
@@ -729,14 +753,14 @@
             dma((p.count, p.dp - 1)), dma((p.count, p.dp - 1)),
             dma((p.n_dy, 2)), dma((p.n_dy, 2)),
             dma((4, 4)), dma((4, 4)), dma((4, 8)), dma((4, 8)),
-            dma((3,)), dma((3,)),
+            dma((7,)), dma((7,)),
             dma((p.dp,)), dma((3,)), dma((3,)),
         ]
         out = pl.pallas_call(
             functools.partial(gather_kernel, p),
-            out_shape=o_shapes + [pltpu.VMEM(v.shape, F32) for v in row_shapes + row_shapes[-2:]] + bufs,
+            out_shape=o_shapes + [pltpu.VMEM(v.shape, F32) for v in row_shapes + row_shapes[-2:]] + [rest] + bufs,
             in_specs=[any_spec] * 11 + [vmem_spec] * 8 + [pl.BlockSpec(memory_space=pltpu.SMEM)],
-            out_specs=[vmem_spec, any_spec, up_spec, vmem_spec] + [vmem_spec] * 10 + [any_spec] * 2,
+            out_specs=[vmem_spec, any_spec, up_spec, vmem_spec] + [vmem_spec] * 10 + [any_spec] * 3,
             scratch_shapes=scratch,
             compiler_params=pltpu.CompilerParams(collective_id=0, has_side_effects=True, vmem_limit_bytes=VMEM_LIMIT),
         )(x_attn, dy_attn, x_mlp, dy_gate, dy_up, h_mlp, dy_out, w_attn, w_gate, w_up, w_down, *stats, hyper_params)
@@ -749,8 +773,13 @@
                             pltpu.VMEM((p.mc, LANES), F32), dma((2 * p.ng,)), dma((2 * p.ng,)), dma((9 + p.ng,)),
                             dma((p.nh,)), dma((p.nh,))],
             compiler_params=pltpu.CompilerParams(vmem_limit_bytes=STORE_LIMIT),
+            cost_estimate=pl.CostEstimate(flops=60_000_000_000, bytes_accessed=90_000_000, transcendentals=0),
         )(*[pltpu.with_memory_space_constraint(v, pltpu.VMEM) if i not in HBM_KEPT else v for i, v in enumerate(out[:14])],
           w_down)
+        z = lax.axis_index('dp')
+        got = lax.ppermute(out[14], 'dp', [(1, 0), (2, 3)])
+        rows = jnp.where((z == 1) | (z == 2), out[14], got)
+        res = [lax.dynamic_update_slice(res[0], rows, (p.first_rows, 0))] + list(res[1:])
         result = []
         for mat in MATS:
             result += [res[mat], res[4 + 2 * mat].reshape(-1), res[5 + 2 * mat].reshape(-1)]

time: 967 us -> 954 us (0.987)
  Pallas kernels: 966 us -> 948 us
    pallas_call x1, Pallas kernels: 936 us -> 918 us  [per_device(): pl.pallas_call(functools.partial(gather_kernel, p), out_shape=o_shapes +...]
  transfers between devices with their start and end apart: 0 -> 1, of which waited for: 0 -> 0; matrix products, arithmetic and copies ran while one was open for 0% -> 0% of each run, Pallas kernels for 0% -> 3%
where the time goes in v7:
time: 954 us; the launch traced here: 952 us
  Pallas kernels  948 us (99%)
    pallas_call x1, Pallas kernels, per_device(): pl.pallas_call(functools.partial(gather_kernel, p), out_shape=o_shapes +...  918 us
    pallas_call x1, Pallas kernels, per_device(): pl.pallas_call(functools.partial(store_kernel, p), out_shape=w_shapes + r...  29.8 us
  transfers between devices with their start and end apart: 1, of which 0 were waited for; matrix products, arithmetic and copies ran while one was open for 0% of the time, Pallas kernels for 3%

profile of v7, /device:TPU:0, one launch (start us, length us, event | category | flops | bytes accessed | tf_op | source)
XLA Modules:
  0.0 952.4 jit_solution(3540612237925623577)
XLA Ops:
  0.7 918.3 %shard_map.283 = (f32[512,1024]{1,0:T(8,128)S(1)}, f32[512,8192]{1,0:T(8,128)}, f32[8,512,1024]{2,1,0:T(8,128)S(1)}, f32[8,512,1024]{2,1,0:T(8,128)S(1)}, f32[1,...) custom-call(bf16[1024,512]{1,0:T(8,128)(2,1)} %x_attn.1, ...), custom_call_target="tpu_custom_call" | custom-call | tf_op jit(solution)/shard_map/pallas_call | solution.py:759
  918.9 1.3 collective-permute-start
  920.2 29.8 %shard_map.284 = (f32[512,1024]{1,0:T(8,128)}, f32[512,8192]{1,0:T(8,128)}, f32[512,8192]{1,0:T(8,128)}, f32[4096,1024]{1,0:T(8,128)}, f32[1,512]{1,0:T(1,128)},...) custom-call(f32[512,1024]{1,0:T(8,128)S(1)} %get-tuple-element.39.o_, ...), custom_call_target="tpu_custom_call" | custom-call | flops 60000002048 | bytes 90000000 | tf_op jit(solution)/shard_map/pallas_call | solution.py:767
  950.0 0.0 collective-permute-done
  950.0 2.4 select_dynamic-update-slice_fusion
Async XLA Ops:
  918.9 31.1 %collective-permute-start = (f32[256,1024]{1,0:T(8,128)}, f32[256,1024]{1,0:T(8,128)}, u32[]{:S(2)}, u32[]{:S(2)}) collective-permute-start(f32[256,1024]{1,0:T(8,128)} %get-tuple-element.54), channel_id=1, source_target_pairs={{8,0},{16,24},{9,1},{17,25},{10,2},{18,26},{11,3},{19,27},{12,4},{... | collective-permute-start | bytes 3145736 | tf_op jit(solution)/shard_map/ppermute | solution.py:780

commit v8 on v7

--- a/solution.py
+++ b/solution.py
@@ -16,6 +16,7 @@
 MATS = (ATTN, GATE, UP, DOWN)
 FIRST = {'gate': ('x_mlp', 0), 'attn': ('x_attn', 0), 'up': ('x_mlp', 0), 'h': ('out', 0)}
 AHEAD_MID, AHEAD_END = 2, 6
+PARTS = 4
 LATE_MID, LATE_END = 3, 2
 VMEM_LIMIT = 29 * 1024 * 1024
 STORE_LIMIT = 29 * 1024 * 1024
@@ -51,7 +52,7 @@
                       + u + [('out', 0)] + h[2:])
         self.count = len(self.order)
         self.place = {v: k for k, v in enumerate(self.order)}
-        self.first_rows = self.mc // 2
+        self.first_rows = self.mc * 5 // 16
         self.n_dy = 2 * self.ng + 2
         self.n_x = self.nh + 2
         self.pieces = max(self.ng, self.nh)
@@ -148,19 +149,32 @@
     x_q = pl.ds(pl.multiple_of(flip_row(2) * p.tq, p.tq), p.tq)
     my_h = pl.ds(pl.multiple_of(y * p.th, p.th), p.th)
 
-    def slot(k, s, dy):
-        return buf_d.at[p.at(k), s, my_q, :] if dy else buf_x.at[p.at(k), s, my_h, :]
-
-    def pass_on(k, dy, src, to_z, to_slot, sem):
+    def rows_of(dy, part):
+        if dy:
+            return my_q
+        if part is None:
+            return my_h
+        size = p.th // PARTS
+        return pl.ds(pl.multiple_of(y * p.th + part * size, size), size)
+
+    def line_of(k, part):
+        return k if part is None else k + part
+
+    def slot(k, s, dy, part):
+        return (buf_d if dy else buf_x).at[p.at(k), s, rows_of(dy, part), :]
+
+    def pass_on(k, dy, part, src, to_z, to_slot, sem):
+        line = line_of(k, part)
         return pltpu.make_async_remote_copy(
-            src_ref=src, dst_ref=slot(k, to_slot, dy), send_sem=z_send.at[k, sem], recv_sem=z_recv.at[k, to_slot],
-            device_id=(to_z, y, r), device_id_type=MESH)
-
-    def spread(k, s, dy):
+            src_ref=src, dst_ref=slot(k, to_slot, dy, part), send_sem=z_send.at[line, sem],
+            recv_sem=z_recv.at[line, to_slot], device_id=(to_z, y, r), device_id_type=MESH)
+
+    def spread(k, s, dy, part):
         to = (z, y, flip_row(2)) if dy else (z, 1 - y, r)
+        line = line_of(k, part)
         return pltpu.make_async_remote_copy(
-            src_ref=slot(k, s, dy), dst_ref=slot(k, s, dy), send_sem=f_send.at[k, s], recv_sem=f_recv.at[k, s],
-            device_id=to, device_id_type=MESH)
+            src_ref=slot(k, s, dy, part), dst_ref=slot(k, s, dy, part), send_sem=f_send.at[line, s],
+            recv_sem=f_recv.at[line, s], device_id=to, device_id_type=MESH)
 
     def partner(k, which):
         part = buf_d.at[p.at(k), :, x_q if which else my_q, :]
@@ -168,10 +182,17 @@
             src_ref=part, dst_ref=part, send_sem=c_send.at[p.at(k), which], recv_sem=c_recv.at[p.at(k), which],
             device_id=(z, y, flip_row(1)), device_id_type=MESH)
 
+    def in_parts(k, go):
+        pl.when(k != p.count - 1)(lambda: go(None))
+
+        @pl.when(k == p.count - 1)
+        def _():
+            pl.loop(0, PARTS)(go)
+
     def typed(k, go):
         used = mid | jnp.logical_not(p.is_attn(k))
-        pl.when(p.is_dy(k) & used)(lambda: go(True))
-        pl.when(jnp.logical_not(p.is_dy(k)) & used)(lambda: go(False))
+        pl.when(p.is_dy(k) & used)(lambda: go(True, None))
+        pl.when(jnp.logical_not(p.is_dy(k)) & used)(lambda: in_parts(k, lambda part: go(False, part)))
 
     def cut(ref, at, size):
         return ref.at[:, pl.ds(pl.multiple_of(at * size, size), size)]
@@ -179,21 +200,27 @@
     def down_rows(ref, i):
         return ref.at[pl.ds(pl.multiple_of(i * p.mc, p.mc), p.mc), :]
 
-    def own_to(k, dy, src):
+    def own_to(k, dy, part, src):
         @pl.when(jnp.logical_not(mid))
         def _():
-            pass_on(k, dy, src, jnp.where(low, 1, 2), jnp.where(low, 2, 0), 0).start()
+            pass_on(k, dy, part, src, jnp.where(low, 1, 2), jnp.where(low, 2, 0), 0).start()
 
         @pl.when(mid)
         def _():
             @pl.when(jnp.logical_not(p.is_attn(k)))
             def _():
-                pass_on(k, dy, src, end_z, jnp.where(low, 0, 2), 0).start()
-            pass_on(k, dy, src, mate_z, jnp.where(low, 2, 0), 1).start()
+                pass_on(k, dy, part, src, end_z, jnp.where(low, 0, 2), 0).start()
+            pass_on(k, dy, part, src, mate_z, jnp.where(low, 2, 0), 1).start()
 
     def send_own(k):
         def go(ref, at, size, dy):
-            own_to(k, dy, ref.at[my_q if dy else my_h, pl.ds(pl.multiple_of(at * size, size), size)])
+            def send(part):
+                own_to(k, dy, part, ref.at[rows_of(dy, part), pl.ds(pl.multiple_of(at * size, size), size)])
+
+            if ref is h_mlp:
+                in_parts(k, send)
+            else:
+                send(None)
 
         for name, ref, dy in (('x_mlp', x_mlp, False), ('gate', dy_gate, True), ('x_attn', x_attn, False),
                               ('attn', dy_attn, True), ('up', dy_up, True), ('out', dy_out, True), ('h', h_mlp, False)):
@@ -204,24 +231,28 @@
     def own_first_left(k):
         @pl.when(jnp.logical_not(mid & p.is_attn(k)))
         def _():
-            pl.when(p.is_dy(k))(lambda: pass_on(k, True, slot(k, 0, True), z, 0, 0).wait_send())
-            pl.when(jnp.logical_not(p.is_dy(k)))(lambda: pass_on(k, False, slot(k, 0, False), z, 0, 0).wait_send())
+            def go(dy, part):
+                pass_on(k, dy, part, slot(k, 0, dy, part), z, 0, 0).wait_send()
+
+            pl.when(p.is_dy(k))(lambda: go(True, None))
+            pl.when(jnp.logical_not(p.is_dy(k)))(lambda: in_parts(k, lambda part: go(False, part)))
 
     def arrive(k, e, whole):
         s = jnp.where(low, e, 2 - e)
 
-        def go(dy):
-            pass_on(k, dy, slot(k, s, dy), z, s, 0).wait_recv()
+        def go(dy, part):
+            here = slot(k, s, dy, part)
+            pass_on(k, dy, part, here, z, s, 0).wait_recv()
 
             @pl.when(mid & (e == 2))
             def _():
-                pass_on(k, dy, slot(k, s, dy), mate_z, 1, 4).start()
+                pass_on(k, dy, part, here, mate_z, 1, 4).start()
 
             @pl.when(mid & (e < 2) & jnp.logical_not(p.is_attn(k)))
             def _():
-                pass_on(k, dy, slot(k, s, dy), end_z, jnp.where(low, s + 1, s - 1), 2 + e).start()
-
-            spread(k, s, dy).start()
+                pass_on(k, dy, part, here, end_z, jnp.where(low, s + 1, s - 1), 2 + e).start()
+
+            spread(k, s, dy, part).start()
             if dy and whole:
                 pl.when(e == jnp.where(mid, 1, 2))(lambda: partner(k, 0).start())
 
@@ -229,7 +260,7 @@
 
     def spread_done(k, dy):
         for s in range(p.dp - 1):
-            spread(k, s, dy).wait_recv()
+            spread(k, s, dy, None).wait_recv()
 
     def load(src, at, size, buf, index, dst):
         copies = [pltpu.make_async_copy(cut(src, at, size), dst.at[z], l_sem.at[0])]
@@ -242,13 +273,11 @@
 
     step_t = min(256, p.tok)
 
-    def turn():
-        @pl.loop(0, p.dp)
-        def _(q):
-            @pl.loop(0, p.tok // step_t)
-            def _(t):
-                at = pl.multiple_of(t * step_t, step_t)
-                lhs[q, :, pl.ds(at, step_t)] = tile_x[q, pl.ds(at, step_t), :].T
+    def turn(q):
+        @pl.loop(0, p.tok // step_t)
+        def _(t):
+            at = pl.multiple_of(t * step_t, step_t)
+            lhs[q, :, pl.ds(at, step_t)] = tile_x[q, pl.ds(at, step_t), :].T
 
     step_n = min(512, p.nc)
     step_r = min(64, p.mc)
@@ -478,14 +507,22 @@
         else:
             renew(mat, half, parts)
 
-    def take_x(src, at, k):
-        spread_done(k, False)
-        load(src, at, p.mc, buf_x, p.at(k), tile_x)
-        turn()
-
-    def again_x():
-        load(x_mlp, 0, p.mc, buf_x, 0, tile_x)
-        turn()
+    def take_x(src, at, k, waits=True):
+        copies = [(pltpu.make_async_copy(cut(src, at, p.mc), tile_x.at[z], l_sem.at[0]), z)]
+        copies[0][0].start()
+        for e in range(p.dp - 1):
+            s = jnp.where(low, e, 2 - e)
+            if src is h_mlp:
+                in_parts(k, lambda part: spread(k, s, False, part).wait_recv())
+            elif waits:
+                spread(k, s, False, None).wait_recv()
+            q = lax.rem(z + s + 1, p.dp)
+            copies.append((pltpu.make_async_copy(buf_x.at[p.at(k), s], tile_x.at[q], l_sem.at[e + 1]), q))
+            copies[-1][0].start()
+            copies[-2][0].wait()
+            turn(copies[-2][1])
+        copies[-1][0].wait()
+        turn(copies[-1][1])
 
     def got(name, i):
         k = look(i, [p.place[name, j] for j in range(sum(1 for n, _ in p.order if n == name))])
@@ -508,7 +545,7 @@
         finish_first(ATTN)
 
     def use_up(i):
-        pl.when(i == 0)(again_x)
+        pl.when(i == 0)(lambda: take_x(x_mlp, 0, jnp.int32(p.place['x_mlp', 0]), False))
         k = got('up', i)
         load(dy_up, i, p.nc, buf_d, p.at(k), tile_d)
         chunk(UP, i)
@@ -595,21 +632,21 @@
 
     @pl.loop(0, p.count)
     def _(k):
-        def go(dy):
-            some = slot(k, 0, dy)
+        def go(dy, part):
+            some = slot(k, 0, dy, part)
 
             @pl.when(mid)
             def _():
-                pass_on(k, dy, some, z, 0, 1).wait_send()
-                pass_on(k, dy, some, z, 0, 4).wait_send()
+                pass_on(k, dy, part, some, z, 0, 1).wait_send()
+                pass_on(k, dy, part, some, z, 0, 4).wait_send()
 
                 @pl.when(jnp.logical_not(p.is_attn(k)))
                 def _():
-                    pass_on(k, dy, some, z, 0, 2).wait_send()
-                    pass_on(k, dy, some, z, 0, 3).wait_send()
+                    pass_on(k, dy, part, some, z, 0, 2).wait_send()
+                    pass_on(k, dy, part, some, z, 0, 3).wait_send()
 
             for s in range(p.dp - 1):
-                spread(k, s, dy).wait_send()
+                spread(k, s, dy, part).wait_send()
             if dy:
                 partner(k, 0).wait_send()
                 partner(k, 1).wait_send()
@@ -732,6 +769,7 @@
                 jax.ShapeDtypeStruct((p.n_x, p.dp - 1, p.tok, p.mc), BF16)]
         rest = jax.ShapeDtypeStruct((p.mc - p.first_rows, p.nc), F32)
         dma = pltpu.SemaphoreType.DMA
+        lines = p.count + PARTS - 1
         scratch = [
             pltpu.VMEM((p.dp, p.mc, p.tok), BF16),
             pltpu.VMEM((p.dp, p.tok, p.mc), BF16),
@@ -749,8 +787,8 @@
         scratch += [pltpu.VMEM((4, 1, p.cols[mat]), F32) for mat in MATS]
         scratch += [
             pltpu.VMEM((4, 8, 3, 8, LANES), F32),
-            dma((p.count, 5)), dma((p.count, p.dp - 1)),
-            dma((p.count, p.dp - 1)), dma((p.count, p.dp - 1)),
+            dma((lines, 5)), dma((lines, p.dp - 1)),
+            dma((lines, p.dp - 1)), dma((lines, p.dp - 1)),
             dma((p.n_dy, 2)), dma((p.n_dy, 2)),
             dma((4, 4)), dma((4, 4)), dma((4, 8)), dma((4, 8)),
             dma((7,)), dma((7,)),

time: 954 us -> 954 us (level)
  transfers between devices with their start and end apart: 1 -> 1, of which waited for: 0 -> 1; matrix products, arithmetic and copies ran while one was open for 0% -> 0% of each run, Pallas kernels for 3% -> 3%
where the time goes in v8:
time: 954 us; the launch traced here: 953 us
  Pallas kernels  947 us (99%)
    pallas_call x1, Pallas kernels, per_device(): pl.pallas_call(functools.partial(gather_kernel, p), out_shape=o_shapes +...  917 us
    pallas_call x1, Pallas kernels, per_device(): pl.pallas_call(functools.partial(store_kernel, p), out_shape=w_shapes + r...  29.8 us
  transfers between devices with their start and end apart: 1, of which 1 were waited for; matrix products, arithmetic and copies ran while one was open for 0% of the time, Pallas kernels for 3%

profile of v8, /device:TPU:0, one launch (start us, length us, event | category | flops | bytes accessed | tf_op | source)
XLA Modules:
  0.0 952.9 jit_solution(1828866468606735289)
XLA Ops:
  0.7 917.1 %shard_map.283 = (f32[512,1024]{1,0:T(8,128)S(1)}, f32[512,8192]{1,0:T(8,128)}, f32[8,512,1024]{2,1,0:T(8,128)S(1)}, f32[8,512,1024]{2,1,0:T(8,128)S(1)}, f32[1,...) custom-call(bf16[1024,512]{1,0:T(8,128)(2,1)} %x_attn.1, ...), custom_call_target="tpu_custom_call" | custom-call | tf_op jit(solution)/shard_map/pallas_call | solution.py:797
  917.7 1.3 collective-permute-start
  919.0 29.8 %shard_map.284 = (f32[512,1024]{1,0:T(8,128)}, f32[512,8192]{1,0:T(8,128)}, f32[512,8192]{1,0:T(8,128)}, f32[4096,1024]{1,0:T(8,128)}, f32[1,512]{1,0:T(1,128)},...) custom-call(f32[512,1024]{1,0:T(8,128)S(1)} %get-tuple-element.39.o_, ...), custom_call_target="tpu_custom_call" | custom-call | flops 60000002048 | bytes 90000000 | tf_op jit(solution)/shard_map/pallas_call | solution.py:805
  948.8 1.3 collective-permute-done
  950.1 2.8 select_dynamic-update-slice_fusion
Async XLA Ops:
  917.7 32.4 %collective-permute-start = (f32[352,1024]{1,0:T(8,128)}, f32[352,1024]{1,0:T(8,128)}, u32[]{:S(2)}, u32[]{:S(2)}) collective-permute-start(f32[352,1024]{1,0:T(8,128)} %get-tuple-element.54), channel_id=1, source_target_pairs={{8,0},{16,24},{9,1},{17,25},{10,2},{18,26},{11,3},{19,27},{12,4},{... | collective-permute-start | bytes 4325384 | tf_op jit(solution)/shard_map/ppermute | solution.py:818

commit v9 on v8

--- a/solution.py
+++ b/solution.py
@@ -64,8 +64,7 @@
         self.at_table = [base[n] + i for n, i in self.order]
         self.attn_table = [1 if n in ('x_attn', 'attn') else 0 for n, _ in self.order]
         self.steps = {m: self.schedule(m) for m in (True, False)}
-        last = max(max(v.values()) for v in self.steps.values())
-        self.turns = max(last + 1, 3 * (self.count + LATE_MID + 1))
+        self.turns = {m: max(max(v.values()) + 1, 3 * self.count) for m, v in self.steps.items()}
 
     def schedule(self, mid):
         late = LATE_MID if mid else LATE_END
@@ -104,18 +103,21 @@
                   o_attn, o_gate, o_up, grad, nr_attn, nc_attn, nr_gate, nc_gate, nr_up, nc_up, nr_down, nc_down,
                   al_down, be_down, o_rest, buf_d, buf_x,
                   lhs, tile_x, tile_d, w_buf, r_lanes, r_row, c_sum, a_cols, a_rows, w_sq,
-                  b_attn, b_gate, b_up, b_down,
-                  rs_attn, rs_gate, rs_up, rs_down, cs_attn, cs_gate, cs_up, cs_down, st_all,
-                  z_send, z_recv, f_send, f_recv, c_send, c_recv, r1_send, r1_recv, r2_send, r2_recv,
-                  e_send, e_recv, l_sem, wi_sem, wo_sem):
+                  b_attn, b_gate, b_up, b_down, *more):
     p = plan
+    old_refs = more[:8]
+    (rs_attn, rs_gate, rs_up, rs_down, cs_attn, cs_gate, cs_up, cs_down, st_all,
+     z_send, z_recv, f_send, f_recv, c_send, c_recv, r1_send, r1_recv, r2_send, r2_recv,
+     e_send, e_recv, l_sem, wi_sem, wo_sem, o_sem) = more[8:]
     z, y, r = lax.axis_index('dp'), lax.axis_index('col'), lax.axis_index('row')
     low = z < 2
     mid = (z == 1) | (z == 2)
     end_z = jnp.where(low, 0, 3)
     mate_z = 3 - z
     w_refs = {ATTN: w_attn, GATE: w_gate, UP: w_up, DOWN: w_down}
-    old = {ATTN: (r_attn, c_attn), GATE: (r_gate, c_gate), UP: (r_up, c_up), DOWN: (r_down, c_down)}
+    old_in = (r_attn, c_attn, r_gate, c_gate, r_up, c_up, r_down, c_down)
+    old = {mat: (old_refs[2 * mat], old_refs[2 * mat + 1]) for mat in MATS}
+    old_copies = [pltpu.make_async_copy(a, b, o_sem.at[i]) for i, (a, b) in enumerate(zip(old_in, old_refs))]
     new = {ATTN: (nr_attn, nc_attn), GATE: (nr_gate, nc_gate), UP: (nr_up, nc_up), DOWN: (nr_down, nc_down)}
     b_rows = {ATTN: b_attn, GATE: b_gate, UP: b_up, DOWN: b_down}
     rs = {ATTN: rs_attn, GATE: rs_gate, UP: rs_up, DOWN: rs_down}
@@ -587,6 +589,28 @@
     def to_end_down():
         return sent_to_end((nr_down, nc_down, al_down, be_down), 3)
 
+    def sends_left(k):
+        def go(dy, part):
+            some = slot(k, 0, dy, part)
+
+            @pl.when(mid)
+            def _():
+                pass_on(k, dy, part, some, z, 0, 1).wait_send()
+                pass_on(k, dy, part, some, z, 0, 4).wait_send()
+
+                @pl.when(jnp.logical_not(p.is_attn(k)))
+                def _():
+                    pass_on(k, dy, part, some, z, 0, 2).wait_send()
+                    pass_on(k, dy, part, some, z, 0, 3).wait_send()
+
+            for s in range(p.dp - 1):
+                spread(k, s, dy, part).wait_send()
+            if dy:
+                partner(k, 0).wait_send()
+                partner(k, 1).wait_send()
+
+        typed(k, go)
+
     w_sq[...] = jnp.zeros_like(w_sq)
     ahead = jnp.where(mid, AHEAD_MID, AHEAD_END)
 
@@ -597,14 +621,21 @@
     @pl.when(mid)
     def _():
         arrive(jnp.int32(0), jnp.int32(2), False)
+
+    for c in old_copies:
+        c.start()
+    for c in old_copies:
+        c.wait()
 
     @pl.when(jnp.logical_not(mid))
     def _():
         for k in range(AHEAD_MID):
             arrive(jnp.int32(k), jnp.int32(0), False)
 
-    @pl.loop(0, p.turns)
-    def _(t):
+    last_mid, last_end = p.turns[True], p.turns[False] - 2
+    assert last_end >= 3 * p.count and last_end not in p.steps[False].values()
+
+    def one_turn(t):
         d, turn_no = lax.div(t, 3), lax.rem(t, 3)
         pl.when((turn_no == 0) & (d >= 1) & (d < p.count))(lambda: own_first_left(d - 1))
         early = jnp.where(mid, jnp.where(turn_no == 0, 1, 0), jnp.where(turn_no == 2, AHEAD_MID, 0))
@@ -628,30 +659,12 @@
                 spread_done(k, True)
                 partner(k, 1).start()
 
+        pl.when(t == jnp.where(mid, last_mid, last_end))(lambda: pl.loop(0, p.count)(sends_left))
         work(t)
 
-    @pl.loop(0, p.count)
-    def _(k):
-        def go(dy, part):
-            some = slot(k, 0, dy, part)
-
-            @pl.when(mid)
-            def _():
-                pass_on(k, dy, part, some, z, 0, 1).wait_send()
-                pass_on(k, dy, part, some, z, 0, 4).wait_send()
-
-                @pl.when(jnp.logical_not(p.is_attn(k)))
-                def _():
-                    pass_on(k, dy, part, some, z, 0, 2).wait_send()
-                    pass_on(k, dy, part, some, z, 0, 3).wait_send()
-
-            for s in range(p.dp - 1):
-                spread(k, s, dy, part).wait_send()
-            if dy:
-                partner(k, 0).wait_send()
-                partner(k, 1).wait_send()
-
-        typed(k, go)
+    @pl.loop(0, last_mid + 1)
+    def _(t):
+        pl.when(mid | (t < p.turns[False]))(lambda: one_turn(t))
 
     own_first_left(jnp.int32(p.count - 1))
     for mat in (GATE, UP):
@@ -783,6 +796,7 @@
             pltpu.VMEM((4, 8, LANES), F32),
         ]
         scratch += [pltpu.VMEM((1, p.cols[mat]), F32) for mat in MATS]
+        scratch += [pltpu.VMEM(v.shape, F32) for v in row_shapes]
         scratch += [pltpu.VMEM((2, 1, p.rows[mat]), F32) for mat in MATS]
         scratch += [pltpu.VMEM((4, 1, p.cols[mat]), F32) for mat in MATS]
         scratch += [
@@ -792,12 +806,12 @@
             dma((p.n_dy, 2)), dma((p.n_dy, 2)),
             dma((4, 4)), dma((4, 4)), dma((4, 8)), dma((4, 8)),
             dma((7,)), dma((7,)),
-            dma((p.dp,)), dma((3,)), dma((3,)),
+            dma((p.dp,)), dma((3,)), dma((3,)), dma((8,)),
         ]
         out = pl.pallas_call(
             functools.partial(gather_kernel, p),
             out_shape=o_shapes + [pltpu.VMEM(v.shape, F32) for v in row_shapes + row_shapes[-2:]] + [rest] + bufs,
-            in_specs=[any_spec] * 11 + [vmem_spec] * 8 + [pl.BlockSpec(memory_space=pltpu.SMEM)],
+            in_specs=[any_spec] * 19 + [pl.BlockSpec(memory_space=pltpu.SMEM)],
             out_specs=[vmem_spec, any_spec, up_spec, vmem_spec] + [vmem_spec] * 10 + [any_spec] * 3,
             scratch_shapes=scratch,
             compiler_params=pltpu.CompilerParams(collective_id=0, has_side_effects=True, vmem_limit_bytes=VMEM_LIMIT),

time: 954 us -> 952 us (level)
  no operation moved by 1% of the time
where the time goes in v9:
time: 952 us; the launch traced here: 951 us
  Pallas kernels  945 us (99%)
    pallas_call x1, Pallas kernels, per_device(): pl.pallas_call(functools.partial(gather_kernel, p), out_shape=o_shapes +...  915 us
    pallas_call x1, Pallas kernels, per_device(): pl.pallas_call(functools.partial(store_kernel, p), out_shape=w_shapes + r...  29.8 us
  transfers between devices with their start and end apart: 1, of which 1 were waited for; matrix products, arithmetic and copies ran while one was open for 0% of the time, Pallas kernels for 3%

profile of v9, /device:TPU:0, one launch (start us, length us, event | category | flops | bytes accessed | tf_op | source)
XLA Modules:
  0.0 951.0 jit_solution(2464202975232183704)
XLA Ops:
  0.7 915.2 %shard_map.283 = (f32[512,1024]{1,0:T(8,128)S(1)}, f32[512,8192]{1,0:T(8,128)}, f32[8,512,1024]{2,1,0:T(8,128)S(1)}, f32[8,512,1024]{2,1,0:T(8,128)S(1)}, f32[1,...) custom-call(bf16[1024,512]{1,0:T(8,128)(2,1)} %x_attn.1, ...), custom_call_target="tpu_custom_call" | custom-call | tf_op jit(solution)/shard_map/pallas_call | solution.py:811
  915.8 1.3 collective-permute-start
  917.1 29.8 %shard_map.284 = (f32[512,1024]{1,0:T(8,128)}, f32[512,8192]{1,0:T(8,128)}, f32[512,8192]{1,0:T(8,128)}, f32[4096,1024]{1,0:T(8,128)}, f32[1,512]{1,0:T(1,128)},...) custom-call(f32[512,1024]{1,0:T(8,128)S(1)} %get-tuple-element.39.o_, ...), custom_call_target="tpu_custom_call" | custom-call | flops 60000002048 | bytes 90000000 | tf_op jit(solution)/shard_map/pallas_call | solution.py:819
  946.9 1.3 collective-permute-done
  948.2 2.8 select_dynamic-update-slice_fusion
Async XLA Ops:
  915.8 32.4 %collective-permute-start = (f32[352,1024]{1,0:T(8,128)}, f32[352,1024]{1,0:T(8,128)}, u32[]{:S(2)}, u32[]{:S(2)}) collective-permute-start(f32[352,1024]{1,0:T(8,128)} %get-tuple-element.54), channel_id=1, source_target_pairs={{8,0},{16,24},{9,1},{17,25},{10,2},{18,26},{11,3},{19,27},{12,4},{... | collective-permute-start | bytes 4325384 | tf_op jit(solution)/shard_map/ppermute | solution.py:832

commit v10 on v9

--- a/solution.py
+++ b/solution.py
@@ -632,8 +632,7 @@
         for k in range(AHEAD_MID):
             arrive(jnp.int32(k), jnp.int32(0), False)
 
-    last_mid, last_end = p.turns[True], p.turns[False] - 2
-    assert last_end >= 3 * p.count and last_end not in p.steps[False].values()
+    last_mid, last_end = p.turns[True], p.turns[False] - 1
 
     def one_turn(t):
         d, turn_no = lax.div(t, 3), lax.rem(t, 3)
@@ -659,8 +658,15 @@
                 spread_done(k, True)
                 partner(k, 1).start()
 
-        pl.when(t == jnp.where(mid, last_mid, last_end))(lambda: pl.loop(0, p.count)(sends_left))
         work(t)
+        first_end = 3 * p.count - 3
+        assert first_end not in p.steps[False].values()
+
+        @pl.when((mid & (t == last_mid)) | (jnp.logical_not(mid) & ((t == first_end) | (t == last_end))))
+        def _():
+            @pl.loop(0, p.count)
+            def _(k):
+                pl.when(mid | ((t == first_end) == (k < p.count - 2)))(lambda: sends_left(k))
 
     @pl.loop(0, last_mid + 1)
     def _(t):

time: 952 us -> 951 us (level)
  no operation moved by 1% of the time
where the time goes in v10:
time: 951 us; the launch traced here: 950 us
  Pallas kernels  944 us (99%)
    pallas_call x1, Pallas kernels, per_device(): pl.pallas_call(functools.partial(gather_kernel, p), out_shape=o_shapes +...  914 us
    pallas_call x1, Pallas kernels, per_device(): pl.pallas_call(functools.partial(store_kernel, p), out_shape=w_shapes + r...  29.8 us
  transfers between devices with their start and end apart: 1, of which 1 were waited for; matrix products, arithmetic and copies ran while one was open for 0% of the time, Pallas kernels for 3%

profile of v10, /device:TPU:0, one launch (start us, length us, event | category | flops | bytes accessed | tf_op | source)
XLA Modules:
  0.0 950.1 jit_solution(12613587151988538145)
XLA Ops:
  0.7 914.3 %shard_map.283 = (f32[512,1024]{1,0:T(8,128)S(1)}, f32[512,8192]{1,0:T(8,128)}, f32[8,512,1024]{2,1,0:T(8,128)S(1)}, f32[8,512,1024]{2,1,0:T(8,128)S(1)}, f32[1,...) custom-call(bf16[1024,512]{1,0:T(8,128)(2,1)} %x_attn.1, ...), custom_call_target="tpu_custom_call" | custom-call | tf_op jit(solution)/shard_map/pallas_call | solution.py:817
  914.9 1.3 collective-permute-start
  916.2 29.8 %shard_map.284 = (f32[512,1024]{1,0:T(8,128)}, f32[512,8192]{1,0:T(8,128)}, f32[512,8192]{1,0:T(8,128)}, f32[4096,1024]{1,0:T(8,128)}, f32[1,512]{1,0:T(1,128)},...) custom-call(f32[512,1024]{1,0:T(8,128)S(1)} %get-tuple-element.39.o_, ...), custom_call_target="tpu_custom_call" | custom-call | flops 60000002048 | bytes 90000000 | tf_op jit(solution)/shard_map/pallas_call | solution.py:825
  946.0 1.3 collective-permute-done
  947.3 2.8 select_dynamic-update-slice_fusion
Async XLA Ops:
  914.9 32.4 %collective-permute-start = (f32[352,1024]{1,0:T(8,128)}, f32[352,1024]{1,0:T(8,128)}, u32[]{:S(2)}, u32[]{:S(2)}) collective-permute-start(f32[352,1024]{1,0:T(8,128)} %get-tuple-element.54), channel_id=1, source_target_pairs={{8,0},{16,24},{9,1},{17,25},{10,2},{18,26},{11,3},{19,27},{12,4},{... | collective-permute-start | bytes 4325384 | tf_op jit(solution)/shard_map/ppermute | solution.py:838

commit v11 on v10

--- a/solution.py
+++ b/solution.py
@@ -202,22 +202,26 @@
     def down_rows(ref, i):
         return ref.at[pl.ds(pl.multiple_of(i * p.mc, p.mc), p.mc), :]
 
-    def own_to(k, dy, part, src):
+    def own_to(k, dy, part, src, end_too, mate_too):
         @pl.when(jnp.logical_not(mid))
         def _():
             pass_on(k, dy, part, src, jnp.where(low, 1, 2), jnp.where(low, 2, 0), 0).start()
 
         @pl.when(mid)
         def _():
-            @pl.when(jnp.logical_not(p.is_attn(k)))
+            @pl.when(jnp.logical_not(p.is_attn(k)) & end_too)
             def _():
                 pass_on(k, dy, part, src, end_z, jnp.where(low, 0, 2), 0).start()
-            pass_on(k, dy, part, src, mate_z, jnp.where(low, 2, 0), 1).start()
-
-    def send_own(k):
+
+            @pl.when(mate_too)
+            def _():
+                pass_on(k, dy, part, src, mate_z, jnp.where(low, 2, 0), 1).start()
+
+    def send_own(k, end_too, mate_too):
         def go(ref, at, size, dy):
             def send(part):
-                own_to(k, dy, part, ref.at[rows_of(dy, part), pl.ds(pl.multiple_of(at * size, size), size)])
+                src = ref.at[rows_of(dy, part), pl.ds(pl.multiple_of(at * size, size), size)]
+                own_to(k, dy, part, src, end_too, mate_too)
 
             if ref is h_mlp:
                 in_parts(k, send)
@@ -616,7 +620,7 @@
 
     @pl.loop(0, AHEAD_END)
     def _(k):
-        pl.when(k < ahead)(lambda: send_own(k))
+        pl.when(k < jnp.where(mid, AHEAD_MID + 1, AHEAD_END))(lambda: send_own(k, True, k < AHEAD_MID))
 
     @pl.when(mid)
     def _():
@@ -644,7 +648,7 @@
 
         @pl.when(turn_no == 2)
         def _():
-            pl.when(d + ahead < p.count)(lambda: send_own(d + ahead))
+            pl.when(d + ahead < p.count)(lambda: send_own(d + ahead, d > 0, True))
 
             @pl.when((d == p.count - 1) & mid)
             def _():

time: 951 us -> 951 us (level)
  no operation moved by 1% of the time
where the time goes in v11:
time: 951 us; the launch traced here: 950 us
  Pallas kernels  942 us (99%)
    pallas_call x1, Pallas kernels, per_device(): pl.pallas_call(functools.partial(gather_kernel, p), out_shape=o_shapes +...  912 us
    pallas_call x1, Pallas kernels, per_device(): pl.pallas_call(functools.partial(store_kernel, p), out_shape=w_shapes + r...  29.8 us
  transfers between devices with their start and end apart: 1, of which 1 were waited for; matrix products, arithmetic and copies ran while one was open for 0% of the time, Pallas kernels for 3%

profile of v11, /device:TPU:0, one launch (start us, length us, event | category | flops | bytes accessed | tf_op | source)
XLA Modules:
  0.0 950.1 jit_solution(15154753472288538472)
XLA Ops:
  0.7 912.1 %shard_map.283 = (f32[512,1024]{1,0:T(8,128)S(1)}, f32[512,8192]{1,0:T(8,128)}, f32[8,512,1024]{2,1,0:T(8,128)S(1)}, f32[8,512,1024]{2,1,0:T(8,128)S(1)}, f32[1,...) custom-call(bf16[1024,512]{1,0:T(8,128)(2,1)} %x_attn.1, ...), custom_call_target="tpu_custom_call" | custom-call | tf_op jit(solution)/shard_map/pallas_call | solution.py:821
  912.7 1.3 collective-permute-start
  914.0 29.8 %shard_map.284 = (f32[512,1024]{1,0:T(8,128)}, f32[512,8192]{1,0:T(8,128)}, f32[512,8192]{1,0:T(8,128)}, f32[4096,1024]{1,0:T(8,128)}, f32[1,512]{1,0:T(1,128)},...) custom-call(f32[512,1024]{1,0:T(8,128)S(1)} %get-tuple-element.39.o_, ...), custom_call_target="tpu_custom_call" | custom-call | flops 60000002048 | bytes 90000000 | tf_op jit(solution)/shard_map/pallas_call | solution.py:829
  943.8 3.5 collective-permute-done
  947.3 2.8 select_dynamic-update-slice_fusion
Async XLA Ops:
  912.7 34.5 %collective-permute-start = (f32[352,1024]{1,0:T(8,128)}, f32[352,1024]{1,0:T(8,128)}, u32[]{:S(2)}, u32[]{:S(2)}) collective-permute-start(f32[352,1024]{1,0:T(8,128)} %get-tuple-element.54), channel_id=1, source_target_pairs={{8,0},{16,24},{9,1},{17,25},{10,2},{18,26},{11,3},{19,27},{12,4},{... | collective-permute-start | bytes 4325384 | tf_op jit(solution)/shard_map/ppermute | solution.py:842

commit v12 on v11

--- a/solution.py
+++ b/solution.py
@@ -22,7 +22,7 @@
 STORE_LIMIT = 29 * 1024 * 1024
 UP_KEPT = True
 HBM_KEPT = (1,) if UP_KEPT else (1, 2)
-DEPTH, WIDE = 4, 4
+DEPTH, WIDE = 6, 6
 
 
 def look(k, table):
@@ -52,7 +52,7 @@
                       + u + [('out', 0)] + h[2:])
         self.count = len(self.order)
         self.place = {v: k for k, v in enumerate(self.order)}
-        self.first_rows = self.mc * 5 // 16
+        self.first_rows = self.mc * 13 // 32 // 8 * 8
         self.n_dy = 2 * self.ng + 2
         self.n_x = self.nh + 2
         self.pieces = max(self.ng, self.nh)

time: 951 us -> 948 us (level)
  transfers between devices with their start and end apart: 1 -> 1, of which waited for: 1 -> 0; matrix products, arithmetic and copies ran while one was open for 0% -> 0% of each run, Pallas kernels for 3% -> 3%
where the time goes in v12:
time: 948 us; the launch traced here: 946 us
  Pallas kernels  941 us (99%)
    pallas_call x1, Pallas kernels, per_device(): pl.pallas_call(functools.partial(gather_kernel, p), out_shape=o_shapes +...  912 us
    pallas_call x1, Pallas kernels, per_device(): pl.pallas_call(functools.partial(store_kernel, p), out_shape=w_shapes + r...  29.4 us
  transfers between devices with their start and end apart: 1, of which 0 were waited for; matrix products, arithmetic and copies ran while one was open for 0% of the time, Pallas kernels for 3%

profile of v12, /device:TPU:0, one launch (start us, length us, event | category | flops | bytes accessed | tf_op | source)
XLA Modules:
  0.0 946.1 jit_solution(13604634712964299175)
XLA Ops:
  0.7 912.1 %shard_map.283 = (f32[512,1024]{1,0:T(8,128)S(1)}, f32[512,8192]{1,0:T(8,128)}, f32[8,512,1024]{2,1,0:T(8,128)S(1)}, f32[8,512,1024]{2,1,0:T(8,128)S(1)}, f32[1,...) custom-call(bf16[1024,512]{1,0:T(8,128)(2,1)} %x_attn.1, ...), custom_call_target="tpu_custom_call" | custom-call | tf_op jit(solution)/shard_map/pallas_call | solution.py:821
  912.7 1.3 collective-permute-start
  914.0 29.4 %shard_map.284 = (f32[512,1024]{1,0:T(8,128)}, f32[512,8192]{1,0:T(8,128)}, f32[512,8192]{1,0:T(8,128)}, f32[4096,1024]{1,0:T(8,128)}, f32[1,512]{1,0:T(1,128)},...) custom-call(f32[512,1024]{1,0:T(8,128)S(1)} %get-tuple-element.39.o_, ...), custom_call_target="tpu_custom_call" | custom-call | flops 60000002048 | bytes 90000000 | tf_op jit(solution)/shard_map/pallas_call | solution.py:829
  943.5 0.0 collective-permute-done
  943.5 2.6 select_dynamic-update-slice_fusion
Async XLA Ops:
  912.7 30.7 %collective-permute-start = (f32[304,1024]{1,0:T(8,128)}, f32[304,1024]{1,0:T(8,128)}, u32[]{:S(2)}, u32[]{:S(2)}) collective-permute-start(f32[304,1024]{1,0:T(8,128)} %get-tuple-element.54), channel_id=1, source_target_pairs={{8,0},{16,24},{9,1},{17,25},{10,2},{18,26},{11,3},{19,27},{12,4},{... | collective-permute-start | bytes 3735560 | tf_op jit(solution)/shard_map/ppermute | solution.py:842

commit v13 on v12

--- a/solution.py
+++ b/solution.py
@@ -23,6 +23,7 @@
 UP_KEPT = True
 HBM_KEPT = (1,) if UP_KEPT else (1, 2)
 DEPTH, WIDE = 6, 6
+END_H = {1: 2, 2: 3}
 
 
 def look(k, table):
@@ -52,7 +53,7 @@
                       + u + [('out', 0)] + h[2:])
         self.count = len(self.order)
         self.place = {v: k for k, v in enumerate(self.order)}
-        self.first_rows = self.mc * 13 // 32 // 8 * 8
+        self.first_rows = self.mc * 11 // 32 // 8 * 8
         self.n_dy = 2 * self.ng + 2
         self.n_x = self.nh + 2
         self.pieces = max(self.ng, self.nh)
@@ -74,7 +75,7 @@
                 continue
             for i in range(self.parts[mat]):
                 k = self.place[name, i]
-                need = [3 * (k + late + 1)] if name != 'h' else [3 * (k + late) if mid else 3 * k + 5]
+                need = [3 * (k + late + 1)] if name != 'h' else [3 * (k + late) if mid else 3 * k + END_H.get(self.count - k, 5)]
                 if i == 0:
                     need.append(3 * (self.place[FIRST[name]] + late + (name == 'h')))
                 tasks.append(((name, i), max(need)))
@@ -641,14 +642,17 @@
     def one_turn(t):
         d, turn_no = lax.div(t, 3), lax.rem(t, 3)
         pl.when((turn_no == 0) & (d >= 1) & (d < p.count))(lambda: own_first_left(d - 1))
-        early = jnp.where(mid, jnp.where(turn_no == 0, 1, 0), jnp.where(turn_no == 2, AHEAD_MID, 0))
+        late_own = d == p.count - 2
+        near = jnp.where(late_own, 1, jnp.where(d == p.count - 3, p.count, AHEAD_MID))
+        early = jnp.where(mid, jnp.where(turn_no == 0, 1, 0), jnp.where(turn_no == 2, near, 0))
         e = lax.rem(turn_no + jnp.where(mid, 2, 1), 3)
         k = d + early
         pl.when(k < p.count)(lambda: arrive(k, e, True))
 
         @pl.when(turn_no == 2)
         def _():
-            pl.when(d + ahead < p.count)(lambda: send_own(d + ahead, d > 0, True))
+            own = d + jnp.where(mid, near, AHEAD_END)
+            pl.when(own < p.count)(lambda: send_own(own, d > 0, True))
 
             @pl.when((d == p.count - 1) & mid)
             def _():
@@ -663,8 +667,7 @@
                 partner(k, 1).start()
 
         work(t)
-        first_end = 3 * p.count - 3
-        assert first_end not in p.steps[False].values()
+        first_end = max(set(range(3 * p.count - 4)) - set(p.steps[False].values()))
 
         @pl.when((mid & (t == last_mid)) | (jnp.logical_not(mid) & ((t == first_end) | (t == last_end))))
         def _():

time: 948 us -> 956 us (level)
  transfers between devices with their start and end apart: 1 -> 1, of which waited for: 0 -> 1; matrix products, arithmetic and copies ran while one was open for 0% -> 0% of each run, Pallas kernels for 3% -> 3%
where the time goes in v13:
time: 956 us; the launch traced here: 955 us
  Pallas kernels  948 us (99%)
    pallas_call x1, Pallas kernels, per_device(): pl.pallas_call(functools.partial(gather_kernel, p), out_shape=o_shapes +...  919 us
    pallas_call x1, Pallas kernels, per_device(): pl.pallas_call(functools.partial(store_kernel, p), out_shape=w_shapes + r...  29.4 us
  transfers between devices with their start and end apart: 1, of which 1 were waited for; matrix products, arithmetic and copies ran while one was open for 0% of the time, Pallas kernels for 3%

profile of v13, /device:TPU:0, one launch (start us, length us, event | category | flops | bytes accessed | tf_op | source)
XLA Modules:
  0.0 954.6 jit_solution(15386312334305215622)
XLA Ops:
  0.7 918.9 %shard_map.283 = (f32[512,1024]{1,0:T(8,128)S(1)}, f32[512,8192]{1,0:T(8,128)}, f32[8,512,1024]{2,1,0:T(8,128)S(1)}, f32[8,512,1024]{2,1,0:T(8,128)S(1)}, f32[1,...) custom-call(bf16[1024,512]{1,0:T(8,128)(2,1)} %x_attn.1, ...), custom_call_target="tpu_custom_call" | custom-call | tf_op jit(solution)/shard_map/pallas_call | solution.py:824
  919.6 1.3 collective-permute-start
  920.9 29.4 %shard_map.284 = (f32[512,1024]{1,0:T(8,128)}, f32[512,8192]{1,0:T(8,128)}, f32[512,8192]{1,0:T(8,128)}, f32[4096,1024]{1,0:T(8,128)}, f32[1,512]{1,0:T(1,128)},...) custom-call(f32[512,1024]{1,0:T(8,128)S(1)} %get-tuple-element.39.o_, ...), custom_call_target="tpu_custom_call" | custom-call | flops 60000002048 | bytes 90000000 | tf_op jit(solution)/shard_map/pallas_call | solution.py:832
  950.3 1.6 collective-permute-done
  951.9 2.7 select_dynamic-update-slice_fusion
Async XLA Ops:
  919.6 32.4 %collective-permute-start = (f32[336,1024]{1,0:T(8,128)}, f32[336,1024]{1,0:T(8,128)}, u32[]{:S(2)}, u32[]{:S(2)}) collective-permute-start(f32[336,1024]{1,0:T(8,128)} %get-tuple-element.54), channel_id=1, source_target_pairs={{8,0},{16,24},{9,1},{17,25},{10,2},{18,26},{11,3},{19,27},{12,4},{... | collective-permute-start | bytes 4128776 | tf_op jit(solution)/shard_map/ppermute | solution.py:845

commit v14 on v12

--- a/solution.py
+++ b/solution.py
@@ -74,7 +74,7 @@
                 continue
             for i in range(self.parts[mat]):
                 k = self.place[name, i]
-                need = [3 * (k + late + 1)] if name != 'h' else [3 * (k + late) if mid else 3 * k + 5]
+                need = [3 * (k + late + 1)] if name != 'h' else [3 * (k + late) if mid else 3 * k + (3 if k == self.count - 1 else 5)]
                 if i == 0:
                     need.append(3 * (self.place[FIRST[name]] + late + (name == 'h')))
                 tasks.append(((name, i), max(need)))

time: 948 us -> 948 us (level)
  no operation moved by 1% of the time
where the time goes in v14:
time: 948 us; the launch traced here: 946 us
  Pallas kernels  942 us (99%)
    pallas_call x1, Pallas kernels, per_device(): pl.pallas_call(functools.partial(gather_kernel, p), out_shape=o_shapes +...  912 us
    pallas_call x1, Pallas kernels, per_device(): pl.pallas_call(functools.partial(store_kernel, p), out_shape=w_shapes + r...  29.4 us
  transfers between devices with their start and end apart: 1, of which 0 were waited for; matrix products, arithmetic and copies ran while one was open for 0% of the time, Pallas kernels for 3%

profile of v14, /device:TPU:0, one launch (start us, length us, event | category | flops | bytes accessed | tf_op | source)
XLA Modules:
  0.0 946.1 jit_solution(5385126566577304254)
XLA Ops:
  0.7 912.1 %shard_map.283 = (f32[512,1024]{1,0:T(8,128)S(1)}, f32[512,8192]{1,0:T(8,128)}, f32[8,512,1024]{2,1,0:T(8,128)S(1)}, f32[8,512,1024]{2,1,0:T(8,128)S(1)}, f32[1,...) custom-call(bf16[1024,512]{1,0:T(8,128)(2,1)} %x_attn.1, ...), custom_call_target="tpu_custom_call" | custom-call | tf_op jit(solution)/shard_map/pallas_call | solution.py:821
  912.8 1.3 collective-permute-start
  914.1 29.4 %shard_map.284 = (f32[512,1024]{1,0:T(8,128)}, f32[512,8192]{1,0:T(8,128)}, f32[512,8192]{1,0:T(8,128)}, f32[4096,1024]{1,0:T(8,128)}, f32[1,512]{1,0:T(1,128)},...) custom-call(f32[512,1024]{1,0:T(8,128)S(1)} %get-tuple-element.39.o_, ...), custom_call_target="tpu_custom_call" | custom-call | flops 60000002048 | bytes 90000000 | tf_op jit(solution)/shard_map/pallas_call | solution.py:829
  943.5 0.0 collective-permute-done
  943.5 2.6 select_dynamic-update-slice_fusion
Async XLA Ops:
  912.8 30.7 %collective-permute-start = (f32[304,1024]{1,0:T(8,128)}, f32[304,1024]{1,0:T(8,128)}, u32[]{:S(2)}, u32[]{:S(2)}) collective-permute-start(f32[304,1024]{1,0:T(8,128)} %get-tuple-element.54), channel_id=1, source_target_pairs={{8,0},{16,24},{9,1},{17,25},{10,2},{18,26},{11,3},{19,27},{12,4},{... | collective-permute-start | bytes 3735560 | tf_op jit(solution)/shard_map/ppermute | solution.py:842

commit v15 on v14

--- a/solution.py
+++ b/solution.py
@@ -52,7 +52,7 @@
                       + u + [('out', 0)] + h[2:])
         self.count = len(self.order)
         self.place = {v: k for k, v in enumerate(self.order)}
-        self.first_rows = self.mc * 13 // 32 // 8 * 8
+        self.first_rows = self.mc * 12 // 32 // 8 * 8
         self.n_dy = 2 * self.ng + 2
         self.n_x = self.nh + 2
         self.pieces = max(self.ng, self.nh)

time: 948 us -> 948 us (level)
  transfers between devices with their start and end apart: 1 -> 1, of which waited for: 0 -> 1; matrix products, arithmetic and copies ran while one was open for 0% -> 0% of each run, Pallas kernels for 3% -> 3%
where the time goes in v15:
time: 948 us; the launch traced here: 947 us
  Pallas kernels  942 us (99%)
    pallas_call x1, Pallas kernels, per_device(): pl.pallas_call(functools.partial(gather_kernel, p), out_shape=o_shapes +...  912 us
    pallas_call x1, Pallas kernels, per_device(): pl.pallas_call(functools.partial(store_kernel, p), out_shape=w_shapes + r...  29.4 us
  transfers between devices with their start and end apart: 1, of which 1 were waited for; matrix products, arithmetic and copies ran while one was open for 0% of the time, Pallas kernels for 3%

profile of v15, /device:TPU:0, one launch (start us, length us, event | category | flops | bytes accessed | tf_op | source)
XLA Modules:
  0.0 947.1 jit_solution(4950212497377251535)
XLA Ops:
  0.7 912.1 %shard_map.283 = (f32[512,1024]{1,0:T(8,128)S(1)}, f32[512,8192]{1,0:T(8,128)}, f32[8,512,1024]{2,1,0:T(8,128)S(1)}, f32[8,512,1024]{2,1,0:T(8,128)S(1)}, f32[1,...) custom-call(bf16[1024,512]{1,0:T(8,128)(2,1)} %x_attn.1, ...), custom_call_target="tpu_custom_call" | custom-call | tf_op jit(solution)/shard_map/pallas_call | solution.py:821
  912.8 1.3 collective-permute-start
  914.1 29.4 %shard_map.284 = (f32[512,1024]{1,0:T(8,128)}, f32[512,8192]{1,0:T(8,128)}, f32[512,8192]{1,0:T(8,128)}, f32[4096,1024]{1,0:T(8,128)}, f32[1,512]{1,0:T(1,128)},...) custom-call(f32[512,1024]{1,0:T(8,128)S(1)} %get-tuple-element.39.o_, ...), custom_call_target="tpu_custom_call" | custom-call | flops 60000002048 | bytes 90000000 | tf_op jit(solution)/shard_map/pallas_call | solution.py:829
  943.5 1.0 collective-permute-done
  944.5 2.6 select_dynamic-update-slice_fusion
Async XLA Ops:
  912.8 31.7 %collective-permute-start = (f32[320,1024]{1,0:T(8,128)}, f32[320,1024]{1,0:T(8,128)}, u32[]{:S(2)}, u32[]{:S(2)}) collective-permute-start(f32[320,1024]{1,0:T(8,128)} %get-tuple-element.54), channel_id=1, source_target_pairs={{8,0},{16,24},{9,1},{17,25},{10,2},{18,26},{11,3},{19,27},{12,4},{... | collective-permute-start | bytes 3932168 | tf_op jit(solution)/shard_map/ppermute | solution.py:842
